TPU v7x, 768 devices: a whole 4x8x12 slice. The times are simulated.
768 devices in a mesh: slab: 768 (over y, z, x, core).
Axes of the slice: x: 4, y: 8, z: 12, core: 2. Of those that a mesh axis runs over, the one named last changes fastest.
Arguments:
- load_terms: float32 [8, 8, 8, 98304], P(None, None, None, 'slab'), may hold values from -12 to 12
- geometry: float32 [3, 8, 8, 8, 98304], P(None, None, None, None, 'slab'), may hold values from 0.02 to 0.2
- mass_terms: float32 [8, 8, 8, 98304], P(None, None, None, 'slab'), may hold values from 1 to 4
- element_order: int32 [768, 128], P('slab'), may hold values from 0 to 127, each once within a row
Outputs:
- solution: float32 [8, 8, 8, 98304], P(None, None, None, 'slab')
- residual: float32 [8, 8, 8, 98304], P(None, None, None, 'slab')
Inputs may be any that keep to these rules, and one draw needn't show every extreme that they name: `element_order`: each device's row lists each of its 128 cells once.
All inputs are finite; a program needn't handle non-finite values.
Results may differ from a plain program's by a relative error of at most 0.0001.
Values sent between devices are 32-bit elements; how exact they have to be, the bound alone decides.
A program may use at most 32 MiB of HBM per device.

v0:
```python
import functools

import jax
import jax.numpy as jnp
import numpy as np
from jax import lax
from jax.sharding import Mesh
from jax.sharding import PartitionSpec as P

EL_X = 1
EL_Y = 8
EL_Z = 16
SLAB = ("slab_0", "slab_1", "slab_2", "slab_3")


spectrum_centre = 1.65
spectrum_half = 1.35


def padded_2(block, sides, width):
    for axis, dim in sides:
        count = lax.axis_size(axis)
        forward = [(i, i + 1) for i in range(count - 1)]
        forward.append((count - 1, 0))
        backward = [(target, source) for source, target in forward]
        low = lax.ppermute(
            lax.slice_in_dim(block, block.shape[dim] - width, None, axis=dim), axis, forward
        )
        high = lax.ppermute(lax.slice_in_dim(block, 0, width, axis=dim), axis, backward)
        block = jnp.concatenate([low, block, high], axis=dim)
    return block


def over_axes(shard, axes):
    return functools.reduce(lax.psum, axes, shard)


def legendre_table(positions, points):
    columns = [positions * 0.0 + 1.0, positions]
    for degree_now in range(2, points):
        columns.append(
            ((2 * degree_now - 1) * positions * columns[-1] - (degree_now - 1) * columns[-2])
            / degree_now
        )
    return np.stack(columns, axis=1)


def gll_derivative(points):
    degree = points - 1
    grid_nodes = -np.cos(np.pi * np.arange(points) / degree)
    for repeat in range(100):
        legendre = legendre_table(grid_nodes, points)
        grid_nodes = grid_nodes - (grid_nodes * legendre[:, degree] - legendre[:, degree - 1]) / (
            points * legendre[:, degree]
        )
    legendre = legendre_table(grid_nodes, points)
    top_values = legendre[:, degree]
    index_list = np.arange(points)
    same_index = index_list[:, None] == index_list[None, :]
    spacing = grid_nodes[:, None] - grid_nodes[None, :]
    spacing = np.where(same_index, 1.0, spacing)
    deriv_table = top_values[:, None] / (top_values[None, :] * spacing)
    deriv_table = np.where(same_index, 0.0, deriv_table)
    deriv_table[0, 0] = -degree * points / 4.0
    deriv_table[degree, degree] = degree * points / 4.0
    return deriv_table


def local_apply(values, geometry, mass_terms, deriv_table):
    highest = lax.Precision.HIGHEST
    grad_one = jnp.einsum("ma,abce->mbce", deriv_table, values, precision=highest)
    result = jnp.einsum("ma,mbce->abce", deriv_table, geometry[0] * grad_one, precision=highest)
    grad_two = jnp.einsum("mb,abce->amce", deriv_table, values, precision=highest)
    result = result + jnp.einsum(
        "mb,amce->abce", deriv_table, geometry[1] * grad_two, precision=highest
    )
    grad_three = jnp.einsum("mc,abce->abme", deriv_table, values, precision=highest)
    result = result + jnp.einsum(
        "mc,abme->abce", deriv_table, geometry[2] * grad_three, precision=highest
    )
    return result + mass_terms * values


def local_diagonal(geometry, mass_terms, deriv_table):
    highest = lax.Precision.HIGHEST
    squared = deriv_table * deriv_table
    result = jnp.einsum("ma,mbce->abce", squared, geometry[0], precision=highest)
    result = result + jnp.einsum("mb,amce->abce", squared, geometry[1], precision=highest)
    result = result + jnp.einsum("mc,abme->abce", squared, geometry[2], precision=highest)
    return result + mass_terms


def build_tables(element_order):
    cell_ids = element_order[0]
    elem_count = cell_ids.shape[0]
    cross_count = EL_Y * EL_Z
    column_ids = jnp.arange(elem_count, dtype=jnp.int32)
    inverse = jnp.zeros((elem_count,), jnp.int32).at[cell_ids].set(column_ids)
    pos_x = cell_ids // cross_count
    pos_y = cell_ids // EL_Z % EL_Y
    pos_z = cell_ids % EL_Z
    across = pos_y * EL_Z + pos_z
    plus_x = jnp.where(
        pos_x + 1 < EL_X,
        inverse[jnp.minimum(cell_ids + cross_count, elem_count - 1)],
        elem_count + across,
    )
    minus_x = jnp.where(
        pos_x > 0, inverse[jnp.maximum(cell_ids - cross_count, 0)], elem_count + across
    )
    plus_y = jnp.where(
        pos_y + 1 < EL_Y, inverse[jnp.minimum(cell_ids + EL_Z, elem_count - 1)], elem_count
    )
    minus_y = jnp.where(pos_y > 0, inverse[jnp.maximum(cell_ids - EL_Z, 0)], elem_count)
    base_z = cell_ids - pos_z
    plus_z = inverse[base_z + (pos_z + 1) % EL_Z]
    minus_z = inverse[base_z + (pos_z + EL_Z - 1) % EL_Z]
    return {
        "plus_x": plus_x,
        "minus_x": minus_x,
        "plus_y": plus_y,
        "minus_y": minus_y,
        "plus_z": plus_z,
        "minus_z": minus_z,
        "pos_y": pos_y,
        "first_cols": inverse,
        "last_cols": inverse,
    }


def node_weights(tables, points):
    node_ids = jnp.arange(points)
    end_node = (node_ids == 0) | (node_ids == points - 1)
    edge_mult = jnp.where(end_node, 2.0, 1.0).astype(jnp.float32)
    pos_y = tables["pos_y"]
    low_shared = (node_ids == 0)[:, None] & (pos_y > 0)[None, :]
    high_shared = (node_ids == points - 1)[:, None] & (pos_y < EL_Y - 1)[None, :]
    mid_mult = jnp.where(low_shared | high_shared, 2.0, 1.0).astype(jnp.float32)
    return 1.0 / (
        edge_mult[:, None, None, None] * mid_mult[None, :, None, :] * edge_mult[None, None, :, None]
    )


def boundary_faces(values, tables):
    low_face = jnp.take(values[0], tables["first_cols"], axis=2)
    high_face = jnp.take(values[-1], tables["last_cols"], axis=2)
    return jnp.stack([low_face, high_face])


def assemble(values, tables, padded):
    low_face = values[0]
    high_face = values[-1]
    low_ext = jnp.concatenate([low_face, padded[3]], axis=2)
    high_ext = jnp.concatenate([high_face, padded[0]], axis=2)
    new_high = high_face + jnp.take(low_ext, tables["plus_x"], axis=2)
    new_low = low_face + jnp.take(high_ext, tables["minus_x"], axis=2)
    values = jnp.concatenate([new_low[None], values[1:-1], new_high[None]], axis=0)
    low_face = values[:, 0]
    high_face = values[:, -1]
    zero_column = jnp.zeros(low_face.shape[:2] + (1,), values.dtype)
    low_ext = jnp.concatenate([low_face, zero_column], axis=2)
    high_ext = jnp.concatenate([high_face, zero_column], axis=2)
    new_high = high_face + jnp.take(low_ext, tables["plus_y"], axis=2)
    new_low = low_face + jnp.take(high_ext, tables["minus_y"], axis=2)
    values = jnp.concatenate([new_low[:, None], values[:, 1:-1], new_high[:, None]], axis=1)
    low_face = values[:, :, 0]
    high_face = values[:, :, -1]
    new_high = high_face + jnp.take(low_face, tables["plus_z"], axis=2)
    new_low = low_face + jnp.take(high_face, tables["minus_z"], axis=2)
    return jnp.concatenate([new_low[:, :, None], values[:, :, 1:-1], new_high[:, :, None]], axis=2)


def on_device(load_terms, geometry, mass_terms, element_order):
    points = load_terms.shape[0]
    deriv_table = jnp.asarray(gll_derivative(points), jnp.float32)
    tables = build_tables(element_order)
    weight = node_weights(tables, points)
    diag_local = local_diagonal(geometry, mass_terms, deriv_table)
    stacked = jnp.stack([boundary_faces(load_terms, tables), boundary_faces(diag_local, tables)])
    both_faces = padded_2(stacked, ((SLAB, 1),), 1)
    load_padded = both_faces[0]
    diag_padded = both_faces[1]
    start = assemble(load_terms, tables, load_padded)
    inv_diag = 1.0 / assemble(diag_local, tables, diag_padded)

    def operate(values):
        local_part = local_apply(values, geometry, mass_terms, deriv_table)
        padded = padded_2(boundary_faces(local_part, tables), ((SLAB, 0),), 1)
        return assemble(local_part, tables, padded)

    ratio_sigma = spectrum_centre / spectrum_half
    step_vec = inv_diag * start / spectrum_centre
    precond = step_vec
    rho_prev = 1.0 / ratio_sigma
    rho_next = 1.0 / (2.0 * ratio_sigma - rho_prev)
    misfit = start - operate(precond)
    step_vec = rho_next * rho_prev * step_vec + 2.0 * rho_next / spectrum_half * inv_diag * misfit
    precond = precond + step_vec
    image_vec = operate(precond)
    numerator, denominator = (
        over_axes(jnp.sum(weight * start * precond), SLAB),
        over_axes(jnp.sum(weight * precond * image_vec), SLAB),
    )
    step_size = numerator / denominator
    return (step_size * precond, start - step_size * image_vec)


def solution(mesh):
    torus = Mesh(mesh.devices.reshape(8, 12, 4, 2), ("slab_0", "slab_1", "slab_2", "slab_3"))
    placed = (
        P(None, None, None, SLAB),
        P(None, None, None, None, SLAB),
        P(None, None, None, SLAB),
        P(SLAB, None),
    )
    return jax.shard_map(
        on_device,
        mesh=torus,
        in_specs=placed,
        out_specs=(P(None, None, None, SLAB), P(None, None, None, SLAB)),
        check_vma=False,
    )
```

profile of v0, /device:TPU:1, one launch (start us, length us, event | category | flops | bytes accessed | tf_op | source)
XLA Modules:
  0.0 235.8 jit_solution(11798250117350814003)
XLA Ops:
  0.6 1.3 fusion.54
  1.9 1.3 fusion.55
  4.2 1.1 fusion.66
  11.7 1.7 gather_fusion.6
  13.6 1.0 copy.50
  14.7 1.7 gather_fusion.7
  17.2 12.4 %collective-permute-start.1 = (f32[2,1,8,8,128]{4,3,2,1,0:T(8,128)S(1)}, f32[2,1,8,8,128]{4,3,2,1,0:T(8,128)S(1)}, u32[]{:S(2)}, u32[]{:S(2)}) collective-permute-start(f32[2,1,8,8,128]{4,3,2,1,0:T(8,128)S(1)} %get-tuple-element.71), channel_id=1, source_target_pairs={{1,0},{2,1},{3,2},{4,3},{5,4},{6,5},{7,6},{8,7},{9,8},{10,9},{11,1... | collective-permute-start | bytes 196616 | tf_op jit(solution)/shard_map/ppermute | solution.py:29
  29.6 1.9 collective-permute-start
  32.2 1.2 gather_fusion.4
  34.7 1.2 gather_fusion.5
  37.3 1.2 gather_fusion.2
  39.0 1.2 gather_fusion.3
  40.3 1.2 gather_fusion
  41.5 1.4 gather_fusion.1
  45.5 1.6 gather_fusion.17
  47.0 1.2 copy.84
  48.2 1.4 slice_bitcast_fusion.7
  50.1 1.6 gather_fusion.16
  51.6 1.2 copy.82
  53.3 1.6 gather_fusion.11
  54.8 1.2 copy.67
  56.5 1.6 gather_fusion.10
  58.1 1.2 copy.64
  66.4 1.0 copy.75
  67.4 2.5 %gather_fusion.14 = f32[128,8,8]{2,1,0:T(8,128)} fusion(f32[8,8,128]{1,0,2:T(8,128)} %copy.75, s32[1024]{0:T(1024)S(1)} %pad_clamp_fusion.2), kind=kCustom, calls=%fused_computation.6.clone | custom fusion | bytes 66048 | tf_op jit(solution)/shard_map/jit(_take)/gather | solution.py:169
  69.9 1.2 copy.76
  71.1 1.0 copy.77
  72.1 2.5 %gather_fusion.15 = f32[128,8,8]{2,1,0:T(8,128)} fusion(f32[8,8,128]{1,0,2:T(8,128)} %copy.77, s32[1024]{0:T(1024)S(1)} %pad_clamp_fusion), kind=kCustom, calls=%fused_computation.7.clone | custom fusion | bytes 66048 | tf_op jit(solution)/shard_map/jit(_take)/gather | solution.py:168
  74.6 1.2 copy.78
  75.8 1.0 copy.95
  76.9 2.5 %gather_fusion.21 = f32[128,8,8]{2,1,0:T(8,128)} fusion(f32[8,8,128]{1,0,2:T(8,128)} %copy.95, s32[1024]{0:T(1024)S(1)} %pad_clamp_fusion), kind=kCustom, calls=%fused_computation.9.clone | custom fusion | bytes 66048 | tf_op jit(solution)/shard_map/jit(_take)/gather | solution.py:168
  79.3 1.2 copy.96
  80.5 1.0 copy.93
  81.6 2.5 %gather_fusion.20 = f32[128,8,8]{2,1,0:T(8,128)} fusion(f32[8,8,128]{1,0,2:T(8,128)} %copy.93, s32[1024]{0:T(1024)S(1)} %pad_clamp_fusion.2), kind=kCustom, calls=%fused_computation.8.clone | custom fusion | bytes 66048 | tf_op jit(solution)/shard_map/jit(_take)/gather | solution.py:169
  84.0 1.2 copy.94
  89.7 2.5 %gather_fusion.24 = f32[128,8,8]{2,1,0:T(8,128)} fusion(f32[8,8,128]{1,0,2:T(8,128)} %copy.105, s32[1024]{0:T(1024)S(1)} %pad_clamp_fusion.11), kind=kCustom, calls=%fused_computation.11.clone | custom fusion | bytes 66048 | tf_op jit(solution)/shard_map/jit(_take)/gather | solution.py:145
  92.2 1.2 copy.106
  93.4 1.0 copy.101
  94.4 2.5 %gather_fusion.22 = f32[128,8,8]{2,1,0:T(8,128)} fusion(f32[8,8,128]{1,0,2:T(8,128)} %copy.101, s32[1024]{0:T(1024)S(1)} %pad_clamp_fusion.11), kind=kCustom, calls=%fused_computation.10.clone | custom fusion | bytes 66048 | tf_op jit(solution)/shard_map/jit(_take)/gather | solution.py:146
  96.9 1.2 copy.102
  98.8 10.1 %collective-permute-start.3 = (f32[1,8,8,128]{3,2,1,0:T(8,128)S(1)}, f32[1,8,8,128]{3,2,1,0:T(8,128)S(1)}, u32[]{:S(2)}, u32[]{:S(2)}) collective-permute-start(f32[1,8,8,128]{3,2,1,0:T(8,128)S(1)} %get-tuple-element.81), channel_id=1, source_target_pairs={{1,0},{2,1},{3,2},{4,3},{5,4},{6,5},{7,6},{8,7},{9,8},{10,9},{11,1... | collective-permute-start | bytes 98312 | tf_op jit(solution)/shard_map/ppermute | solution.py:29
  109.0 2.1 collective-permute-start.2
  111.3 1.4 copy.107
  112.7 2.8 %gather_fusion.25 = f32[128,8,8]{2,1,0:T(8,128)} fusion(f32[8,8,256]{1,0,2:T(8,128)} %copy.107, s32[1024]{0:T(1024)} %copy-done.15), kind=kCustom, calls=%fused_computation.22.clone | custom fusion | bytes 66048 | tf_op jit(solution)/shard_map/jit(_take)/gather | solution.py:155
  115.5 1.2 copy.108
  116.7 2.3 collective-permute-done.2
  119.0 1.4 copy.103
  120.3 2.8 %gather_fusion.23 = f32[128,8,8]{2,1,0:T(8,128)} fusion(f32[8,8,256]{1,0,2:T(8,128)} %copy.103, s32[1024]{0:T(1024)} %copy-done.14), kind=kCustom, calls=%fused_computation.21.clone | custom fusion | bytes 66048 | tf_op jit(solution)/shard_map/jit(_take)/gather | solution.py:156
  123.1 1.2 copy.104
  126.6 1.8 gather_fusion.26
  128.6 1.2 fusion.34
  131.7 1.8 gather_fusion.27
  135.7 1.0 copy.117
  136.7 1.8 gather_fusion.28
  139.4 1.4 fusion.32
  141.8 1.6 gather_fusion.29
  143.3 1.2 copy.120
  151.1 10.0 %collective-permute-start.5 = (f32[1,8,8,128]{3,2,1,0:T(8,128)S(1)}, f32[1,8,8,128]{3,2,1,0:T(8,128)S(1)}, u32[]{:S(2)}, u32[]{:S(2)}) collective-permute-start(f32[1,8,8,128]{3,2,1,0:T(8,128)S(1)} %get-tuple-element.79), channel_id=1, source_target_pairs={{1,0},{2,1},{3,2},{4,3},{5,4},{6,5},{7,6},{8,7},{9,8},{10,9},{11,1... | collective-permute-start | bytes 98312 | tf_op jit(solution)/shard_map/ppermute | solution.py:29
  161.2 1.9 collective-permute-start.4
  164.8 3.0 %collective-permute-done.4 = f32[1,8,8,128]{3,2,1,0:T(8,128)S(1)} collective-permute-done((f32[1,8,8,128]{3,2,1,0:T(8,128)S(1)}, f32[1,8,8,128]{3,2,1,0:T(8,128)S(1)}, u32[]{:S(2)}, u32[]{:S(2)}) %collective-permute-start.4) | collective-permute-done | bytes 32800 | tf_op jit(solution)/shard_map/ppermute | solution.py:26
  177.7 11.3 %all-reduce.9 = (f32[]{:T(128)}, f32[]{:T(128)}) all-reduce(f32[]{:T(128)} %get-tuple-element.10, f32[]{:T(128)} %get-tuple-element.9), channel_id=1, replica_groups=mesh['slab_0'=8,'slab_1'=12,'slab_2'=4,'slab_3'=2] {'slab_0'}, use_global_device_ids=true, to_apply=%region_2.6 | all-reduce | flops 2 | bytes 16 | tf_op jit(solution)/shard_map/psum | solution.py:35
  189.1 16.0 %all-reduce.8 = (f32[]{:T(128)}, f32[]{:T(128)}) all-reduce(f32[]{:T(128)} %get-tuple-element.13, f32[]{:T(128)} %get-tuple-element.14), channel_id=1, replica_groups=mesh['slab_0'=8,'slab_1'=12,'slab_2'=4,'slab_3'=2] {'slab_1'}, use_global_device_ids=true, to_apply=%region_3.7 | all-reduce | flops 2 | bytes 16 | tf_op jit(solution)/shard_map/psum | solution.py:35
  205.1 15.4 %all-reduce.10 = (f32[]{:T(128)}, f32[]{:T(128)}) all-reduce(f32[]{:T(128)} %get-tuple-element.11, f32[]{:T(128)} %get-tuple-element.12), channel_id=1, replica_groups=mesh['slab_0'=8,'slab_1'=12,'slab_2'=4,'slab_3'=2] {'slab_2'}, use_global_device_ids=true, to_apply=%region_4.8 | all-reduce | flops 2 | bytes 16 | tf_op jit(solution)/shard_map/psum | solution.py:35
  220.4 12.5 %all-reduce.11 = (f32[]{:T(128)}, f32[]{:T(128)}) all-reduce(f32[]{:T(128)} %get-tuple-element.15, f32[]{:T(128)} %get-tuple-element.16), channel_id=1, replica_groups=mesh['slab_0'=8,'slab_1'=12,'slab_2'=4,'slab_3'=2] {'slab_3'}, use_global_device_ids=true, to_apply=%region_5.9 | all-reduce | flops 2 | bytes 16 | tf_op jit(solution)/shard_map/psum | solution.py:35
  (255 shorter events, 55.8 us)
Async XLA Ops:
  0.6 4.7 %copy-start.1 = (f32[3,8,8,8,128]{4,3,2,1,0:T(8,128)S(1)}, f32[3,8,8,8,128]{4,3,2,1,0:T(8,128)}, u32[]{:S(2)}) copy-start(f32[3,8,8,8,128]{4,3,2,1,0:T(8,128)} %param.12) | copy-start | bytes 2359300
  4.2 12.4 %copy-start.31 = (pred[128]{0:T(512)(128)(4,1)}, pred[128]{0:T(512)(128)(4,1)S(1)}, u32[]{:S(2)}) copy-start(pred[128]{0:T(512)(128)(4,1)S(1)} %compare_and_fusion.6) | copy-start | bytes 388
  4.2 1.1 copy-start.11
  5.7 1.0 copy-start
  9.8 1.0 copy-start.2
  17.2 27.8 %collective-permute-start.1 = (f32[2,1,8,8,128]{4,3,2,1,0:T(8,128)S(1)}, f32[2,1,8,8,128]{4,3,2,1,0:T(8,128)S(1)}, u32[]{:S(2)}, u32[]{:S(2)}) collective-permute-start(f32[2,1,8,8,128]{4,3,2,1,0:T(8,128)S(1)} %get-tuple-element.71), channel_id=1, source_target_pairs={{1,0},{2,1},{3,2},{4,3},{5,4},{6,5},{7,6},{8,7},{9,8},{10,9},{11,1... | collective-permute-start | bytes 196616 | tf_op jit(solution)/shard_map/ppermute | solution.py:29
  29.6 18.6 %collective-permute-start = (f32[2,1,8,8,128]{4,3,2,1,0:T(8,128)}, f32[2,1,8,8,128]{4,3,2,1,0:T(8,128)}, u32[]{:S(2)}, u32[]{:S(2)}) collective-permute-start(f32[2,1,8,8,128]{4,3,2,1,0:T(8,128)} %get-tuple-element.70), channel_id=1, source_target_pairs={{0,1},{1,2},{2,3},{3,4},{4,5},{5,6},{6,7},{7,8},{8,9},{9,10},{10,1... | collective-permute-start | bytes 196616 | tf_op jit(solution)/shard_map/ppermute | solution.py:26
  31.6 0.7 copy-start.39
  34.0 0.7 copy-start.37
  34.0 0.7 copy-start.38
  36.0 0.7 copy-start.34
  36.6 0.6 copy-start.36
  41.5 2.0 slice-start
  43.5 15.8 %copy-start.22 = (pred[128]{0:T(512)(128)(4,1)}, pred[128]{0:T(512)(128)(4,1)S(1)}, u32[]{:S(2)}) copy-start(pred[128]{0:T(512)(128)(4,1)S(1)} %get-tuple-element.93) | copy-start | bytes 388
  43.5 15.8 %copy-start.25 = (pred[128]{0:T(512)(128)(4,1)}, pred[128]{0:T(512)(128)(4,1)S(1)}, u32[]{:S(2)}) copy-start(pred[128]{0:T(512)(128)(4,1)S(1)} %get-tuple-element.48) | copy-start | bytes 388
  43.5 9.7 %copy-start.15 = (s32[1024]{0:T(1024)}, s32[1024]{0:T(1024)S(1)}, u32[]{:S(2)}) copy-start(s32[1024]{0:T(1024)S(1)} %pad_clamp_fusion.8) | copy-start | bytes 12292
  43.6 12.9 %copy-start.14 = (s32[1024]{0:T(1024)}, s32[1024]{0:T(1024)S(1)}, u32[]{:S(2)}) copy-start(s32[1024]{0:T(1024)S(1)} %pad_clamp_fusion.10) | copy-start | bytes 12292
  43.7 16.0 %copy-start.13 = (s32[1024]{0:T(1024)}, s32[1024]{0:T(1024)S(1)}, u32[]{:S(2)}) copy-start(s32[1024]{0:T(1024)S(1)} %pad_clamp_fusion.6) | copy-start | bytes 12292
  44.3 37.2 %copy-start.12 = (s32[1024]{0:T(1024)}, s32[1024]{0:T(1024)S(1)}, u32[]{:S(2)}) copy-start(s32[1024]{0:T(1024)S(1)} %pad_clamp_fusion.2) | copy-start | bytes 12292
  51.6 1.2 copy-start.10
  58.0 1.3 copy-start.3
  62.1 0.6 copy-start.18
  65.5 0.7 copy-start.20
  69.9 1.2 copy-start.16
  84.0 1.2 copy-start.28
  85.5 0.7 copy-start.5
  96.9 1.2 copy-start.32
  98.8 12.5 %collective-permute-start.3 = (f32[1,8,8,128]{3,2,1,0:T(8,128)S(1)}, f32[1,8,8,128]{3,2,1,0:T(8,128)S(1)}, u32[]{:S(2)}, u32[]{:S(2)}) collective-permute-start(f32[1,8,8,128]{3,2,1,0:T(8,128)S(1)} %get-tuple-element.81), channel_id=1, source_target_pairs={{1,0},{2,1},{3,2},{4,3},{5,4},{6,5},{7,6},{8,7},{9,8},{10,9},{11,1... | collective-permute-start | bytes 98312 | tf_op jit(solution)/shard_map/ppermute | solution.py:29
  109.0 10.0 %collective-permute-start.2 = (f32[1,8,8,128]{3,2,1,0:T(8,128)}, f32[1,8,8,128]{3,2,1,0:T(8,128)S(1)}, u32[]{:S(2)}, u32[]{:S(2)}) collective-permute-start(f32[1,8,8,128]{3,2,1,0:T(8,128)} %get-tuple-element.80), channel_id=1, source_target_pairs={{0,1},{1,2},{2,3},{3,4},{4,5},{5,6},{6,7},{7,8},{8,9},{9,10},{10,1... | collective-permute-start | bytes 98312 | tf_op jit(solution)/shard_map/ppermute | solution.py:26
  123.1 1.2 copy-start.23
  123.1 1.2 copy-start.26
  125.1 0.6 copy-start.6
  135.1 0.6 copy-start.7
  143.3 1.3 copy-start.8
  143.3 1.3 copy-start.29
  143.3 1.3 copy-start.4
  144.6 0.8 copy-start.9
  150.5 0.6 copy-start.33
  151.1 10.0 %copy-start.35 = (f32[8]{0:T(128)S(1)}, f32[8]{0:T(128)}, u32[]{:S(2)}) copy-start(f32[8]{0:T(128)} %or_select_fusion.1) | copy-start | bytes 100
  151.1 12.1 %collective-permute-start.5 = (f32[1,8,8,128]{3,2,1,0:T(8,128)S(1)}, f32[1,8,8,128]{3,2,1,0:T(8,128)S(1)}, u32[]{:S(2)}, u32[]{:S(2)}) collective-permute-start(f32[1,8,8,128]{3,2,1,0:T(8,128)S(1)} %get-tuple-element.79), channel_id=1, source_target_pairs={{1,0},{2,1},{3,2},{4,3},{5,4},{6,5},{7,6},{8,7},{9,8},{10,9},{11,1... | collective-permute-start | bytes 98312 | tf_op jit(solution)/shard_map/ppermute | solution.py:29
  161.2 6.6 %collective-permute-start.4 = (f32[1,8,8,128]{3,2,1,0:T(8,128)S(1)}, f32[1,8,8,128]{3,2,1,0:T(8,128)S(1)}, u32[]{:S(2)}, u32[]{:S(2)}) collective-permute-start(f32[1,8,8,128]{3,2,1,0:T(8,128)S(1)} %get-tuple-element.78), channel_id=1, source_target_pairs={{0,1},{1,2},{2,3},{3,4},{4,5},{5,6},{6,7},{7,8},{8,9},{9,10},{10,1... | collective-permute-start | bytes 98312 | tf_op jit(solution)/shard_map/ppermute | solution.py:26
  169.1 0.6 copy-start.24
  169.1 0.6 copy-start.27
  171.0 0.6 copy-start.19
  172.9 0.6 copy-start.21
  174.7 0.6 copy-start.17
  176.3 0.7 copy-start.30
where the time goes:
time: 238 us; the launch traced here: 236 us
  local copies, waits for them, and re-layouts  113 us (47%)
  blocking collectives  55.2 us (23%)
  starting transfers between devices  38.5 us (16%)
  other arithmetic  13.6 us (6%)
  matrix products  6.62 us (3%)
  waiting for transfers between devices  5.32 us (2%)
  between operations  3.3 us (1%)
    psum x4, blocking collectives, over_axes(): return functools.reduce(lax.psum, axes, shard)  55.2 us
    ppermute x3, starting transfers between devices, padded_2(): lax.ppermute(lax.slice_in_dim(block, 0, width, axis=dim), axis, backward)  32.5 us
    unnamed x91, local copies, waits for them, and re-layouts  14 us
    gather x8, local copies, waits for them, and re-layouts, assemble(): new_high = high_face + jnp.take(low_face, tables['plus_z'], axis=2)  11.1 us
    gather x8, local copies, waits for them, and re-layouts, assemble(): new_low = low_face + jnp.take(high_face, tables['minus_z'], axis=2)  11 us
    gather x8, local copies, waits for them, and re-layouts, assemble(): new_low = low_face + jnp.take(high_ext, tables['minus_x'], axis=2)  10.6 us
    gather x8, local copies, waits for them, and re-layouts, assemble(): new_high = high_face + jnp.take(low_ext, tables['plus_x'], axis=2)  10.6 us
    gather x8, local copies, waits for them, and re-layouts, boundary_faces(): high_face = jnp.take(values[-1], tables['last_cols'], axis=2)  7.42 us
  transfers between devices with their start and end apart: 6, of which 2 were waited for; matrix products, arithmetic and copies ran while one was open for 9% of the time, Pallas kernels for 0%

commit v1 on v0

v1 whole, which is shorter than its diff:
```python
import functools

import jax
import jax.numpy as jnp
import numpy as np
from jax import lax
from jax.experimental import pallas as pl
from jax.experimental.pallas import tpu as pltpu
from jax.sharding import PartitionSpec as P

N = 8
EL_Y = 8
EL_Z = 16
LANES = 128
ROWS = N * N * N
FACE = N * N
CENTRE = 1.65
HALF = 1.35
MESH = pl.DeviceIdType.MESH
PHASES = ((8, 1), (8, 96), (12, 8))


def legendre_table(positions, points):
    columns = [positions * 0.0 + 1.0, positions]
    for degree in range(2, points):
        columns.append(
            ((2 * degree - 1) * positions * columns[-1] - (degree - 1) * columns[-2]) / degree
        )
    return np.stack(columns, axis=1)


def gll_derivative(points):
    degree = points - 1
    nodes = -np.cos(np.pi * np.arange(points) / degree)
    for _ in range(100):
        legendre = legendre_table(nodes, points)
        nodes = nodes - (nodes * legendre[:, degree] - legendre[:, degree - 1]) / (
            points * legendre[:, degree]
        )
    legendre = legendre_table(nodes, points)
    top = legendre[:, degree]
    same = np.eye(points, dtype=bool)
    spacing = np.where(same, 1.0, nodes[:, None] - nodes[None, :])
    table = np.where(same, 0.0, top[:, None] / (top[None, :] * spacing))
    table[0, 0] = -degree * points / 4.0
    table[degree, degree] = degree * points / 4.0
    return table


DERIV = gll_derivative(N).astype(np.float32).astype(np.float64)
SQUARED = DERIV * DERIV
SIGMA = CENTRE / HALF
RHO0 = 1.0 / SIGMA
RHO1 = 1.0 / (2.0 * SIGMA - RHO0)
COEF_Z = (1.0 + RHO1 * RHO0) / CENTRE + 2.0 * RHO1 / HALF
COEF_Q = 2.0 * RHO1 / HALF / CENTRE


def contract(table, terms, sign):
    half = N // 2
    even = [terms[j] + terms[N - 1 - j] for j in range(half)]
    odd = [terms[j] - terms[N - 1 - j] for j in range(half)]
    out = [None] * N
    for i in range(half):
        e = o = None
        for j in range(half):
            ce = float(table[i, j] + table[i, N - 1 - j]) / 2
            co = float(table[i, j] - table[i, N - 1 - j]) / 2
            e = ce * even[j] if e is None else e + ce * even[j]
            o = co * odd[j] if o is None else o + co * odd[j]
        out[i] = e + o
        out[N - 1 - i] = (o - e) if sign < 0 else (e - o)
    return out


def tile(row):
    return pl.ds(pl.multiple_of(row, 8), 8)


def normal(ref, a, b):
    return ref[tile((a * N + b) * N), :]


def across(a, c):
    return pl.ds(a * FACE + c, N, stride=N)


def stiffness(v, g0, g1, g2t, ms, out, tmp):
    def along_c(a, _):
        vt = [v[across(a, c), :] for c in range(N)]
        s = contract(DERIV, vt, -1)
        s = [s[c] * normal(g2t, a, c) for c in range(N)]
        s = contract(DERIV.T, s, -1)
        for c in range(N):
            tmp[across(a, c), :] = s[c]
        return 0

    lax.fori_loop(0, N, along_c, 0)

    def along_b(a, _):
        vb = [normal(v, a, b) for b in range(N)]
        s = contract(DERIV, vb, -1)
        s = [s[b] * normal(g1, a, b) for b in range(N)]
        s = contract(DERIV.T, s, -1)
        for b in range(N):
            out[tile((a * N + b) * N), :] = (
                s[b] + normal(ms, a, b) * vb[b] + normal(tmp, a, b)
            )
        return 0

    lax.fori_loop(0, N, along_b, 0)

    def along_a(b, _):
        va = [normal(v, a, b) for a in range(N)]
        s = contract(DERIV, va, -1)
        s = [s[a] * normal(g0, a, b) for a in range(N)]
        s = contract(DERIV.T, s, -1)
        for a in range(N):
            out[tile((a * N + b) * N), :] = normal(out, a, b) + s[a]
        return 0

    lax.fori_loop(0, N, along_a, 0)


def local_diagonal(g0, g1, g2t, ms, out, tmp):
    def along_c(a, _):
        s = contract(SQUARED.T, [normal(g2t, a, c) for c in range(N)], 1)
        for c in range(N):
            tmp[across(a, c), :] = s[c]
        return 0

    lax.fori_loop(0, N, along_c, 0)

    def along_b(a, _):
        s = contract(SQUARED.T, [normal(g1, a, b) for b in range(N)], 1)
        for b in range(N):
            out[tile((a * N + b) * N), :] = s[b] + normal(ms, a, b) + normal(tmp, a, b)
        return 0

    lax.fori_loop(0, N, along_b, 0)

    def along_a(b, _):
        s = contract(SQUARED.T, [normal(g0, a, b) for a in range(N)], 1)
        for a in range(N):
            out[tile((a * N + b) * N), :] = normal(out, a, b) + s[a]
        return 0

    lax.fori_loop(0, N, along_a, 0)


def assemble_yz(v):
    lane = lax.broadcasted_iota(jnp.int32, (8, LANES), 1)
    up = lane < LANES - EL_Z
    down = lane >= EL_Z
    wrap_up = (lane & (EL_Z - 1)) == EL_Z - 1
    wrap_down = (lane & (EL_Z - 1)) == 0

    def one(a, _):
        low = normal(v, a, 0)
        high = normal(v, a, N - 1)
        v[tile((a * N + N - 1) * N), :] = high + jnp.where(
            up, pltpu.roll(low, LANES - EL_Z, 1), 0.0
        )
        v[tile(a * FACE), :] = low + jnp.where(down, pltpu.roll(high, EL_Z, 1), 0.0)
        low = v[across(a, 0), :]
        high = v[across(a, N - 1), :]
        nxt = jnp.where(wrap_up, pltpu.roll(low, EL_Z - 1, 1), pltpu.roll(low, LANES - 1, 1))
        prv = jnp.where(wrap_down, pltpu.roll(high, LANES - EL_Z + 1, 1), pltpu.roll(high, 1, 1))
        v[across(a, N - 1), :] = high + nxt
        v[across(a, 0), :] = low + prv
        return 0

    lax.fori_loop(0, N, one, 0)


def lane_pick(x, idx):
    return jnp.take_along_axis(x, idx, axis=1, mode="promise_in_bounds")


def step_kernel(
    load_h, geom_h, mass_h, order_h, p_h, r_h, im_h, al_o,
    ld, g0, g1, g2, g2t, ms, r, dg, z, y, u, tmp,
    face_r, face_d, face_y, face_u, dots, got0, got1, got2,
    order_v, in_sems, out_sems, x_send, x_recv, s_send, s_recv,
):
    count = lax.axis_size("slab")
    me = lax.axis_index("slab")
    right = lax.rem(me + 1, count)
    left = lax.rem(me + count - 1, count)
    loads = [
        pltpu.make_async_copy(src, dst, in_sems.at[k])
        for k, (src, dst) in enumerate(
            (
                (order_h, order_v),
                (load_h, ld),
                (geom_h.at[0], g0),
                (geom_h.at[1], g1),
                (geom_h.at[2], g2),
                (mass_h, ms),
            )
        )
    ]
    for copy in loads:
        copy.start()

    peers = []
    for members, stride in PHASES:
        pos = lax.rem(me // stride, members)
        peers.append(
            [me + (lax.rem(pos + j, members) - pos) * stride for j in range(1, members)]
        )
    barrier = pltpu.get_barrier_semaphore()
    everyone = [left, right] + [q for ring in peers for q in ring]
    for q in everyone:
        pl.semaphore_signal(barrier, inc=1, device_id=(q,), device_id_type=MESH)

    loads[0].wait()
    order = jnp.broadcast_to(order_v[...], (8, LANES))
    hit = (
        jnp.broadcast_to(order_v[...], (LANES, LANES))
        == lax.broadcasted_iota(jnp.int32, (LANES, LANES), 0)
    ).astype(jnp.float32)
    columns = lax.broadcasted_iota(jnp.int32, (8, LANES), 1).astype(jnp.float32)
    inverse = lax.dot_general(
        columns, hit, (((1,), (1,)), ((), ())), preferred_element_type=jnp.float32
    )
    inverse = (inverse + 0.5).astype(jnp.int32)

    def reorder(src, dst, idx):
        def one(k, _):
            for i in range(4):
                rows = tile((k * 4 + i) * 8)
                dst[rows, :] = lane_pick(src[rows, :], idx)
            return 0

        lax.fori_loop(0, ROWS // 32, one, 0)

    loads[1].wait()
    reorder(ld, ld, inverse)

    def copy_rows(src, dst):
        def one(k, _):
            for i in range(8):
                rows = tile((k * 8 + i) * 8)
                dst[rows, :] = src[rows, :]
            return 0

        lax.fori_loop(0, ROWS // 64, one, 0)

    copy_rows(ld, r)
    assemble_yz(r)
    loads[2].wait()
    reorder(g0, g0, inverse)
    loads[3].wait()
    reorder(g1, g1, inverse)
    loads[4].wait()

    def turn(a, _):
        for c in range(N):
            g2t[tile((a * N + c) * N), :] = lane_pick(g2[across(a, c), :], inverse)
        return 0

    lax.fori_loop(0, N, turn, 0)
    loads[5].wait()
    reorder(ms, ms, inverse)
    local_diagonal(g0, g1, g2t, ms, dg, tmp)
    assemble_yz(dg)

    pl.semaphore_wait(barrier, len(everyone))

    low, high = pl.ds(0, FACE), pl.ds(ROWS - FACE, FACE)

    def exchange(v, faces, k):
        copies = [
            pltpu.make_async_remote_copy(
                src_ref=v.at[high if i == 0 else low],
                dst_ref=faces.at[i],
                send_sem=x_send.at[2 * k + i],
                recv_sem=x_recv.at[2 * k + i],
                device_id=(right if i == 0 else left,),
                device_id_type=MESH,
            )
            for i in range(2)
        ]
        for copy in copies:
            copy.start()
        return copies

    def merge(v, faces, copies):
        for copy in copies:
            copy.wait()
        v[low, :] = v[low, :] + faces[0]
        v[high, :] = v[high, :] + faces[1]

    first = exchange(r, face_r, 0)
    second = exchange(dg, face_d, 1)
    merge(r, face_r, first)
    merge(dg, face_d, second)

    def each(body, init=0, per=4):
        def one(k, carry):
            for i in range(per):
                carry = body(tile((k * per + i) * 8), carry)
            return carry

        return lax.fori_loop(0, ROWS // 8 // per, one, init)

    def to_z(rows, carry):
        inv = 1.0 / dg[rows, :]
        dg[rows, :] = inv
        z[rows, :] = inv * r[rows, :]
        return carry

    each(to_z)
    stiffness(z, g0, g1, g2t, ms, y, tmp)
    assemble_yz(y)
    third = exchange(y, face_y, 2)
    merge(y, face_y, third)

    def to_p(rows, carry):
        p = COEF_Z * z[rows, :] - COEF_Q * (dg[rows, :] * y[rows, :])
        z[rows, :] = p
        return carry + ld[rows, :] * p

    zero = jnp.zeros((8, LANES), jnp.float32)
    num = each(to_p, zero)
    stiffness(z, g0, g1, g2t, ms, u, tmp)
    den = each(lambda rows, carry: carry + z[rows, :] * u[rows, :], zero)
    dots[0, 0:1, :] = jnp.sum(num, axis=0, keepdims=True)
    dots[0, 1:2, :] = jnp.sum(den, axis=0, keepdims=True)

    gots = (got0, got1, got2)

    def spread(k):
        base = sum(m - 1 for m, _ in PHASES[:k])
        copies = [
            pltpu.make_async_remote_copy(
                src_ref=dots.at[k],
                dst_ref=gots[k].at[j],
                send_sem=s_send.at[base + j],
                recv_sem=s_recv.at[base + j],
                device_id=(q,),
                device_id_type=MESH,
            )
            for j, q in enumerate(peers[k])
        ]
        for copy in copies:
            copy.start()
        return copies

    def gather(k, copies):
        total = dots[k]
        for j, copy in enumerate(copies):
            copy.wait_recv()
        for j in range(len(copies)):
            total = total + gots[k][j]
        return total

    ring0 = spread(0)
    assemble_yz(u)
    fourth = exchange(u, face_u, 3)

    dots[1] = gather(0, ring0)
    ring1 = spread(1)
    reorder(z, y, order)
    reorder(r, tmp, order)
    puts = [
        pltpu.make_async_copy(y, p_h, out_sems.at[0]),
        pltpu.make_async_copy(tmp, r_h, out_sems.at[1]),
        pltpu.make_async_copy(u, im_h, out_sems.at[2]),
    ]
    puts[0].start()
    puts[1].start()
    dots[2] = gather(1, ring1)
    ring2 = spread(2)
    merge(u, face_u, fourth)
    reorder(u, u, order)
    puts[2].start()
    total = gather(2, ring2)
    sums = jnp.sum(total, axis=1, keepdims=True)
    al_o[...] = jnp.broadcast_to(sums[0:1, :] / sums[1:2, :], (8, LANES))
    for copy in ring0 + ring1 + ring2:
        copy.wait_send()
    for copy in puts:
        copy.wait()


def on_device(load_terms, geometry, mass_terms, element_order):
    flat = jax.ShapeDtypeStruct((ROWS, LANES), jnp.float32)
    vm = lambda *shape: pltpu.VMEM(shape, jnp.float32)
    field = vm(ROWS, LANES)
    face = vm(2, FACE, LANES)
    links = sum(m - 1 for m, _ in PHASES)
    p, r, im, alpha = pl.pallas_call(
        step_kernel,
        out_shape=(flat, flat, flat, jax.ShapeDtypeStruct((8, LANES), jnp.float32)),
        in_specs=[pl.BlockSpec(memory_space=pl.ANY)] * 4,
        out_specs=(
            *[pl.BlockSpec(memory_space=pl.ANY)] * 3,
            pl.BlockSpec(memory_space=pltpu.VMEM),
        ),
        scratch_shapes=[
            *[field] * 12,
            face, face, face, face,
            vm(3, 2, LANES), *[vm(m - 1, 2, LANES) for m, _ in PHASES],
            pltpu.VMEM((1, LANES), jnp.int32),
            pltpu.SemaphoreType.DMA((6,)),
            pltpu.SemaphoreType.DMA((3,)),
            pltpu.SemaphoreType.DMA((8,)),
            pltpu.SemaphoreType.DMA((8,)),
            pltpu.SemaphoreType.DMA((links,)),
            pltpu.SemaphoreType.DMA((links,)),
        ],
        compiler_params=pltpu.CompilerParams(collective_id=0, has_side_effects=True),
        name="cg_step",
    )(
        load_terms.reshape(ROWS, LANES),
        geometry.reshape(3, ROWS, LANES),
        mass_terms.reshape(ROWS, LANES),
        element_order,
    )
    alpha = alpha[0:1, :]
    shape = load_terms.shape
    return (alpha * p).reshape(shape), (r - alpha * im).reshape(shape)


def solution(mesh):
    last = P(None, None, None, "slab")
    return jax.shard_map(
        on_device,
        mesh=mesh,
        in_specs=(last, P(None, None, None, None, "slab"), last, P("slab", None)),
        out_specs=(last, last),
        check_vma=False,
    )
```

time: 238 us -> 52.6 us (0.22)
  local copies, waits for them, and re-layouts: 113 us -> 0.68 us
  blocking collectives: 55.2 us -> 0 us
  Pallas kernels: 0 us -> 49.1 us
  starting transfers between devices: 38.5 us -> 0 us
  other arithmetic: 13.6 us -> 1.94 us
  matrix products: 6.62 us -> 0 us
  waiting for transfers between devices: 5.32 us -> 0 us
  between operations: 3.3 us -> 0.64 us
    gather x70 -> x0, local copies, waits for them, and re-layouts: 76.7 us -> none  [the longest x8 11.1 us: assemble(): new_high = high_face + jnp.take(low_face, tables['plus_z'], axis=2)]
    psum x4 -> x0, blocking collectives: 55.2 us -> none  [over_axes(): return functools.reduce(lax.psum, axes, shard)]
    pallas_call x0 -> x1, Pallas kernels: none -> 49.1 us  [on_device(): pl.pallas_call(step_kernel, out_shape=(flat, flat, flat, jax.ShapeDtypeSt...]
    ppermute x6 -> x0, starting transfers between devices: 38.5 us -> none  [the longest x3 32.5 us: padded_2(): lax.ppermute(lax.slice_in_dim(block, 0, width, axis=dim), axis, backward)]
    unnamed x91 -> x0, local copies, waits for them, and re-layouts: 14 us -> none
    squeeze x22 -> x0, local copies, waits for them, and re-layouts: 13.1 us -> none  [the longest x5 3.33 us: assemble(): high_face = values[:, :, -1]]
    concatenate x16 -> x0, local copies, waits for them, and re-layouts: 7.09 us -> none  [the longest x4 2.59 us: assemble(): high_ext = jnp.concatenate([high_face, padded[0]], axis=2)]
    dot_general x15 -> x0, matrix products: 6.62 us -> none  [the longest x2 1.08 us: local_apply(): jnp.einsum('ma,abce->mbce', deriv_table, values, precision=highest)]
  transfers between devices with their start and end apart: 6 -> 0, of which waited for: 2 -> 0; matrix products, arithmetic and copies ran while one was open for 9% -> 0% of each run, Pallas kernels for 0% -> 0%
where the time goes in v1:
time: 52.6 us; the launch traced here: 52.4 us
  Pallas kernels  49.1 us (93%)
  other arithmetic  1.94 us (4%)
  local copies, waits for them, and re-layouts  0.68 us (1%)
  between operations  0.64 us (1%)
    pallas_call x1, Pallas kernels, on_device(): pl.pallas_call(step_kernel, out_shape=(flat, flat, flat, jax.ShapeDtypeSt...  49.1 us
    sub x1, other arithmetic, on_device(): return ((alpha * p).reshape(shape), (r - alpha * im).reshape(shape))  1.94 us

profile of v1, /device:TPU:1, one launch (start us, length us, event | category | flops | bytes accessed | tf_op | source)
XLA Modules:
  0.0 52.4 jit_solution(3606822631974951992)
XLA Ops:
  0.6 49.1 %cg_step.1 = (f32[512,128]{1,0:T(8,128)}, f32[512,128]{1,0:T(8,128)}, f32[512,128]{1,0:T(8,128)}, f32[8,128]{1,0:T(8,128)}) custom-call(f32[512,128]{1,0:T(8,128)} %bitcast.8, f32[3,512,128]{2,1,0:T(8,128)} %bitcast.7, f32[512,128]{1,0:T(8,128)} %bitcast.9, s32[1,128]{1,0:T(1,128)} %order_h.1), custom_call_target="tpu_custom_call" | custom-call | tf_op jit(solution)/shard_map/cg_step/pallas_call | solution.py:394
  49.7 0.7 %slice_bitcast_fusion = f32[128]{0:T(128)S(1)} fusion(f32[8,128]{1,0:T(8,128)} %get-tuple-element.6), kind=kLoop, calls=%fused_computation.2 | loop fusion | bytes 1024 | tf_op jit(solution)/shard_map/mul | solution.py:424
  50.4 1.9 %multiply_subtract_fusion = (f32[512,128]{1,0:T(8,128)}, f32[512,128]{1,0:T(8,128)}) fusion(f32[512,128]{1,0:T(8,128)} %get-tuple-element.8, f32[512,128]{1,0:T(8,128)} %get-tuple-element.9, f32[128]{0:T(128)S(1)} %slice_bitcast_fusion, f32[512,128]{1,0:T(8,128)} %get-tuple-element.7), kind=kLoop, calls=%fused_computation | loop fusion | flops 196608 | bytes 1311232 | tf_op jit(solution)/shard_map/sub | solution.py:424

commit v2 on v1

v2 whole, which is shorter than its diff:
```python
import functools

import jax
import jax.numpy as jnp
import numpy as np
from jax import lax
from jax.experimental import pallas as pl
from jax.experimental.pallas import tpu as pltpu
from jax.sharding import PartitionSpec as P

N = 8
LAST = N - 1
EL_Y = 8
EL_Z = 16
LANES = 128
ROWS = N * N * N
FACE = N * N
CENTRE = 1.65
HALF = 1.35
MESH = pl.DeviceIdType.MESH
PHASES = ((8, 1), (8, 96), (12, 8))
INSIDE = range(1, LAST)


def legendre_table(positions, points):
    columns = [positions * 0.0 + 1.0, positions]
    for degree in range(2, points):
        columns.append(
            ((2 * degree - 1) * positions * columns[-1] - (degree - 1) * columns[-2]) / degree
        )
    return np.stack(columns, axis=1)


def gll_derivative(points):
    degree = points - 1
    nodes = -np.cos(np.pi * np.arange(points) / degree)
    for _ in range(100):
        legendre = legendre_table(nodes, points)
        nodes = nodes - (nodes * legendre[:, degree] - legendre[:, degree - 1]) / (
            points * legendre[:, degree]
        )
    legendre = legendre_table(nodes, points)
    top = legendre[:, degree]
    same = np.eye(points, dtype=bool)
    spacing = np.where(same, 1.0, nodes[:, None] - nodes[None, :])
    table = np.where(same, 0.0, top[:, None] / (top[None, :] * spacing))
    table[0, 0] = -degree * points / 4.0
    table[degree, degree] = degree * points / 4.0
    return table


DERIV = gll_derivative(N).astype(np.float32).astype(np.float64)
SQUARED = DERIV * DERIV
SIGMA = CENTRE / HALF
RHO0 = 1.0 / SIGMA
RHO1 = 1.0 / (2.0 * SIGMA - RHO0)
COEF_Z = (1.0 + RHO1 * RHO0) / CENTRE + 2.0 * RHO1 / HALF
COEF_Q = 2.0 * RHO1 / HALF / CENTRE


def plus(x, y):
    return y if x is None else x + y


def contract(table, terms, sign, rows=range(N)):
    used = [j for j in range(N // 2) if terms[j] is not None]
    even = {j: terms[j] + terms[LAST - j] for j in used}
    odd = {j: terms[j] - terms[LAST - j] for j in used}
    out = [None] * N
    for i in range(N // 2):
        if i not in rows and LAST - i not in rows:
            continue
        e = o = None
        for j in used:
            e = plus(e, float(table[i, j] + table[i, LAST - j]) / 2 * even[j])
            o = plus(o, float(table[i, j] - table[i, LAST - j]) / 2 * odd[j])
        if i in rows:
            out[i] = e + o
        if LAST - i in rows:
            out[LAST - i] = (o - e) if sign < 0 else (e - o)
    return out


def tile(row):
    return pl.ds(row if isinstance(row, int) else pl.multiple_of(row, 8), 8)


def at(a, b):
    return tile((a * N + b) * N)


def across(a, c):
    return pl.ds(a * FACE + c, N, stride=N)


def loop(start, stop, body):
    lax.fori_loop(start, stop, lambda i, _: (body(i), 0)[1], 0)


def inner_stiffness(v, g0, g1, g2t, ms, out, tmp):
    def along_c(a):
        s = contract(DERIV, [v[across(a, c), :] for c in range(N)], -1)
        s = contract(DERIV.T, [s[c] * g2t[at(a, c), :] for c in range(N)], -1)
        for c in range(N):
            tmp[across(a, c), :] = s[c]

    loop(1, LAST, along_c)

    def along_b(a):
        vb = [v[at(a, b), :] for b in range(N)]
        s = contract(DERIV, vb, -1)
        s = contract(DERIV.T, [s[b] * g1[at(a, b), :] for b in range(N)], -1)
        for b in range(N):
            out[at(a, b), :] = s[b] + ms[at(a, b), :] * vb[b] + tmp[at(a, b), :]

    loop(1, LAST, along_b)

    def along_a(b):
        va = [v[at(a, b), :] if a in INSIDE else None for a in range(N)]
        s = contract(DERIV, va, -1)
        s = contract(DERIV.T, [s[a] * g0[at(a, b), :] for a in range(N)], -1)
        for a in range(N):
            out[at(a, b), :] = out[at(a, b), :] + s[a] if a in INSIDE else s[a]

    loop(0, N, along_a)


def inner_diagonal(g0, g1, g2t, ms, out, tmp, ends, cross):
    def along_c(a):
        s = contract(SQUARED.T, [g2t[at(a, c), :] for c in range(N)], 1)
        for c in range(N):
            tmp[across(a, c), :] = s[c]

    loop(1, LAST, along_c)

    def along_b(a):
        s = contract(SQUARED.T, [g1[at(a, b), :] for b in range(N)], 1)
        for b in range(N):
            out[at(a, b), :] = s[b] + ms[at(a, b), :] + tmp[at(a, b), :]

    loop(1, LAST, along_b)

    def along_a(b):
        g = [g0[at(a, b), :] for a in range(N)]
        s = contract(SQUARED.T, g, 1)
        for a in INSIDE:
            out[at(a, b), :] = out[at(a, b), :] + s[a]
        ends[at(0, b), :] = s[0] + ms[at(0, b), :]
        ends[at(1, b), :] = s[LAST] + ms[at(LAST, b), :]
        both = None
        for m in range(N):
            both = plus(both, float(DERIV[m, 0] * DERIV[m, LAST]) * g[m])
        cross[at(0, b), :] = both

    loop(0, N, along_a)


def end_stiffness(v, g1, g2t, ends, cross, tmp):
    for f, a in ((0, 0), (1, LAST)):
        s = contract(DERIV, [v[across(f, c), :] for c in range(N)], -1)
        s = contract(DERIV.T, [s[c] * g2t[at(a, c), :] for c in range(N)], -1)
        for c in range(N):
            tmp[across(f, c), :] = s[c]
    out = []
    for f, a in ((0, 0), (1, LAST)):
        vb = [v[at(f, b), :] for b in range(N)]
        s = contract(DERIV, vb, -1)
        s = contract(DERIV.T, [s[b] * g1[at(a, b), :] for b in range(N)], -1)
        out.append(
            [
                s[b]
                + ends[at(f, b), :] * vb[b]
                + cross[at(0, b), :] * v[at(1 - f, b), :]
                + tmp[at(f, b), :]
                for b in range(N)
            ]
        )
    return out


def add_ends_inside(v, g0, out):
    def one(b):
        ends = [None] * N
        ends[0], ends[LAST] = v[at(0, b), :], v[at(1, b), :]
        s = contract(DERIV, ends, -1)
        s = contract(DERIV.T, [s[a] * g0[at(a, b), :] for a in range(N)], -1, INSIDE)
        for a in INSIDE:
            out[at(a, b), :] = out[at(a, b), :] + s[a]

    loop(0, N, one)


def lane_pick(x, idx):
    return jnp.take_along_axis(x, idx, axis=1, mode="promise_in_bounds")


def sum_yz(v, planes, lanes):
    for a in planes:
        low, high = v[at(a, 0), :], v[at(a, LAST), :]
        v[at(a, LAST), :] = high + jnp.where(lanes["up"], pltpu.roll(low, LANES - EL_Z, 1), 0.0)
        v[at(a, 0), :] = low + jnp.where(lanes["down"], pltpu.roll(high, EL_Z, 1), 0.0)
    lows = [v[across(a, 0), :] for a in planes]
    highs = [v[across(a, LAST), :] for a in planes]
    nexts = [lane_pick(low, lanes["next"]) for low in lows]
    prevs = [lane_pick(high, lanes["prev"]) for high in highs]
    for k, a in enumerate(planes):
        v[across(a, LAST), :] = highs[k] + nexts[k]
        v[across(a, 0), :] = lows[k] + prevs[k]


def step_kernel(
    load_h, geom_h, mass_h, order_h, p_o, r_o, im_o, al_o,
    ld, g0, g1, g2, g2t, ms, r, dg, z, y, u, tmp,
    r_got, d_got, y_got, u_got, zf, pf, tmpf, ends, cross, dots, got0, got1, got2,
    order_v, in_sems, x_send, x_recv, s_send, s_recv,
):
    stack = []

    def scope(name):
        if stack:
            stack.pop().__exit__(None, None, None)
        if name:
            stack.append(jax.named_scope(name))
            stack[-1].__enter__()

    scope("enter")
    count = lax.axis_size("slab")
    me = lax.axis_index("slab")
    right = lax.rem(me + 1, count)
    left = lax.rem(me + count - 1, count)
    loads = [
        pltpu.make_async_copy(src, dst, in_sems.at[k])
        for k, (src, dst) in enumerate(
            (
                (order_h, order_v),
                (load_h, ld),
                (geom_h.at[0], g0),
                (geom_h.at[1], g1),
                (geom_h.at[2], g2),
                (mass_h, ms),
            )
        )
    ]
    for copy in loads:
        copy.start()

    peers = []
    for members, stride in PHASES:
        pos = lax.rem(me // stride, members)
        peers.append(
            [me + (lax.rem(pos + j, members) - pos) * stride for j in range(1, members)]
        )
    barrier = pltpu.get_barrier_semaphore()
    everyone = [left, right] + [q for ring in peers for q in ring]
    for q in everyone:
        pl.semaphore_signal(barrier, inc=1, device_id=(q,), device_id_type=MESH)

    scope("idx")
    loads[0].wait()
    order = jnp.broadcast_to(order_v[...], (8, LANES))
    hit = (
        jnp.broadcast_to(order_v[...], (LANES, LANES))
        == lax.broadcasted_iota(jnp.int32, (LANES, LANES), 0)
    ).astype(jnp.float32)
    lane = lax.broadcasted_iota(jnp.int32, (8, LANES), 1)
    inverse = lax.dot_general(
        lane.astype(jnp.float32), hit, (((1,), (1,)), ((), ())), preferred_element_type=jnp.float32
    )
    inverse = (inverse + 0.5).astype(jnp.int32)
    in_row = lane & (EL_Z - 1)
    lanes = {
        "up": lane < LANES - EL_Z,
        "down": lane >= EL_Z,
        "next": lane - in_row + ((in_row + 1) & (EL_Z - 1)),
        "prev": lane - in_row + ((in_row + EL_Z - 1) & (EL_Z - 1)),
    }

    def reorder(src, dst, idx, planes=range(N)):
        for a in planes:
            for b in range(N):
                dst[at(a, b), :] = lane_pick(src[at(a, b), :], idx)

    def exchange(v, got, k):
        copies = [
            pltpu.make_async_remote_copy(
                src_ref=v.at[pl.ds(ROWS - FACE if i == 0 else 0, FACE)],
                dst_ref=got.at[pl.ds(i * FACE, FACE)],
                send_sem=x_send.at[2 * k + i],
                recv_sem=x_recv.at[2 * k + i],
                device_id=(right if i == 0 else left,),
                device_id_type=MESH,
            )
            for i in range(2)
        ]
        for copy in copies:
            copy.start()
        return copies

    planes = ((0, 0), (1, LAST))
    both = (0, LAST)
    scope("load_ends")
    loads[1].wait()
    reorder(ld, r, inverse, both)
    sum_yz(r, both, lanes)
    scope("barrier")
    pl.semaphore_wait(barrier, len(everyone))
    scope("diag_ends")
    first = exchange(r, r_got, 0)
    for copy in loads[2:]:
        copy.wait()
    for f, a in planes:
        s = contract(SQUARED.T, [g2[across(a, c), :] for c in range(N)], 1)
        for c in range(N):
            tmpf[across(f, c), :] = s[c]
    for b in range(N):
        s = contract(SQUARED.T, [g0[at(a, b), :] for a in range(N)], 1, both)
        for a in both:
            dg[at(a, b), :] = s[a]
    for f, a in planes:
        s = contract(SQUARED.T, [g1[at(a, b), :] for b in range(N)], 1)
        for b in range(N):
            rows = at(a, b)
            dg[rows, :] = lane_pick(
                s[b] + dg[rows, :] + ms[rows, :] + tmpf[at(f, b), :], inverse
            )
    sum_yz(dg, both, lanes)
    second = exchange(dg, d_got, 1)

    scope("reorder")
    reorder(ld, ld, inverse)
    reorder(g0, g0, inverse)
    reorder(g1, g1, inverse)
    for a in range(N):
        for c in range(N):
            g2t[at(a, c), :] = lane_pick(g2[across(a, c), :], inverse)
    reorder(ms, ms, inverse)
    scope("diag")
    inner_diagonal(g0, g1, g2t, ms, dg, tmp, ends, cross)
    scope("sums")
    sum_yz(dg, INSIDE, lanes)
    for a in INSIDE:
        for b in (0, LAST):
            r[at(a, b), :] = ld[at(a, b), :]
    loop(1, LAST, lambda a: [r.__setitem__((at(a, b), slice(None)), ld[at(a, b), :]) for b in range(1, LAST)])
    sum_yz(r, INSIDE, lanes)

    def inner_z(a):
        for b in range(N):
            inv = 1.0 / dg[at(a, b), :]
            dg[at(a, b), :] = inv
            z[at(a, b), :] = inv * r[at(a, b), :]

    loop(1, LAST, inner_z)
    scope("L1")
    inner_stiffness(z, g0, g1, g2t, ms, y, tmp)

    scope("x1r")
    for copy in first:
        copy.wait()
    scope("x1d")
    for copy in second:
        copy.wait()
    scope("ends1")
    for f, a in planes:
        for b in range(N):
            total = r[at(a, b), :] + r_got[at(f, b), :]
            inv = 1.0 / (dg[at(a, b), :] + d_got[at(f, b), :])
            r[at(a, b), :] = total
            dg[at(a, b), :] = inv
            zf[at(f, b), :] = inv * total
    s = end_stiffness(zf, g1, g2t, ends, cross, tmpf)
    for f, a in planes:
        for b in range(N):
            y[at(a, b), :] = y[at(a, b), :] + s[f][b]
    sum_yz(y, both, lanes)
    third = exchange(y, y_got, 2)

    scope("inner2")
    add_ends_inside(zf, g0, y)
    sum_yz(y, INSIDE, lanes)

    def inner_p(a, num):
        for b in range(N):
            rows = at(a, b)
            p = COEF_Z * z[rows, :] - COEF_Q * (dg[rows, :] * y[rows, :])
            z[rows, :] = p
            num = num + ld[rows, :] * p
        return num

    zero = jnp.zeros((8, LANES), jnp.float32)
    num = lax.fori_loop(1, LAST, inner_p, zero)
    scope("L2")
    inner_stiffness(z, g0, g1, g2t, ms, u, tmp)

    def inner_den(a, den):
        for b in range(N):
            den = den + z[at(a, b), :] * u[at(a, b), :]
        return den

    den = lax.fori_loop(1, LAST, inner_den, zero)

    scope("x2")
    for copy in third:
        copy.wait()
    scope("ends2")
    for f, a in planes:
        for b in range(N):
            rows = at(f, b)
            p = COEF_Z * zf[rows, :] - COEF_Q * (
                dg[at(a, b), :] * (y[at(a, b), :] + y_got[rows, :])
            )
            pf[rows, :] = p
            num = num + ld[at(a, b), :] * p
    s = end_stiffness(pf, g1, g2t, ends, cross, tmpf)
    for f, a in planes:
        for b in range(N):
            old = u[at(a, b), :]
            new = old + s[f][b]
            den = den + pf[at(f, b), :] * (old + new)
            u[at(a, b), :] = new
    dots[0, 0:1, :] = jnp.sum(num, axis=0, keepdims=True)
    dots[0, 1:2, :] = jnp.sum(den, axis=0, keepdims=True)

    gots = (got0, got1, got2)

    def spread(k):
        base = sum(m - 1 for m, _ in PHASES[:k])
        copies = [
            pltpu.make_async_remote_copy(
                src_ref=dots.at[k],
                dst_ref=gots[k].at[j],
                send_sem=s_send.at[base + j],
                recv_sem=s_recv.at[base + j],
                device_id=(q,),
                device_id_type=MESH,
            )
            for j, q in enumerate(peers[k])
        ]
        for copy in copies:
            copy.start()
        return copies

    def gather(k, copies):
        total = dots[k]
        for copy in copies:
            copy.wait_recv()
        for j in range(len(copies)):
            total = total + gots[k][j]
        return total

    ring0 = spread(0)
    scope("u_ends")
    sum_yz(u, both, lanes)
    fourth = exchange(u, u_got, 3)
    add_ends_inside(pf, g0, u)
    scope("ar0")
    dots[1] = gather(0, ring0)
    ring1 = spread(1)
    scope("out_p_r")
    for f, a in planes:
        for b in range(N):
            z[at(a, b), :] = pf[at(f, b), :]
    reorder(z, p_o, order)
    reorder(r, r_o, order)
    sum_yz(u, INSIDE, lanes)
    reorder(u, im_o, order, INSIDE)
    scope("ar1")
    dots[2] = gather(1, ring1)
    ring2 = spread(2)
    scope("x3")
    for copy in fourth:
        copy.wait()
    for f, a in planes:
        for b in range(N):
            im_o[at(a, b), :] = lane_pick(u[at(a, b), :] + u_got[at(f, b), :], order)
    scope("ar2")
    total = gather(2, ring2)
    scope("alpha")
    sums = jnp.sum(total, axis=1, keepdims=True)
    al_o[...] = jnp.broadcast_to(sums[0:1, :] / sums[1:2, :], (8, LANES))
    for copy in ring0 + ring1 + ring2:
        copy.wait_send()
    scope(None)


def finish_kernel(p, r, im, al, x_o, r_o):
    alpha = al[...]

    def one(k):
        for i in range(N):
            rows = tile((k * N + i) * N)
            x_o[rows, :] = alpha * p[rows, :]
            r_o[rows, :] = r[rows, :] - alpha * im[rows, :]

    loop(0, N, one)


def on_device(load_terms, geometry, mass_terms, element_order):
    flat = jax.ShapeDtypeStruct((ROWS, LANES), jnp.float32)
    vm = lambda *shape: pltpu.VMEM(shape, jnp.float32)
    field = vm(ROWS, LANES)
    pair = vm(2 * FACE, LANES)
    links = sum(m - 1 for m, _ in PHASES)
    in_vmem = pl.BlockSpec(memory_space=pltpu.VMEM)
    parts = pl.pallas_call(
        step_kernel,
        out_shape=(flat, flat, flat, jax.ShapeDtypeStruct((8, LANES), jnp.float32)),
        in_specs=[pl.BlockSpec(memory_space=pl.ANY)] * 4,
        out_specs=[in_vmem] * 4,
        scratch_shapes=[
            *[field] * 12,
            *[pair] * 8, vm(FACE, LANES),
            vm(3, 2, LANES), *[vm(m - 1, 2, LANES) for m, _ in PHASES],
            pltpu.VMEM((1, LANES), jnp.int32),
            pltpu.SemaphoreType.DMA((6,)),
            pltpu.SemaphoreType.DMA((8,)),
            pltpu.SemaphoreType.DMA((8,)),
            pltpu.SemaphoreType.DMA((links,)),
            pltpu.SemaphoreType.DMA((links,)),
        ],
        compiler_params=pltpu.CompilerParams(collective_id=0, has_side_effects=True),
        name="cg_step",
    )(
        load_terms.reshape(ROWS, LANES),
        geometry.reshape(3, ROWS, LANES),
        mass_terms.reshape(ROWS, LANES),
        element_order,
    )
    x, res = pl.pallas_call(
        finish_kernel,
        out_shape=(flat, flat),
        in_specs=[in_vmem] * 4,
        out_specs=[in_vmem] * 2,
        name="cg_finish",
    )(*parts)
    shape = load_terms.shape
    return x.reshape(shape), res.reshape(shape)


def solution(mesh):
    last = P(None, None, None, "slab")
    return jax.shard_map(
        on_device,
        mesh=mesh,
        in_specs=(last, P(None, None, None, None, "slab"), last, P("slab", None)),
        out_specs=(last, last),
        check_vma=False,
    )
```

time: 52.6 us -> 44.3 us (0.84)
  Pallas kernels: 49.1 us -> 43.5 us
  other arithmetic: 1.94 us -> 0 us
  local copies, waits for them, and re-layouts: 0.68 us -> 0 us
    pallas_call x1, Pallas kernels: 49.1 us -> 41.5 us  [on_device(): pl.pallas_call(step_kernel, out_shape=(flat, flat, flat, jax.ShapeDtypeSt...]
    pallas_call x0 -> x1, Pallas kernels: none -> 1.97 us  [on_device(): pl.pallas_call(finish_kernel, out_shape=(flat, flat), in_specs=[in_vmem]...]
    sub x1 -> x0, other arithmetic: 1.94 us -> none  [on_device(): return ((alpha * p).reshape(shape), (r - alpha * im).reshape(shape))]
    mul x1 -> x0, local copies, waits for them, and re-layouts: 0.68 us -> none  [on_device(): return ((alpha * p).reshape(shape), (r - alpha * im).reshape(shape))]
where the time goes in v2:
time: 44.3 us; the launch traced here: 44.1 us
  Pallas kernels  43.5 us (98%)
  between operations  0.64 us (1%)
    pallas_call x1, Pallas kernels, on_device(): pl.pallas_call(step_kernel, out_shape=(flat, flat, flat, jax.ShapeDtypeSt...  41.5 us
    pallas_call x1, Pallas kernels, on_device(): pl.pallas_call(finish_kernel, out_shape=(flat, flat), in_specs=[in_vmem]...  1.97 us

profile of v2, /device:TPU:1, one launch (start us, length us, event | category | flops | bytes accessed | tf_op | source)
XLA Modules:
  0.0 44.1 jit_solution(15679555427842311394)
XLA Ops:
  0.6 41.5 %cg_step.1 = (f32[512,128]{1,0:T(8,128)}, f32[512,128]{1,0:T(8,128)}, f32[512,128]{1,0:T(8,128)}, f32[8,128]{1,0:T(8,128)}) custom-call(f32[512,128]{1,0:T(8,128)} %bitcast.6, f32[3,512,128]{2,1,0:T(8,128)} %bitcast.5, f32[512,128]{1,0:T(8,128)} %bitcast.7, s32[1,128]{1,0:T(1,128)} %order_h.1), custom_call_target="tpu_custom_call" | custom-call | tf_op jit(solution)/shard_map/cg_step/pallas_call | solution.py:505
  42.2 2.0 %cg_finish.1 = (f32[512,128]{1,0:T(8,128)}, f32[512,128]{1,0:T(8,128)}) custom-call(f32[512,128]{1,0:T(8,128)} %get-tuple-element.8.p, f32[512,128]{1,0:T(8,128)} %get-tuple-element.9.r, f32[512,128]{1,0:T(8,128)} %get-tuple-element.10.im, f32[8,128]{1,0:T(8,128)} %get-tuple-element.11.al), custom_call_target="tpu_custom_call" | custom-call | tf_op jit(solution)/shard_map/cg_finish/pallas_call | solution.py:529

commit v3 on v2

v3 whole, which is shorter than its diff:
```python
import functools

import jax
import jax.numpy as jnp
import numpy as np
from jax import lax
from jax.experimental import pallas as pl
from jax.experimental.pallas import tpu as pltpu
from jax.sharding import PartitionSpec as P

N = 8
LAST = N - 1
EL_Y = 8
EL_Z = 16
LANES = 128
ROWS = N * N * N
FACE = N * N
CENTRE = 1.65
HALF = 1.35
MESH = pl.DeviceIdType.MESH
TORUS = (8, 12, 4, 2)
INSIDE = range(1, LAST)


def legendre_table(positions, points):
    columns = [positions * 0.0 + 1.0, positions]
    for degree in range(2, points):
        columns.append(
            ((2 * degree - 1) * positions * columns[-1] - (degree - 1) * columns[-2]) / degree
        )
    return np.stack(columns, axis=1)


def gll_derivative(points):
    degree = points - 1
    nodes = -np.cos(np.pi * np.arange(points) / degree)
    for _ in range(100):
        legendre = legendre_table(nodes, points)
        nodes = nodes - (nodes * legendre[:, degree] - legendre[:, degree - 1]) / (
            points * legendre[:, degree]
        )
    legendre = legendre_table(nodes, points)
    top = legendre[:, degree]
    same = np.eye(points, dtype=bool)
    spacing = np.where(same, 1.0, nodes[:, None] - nodes[None, :])
    table = np.where(same, 0.0, top[:, None] / (top[None, :] * spacing))
    table[0, 0] = -degree * points / 4.0
    table[degree, degree] = degree * points / 4.0
    return table


DERIV = gll_derivative(N).astype(np.float32).astype(np.float64)
SQUARED = DERIV * DERIV
SIGMA = CENTRE / HALF
RHO0 = 1.0 / SIGMA
RHO1 = 1.0 / (2.0 * SIGMA - RHO0)
COEF_Z = (1.0 + RHO1 * RHO0) / CENTRE + 2.0 * RHO1 / HALF
COEF_Q = 2.0 * RHO1 / HALF / CENTRE


def plus(x, y):
    return y if x is None else x + y


def contract(table, terms, sign, rows=range(N)):
    used = [j for j in range(N // 2) if terms[j] is not None]
    even = {j: terms[j] + terms[LAST - j] for j in used}
    odd = {j: terms[j] - terms[LAST - j] for j in used}
    out = [None] * N
    for i in range(N // 2):
        if i not in rows and LAST - i not in rows:
            continue
        e = o = None
        for j in used:
            e = plus(e, float(table[i, j] + table[i, LAST - j]) / 2 * even[j])
            o = plus(o, float(table[i, j] - table[i, LAST - j]) / 2 * odd[j])
        if i in rows:
            out[i] = e + o
        if LAST - i in rows:
            out[LAST - i] = (o - e) if sign < 0 else (e - o)
    return out


def tile(row):
    return pl.ds(row if isinstance(row, int) else pl.multiple_of(row, 8), 8)


def at(a, b):
    return tile((a * N + b) * N)


def across(a, c):
    return pl.ds(a * FACE + c, N, stride=N)


LOAD, DIAG, G1, G2 = range(4)


def part(f, kind, i):
    return tile(((f * 4 + kind) * N + i) * N)


def loop(start, stop, body):
    lax.fori_loop(start, stop, lambda i, _: (body(i), 0)[1], 0)


def inner_stiffness(v, g0, g1, g2t, ms, out, tmp):
    def along_c(a):
        s = contract(DERIV, [v[across(a, c), :] for c in range(N)], -1)
        s = contract(DERIV.T, [s[c] * g2t[at(a, c), :] for c in range(N)], -1)
        for c in range(N):
            tmp[across(a, c), :] = s[c]

    loop(1, LAST, along_c)

    def along_b(a):
        vb = [v[at(a, b), :] for b in range(N)]
        s = contract(DERIV, vb, -1)
        s = contract(DERIV.T, [s[b] * g1[at(a, b), :] for b in range(N)], -1)
        for b in range(N):
            out[at(a, b), :] = s[b] + ms[at(a, b), :] * vb[b] + tmp[at(a, b), :]

    loop(1, LAST, along_b)

    def along_a(b):
        va = [v[at(a, b), :] if a in INSIDE else None for a in range(N)]
        s = contract(DERIV, va, -1)
        s = contract(DERIV.T, [s[a] * g0[at(a, b), :] for a in range(N)], -1)
        for a in range(N):
            out[at(a, b), :] = out[at(a, b), :] + s[a] if a in INSIDE else s[a]

    loop(0, N, along_a)


def inner_diagonal(g0, g1, g2t, ms, out, tmp, cross):
    def along_c(a):
        s = contract(SQUARED.T, [g2t[at(a, c), :] for c in range(N)], 1)
        for c in range(N):
            tmp[across(a, c), :] = s[c]

    loop(1, LAST, along_c)

    def along_b(a):
        s = contract(SQUARED.T, [g1[at(a, b), :] for b in range(N)], 1)
        for b in range(N):
            out[at(a, b), :] = s[b] + ms[at(a, b), :] + tmp[at(a, b), :]

    loop(1, LAST, along_b)

    def along_a(b):
        g = [g0[at(a, b), :] for a in range(N)]
        s = contract(SQUARED.T, g, 1, INSIDE)
        for a in INSIDE:
            out[at(a, b), :] = out[at(a, b), :] + s[a]
        both = None
        for m in range(N):
            both = plus(both, float(DERIV[m, 0] * DERIV[m, LAST]) * g[m])
        cross[at(0, b), :] = both

    loop(0, N, along_a)


def face_terms(v, f, mine, theirs, a_sum, tmp):
    s = contract(DERIV, [v[across(f, c), :] for c in range(N)], -1)
    s = contract(DERIV.T, [s[c] * theirs[part(f, G2, c), :] for c in range(N)], -1)
    for c in range(N):
        tmp[across(f, c), :] = s[c]
    vb = [v[at(f, b), :] for b in range(N)]
    s = contract(DERIV, vb, -1)
    s = contract(DERIV.T, [s[b] * theirs[part(f, G1, b), :] for b in range(N)], -1)
    return [s[b] + a_sum[at(f, b), :] * vb[b] + tmp[at(f, b), :] for b in range(N)]


def face_sums(f, mine, theirs, diag, a_sum, tmp):
    g = [[mine[part(f, k, i), :] + theirs[part(f, k, i), :] for i in range(N)] for k in (G1, G2)]
    for k in (G1, G2):
        for i in range(N):
            theirs[part(f, k, i), :] = g[k - G1][i]
    s = contract(SQUARED.T, g[1], 1)
    for c in range(N):
        tmp[across(f, c), :] = s[c]
    s = contract(SQUARED.T, g[0], 1)
    for b in range(N):
        a_sum[at(f, b), :] = diag[at(f, b), :] - s[b] - tmp[at(f, b), :]


def add_ends_inside(v, first, g0, out):
    def one(b):
        ends = [None] * N
        ends[0] = v[tile(first + b * N), :]
        ends[LAST] = v[tile(FACE - first + b * N), :]
        s = contract(DERIV, ends, -1)
        s = contract(DERIV.T, [s[a] * g0[at(a, b), :] for a in range(N)], -1, INSIDE)
        for a in INSIDE:
            out[at(a, b), :] = out[at(a, b), :] + s[a]

    loop(0, N, one)


def lane_pick(x, idx):
    return jnp.take_along_axis(x, idx, axis=1, mode="promise_in_bounds")


def sum_yz(planes, lanes):
    for v, a in planes:
        low, high = v[at(a, 0), :], v[at(a, LAST), :]
        v[at(a, LAST), :] = high + jnp.where(lanes["up"], pltpu.roll(low, LANES - EL_Z, 1), 0.0)
        v[at(a, 0), :] = low + jnp.where(lanes["down"], pltpu.roll(high, EL_Z, 1), 0.0)
    lows = [v[across(a, 0), :] for v, a in planes]
    highs = [v[across(a, LAST), :] for v, a in planes]
    nexts = [lane_pick(low, lanes["next"]) for low in lows]
    prevs = [lane_pick(high, lanes["prev"]) for high in highs]
    for k, (v, a) in enumerate(planes):
        v[across(a, LAST), :] = highs[k] + nexts[k]
        v[across(a, 0), :] = lows[k] + prevs[k]


def step_kernel(
    load_h, geom_h, mass_h, order_h, p_o, r_o, im_o, al_o,
    ld, g0, g1, g2, g2t, ms, r, dg, z, y, u, tmp,
    mine, theirs, w_mine, w_theirs, i_mine, i_theirs, rf, df, zf, pf, yf, a_sum, tmpf, cross,
    dots, got_a, got_b, order_v, in_sems, x_send, x_recv, s_send, s_recv, hello,
):
    stack = []

    def scope(name):
        if stack:
            stack.pop().__exit__(None, None, None)
        if name:
            stack.append(jax.named_scope(name))
            stack[-1].__enter__()

    scope("enter")
    ys, zs, xs, cores = TORUS
    count = lax.axis_size("slab")
    me = lax.axis_index("slab")
    core = lax.rem(me, cores)
    x = lax.rem(me // cores, xs)
    z_at = lax.rem(me // (cores * xs), zs)
    y_at = me // (cores * xs * zs)
    near_to = me + 1 - 2 * core
    far_to = lax.rem(me + count + 2 * core - 1, count)
    sides = (near_to, far_to)
    row_of = (pl.multiple_of((1 - core) * (ROWS - FACE), FACE), pl.multiple_of(core * (ROWS - FACE), FACE))
    face_of = {0: 1 - core, LAST: core}

    def moved(dy=0, dz=0, dx=0):
        to = me
        if dy:
            to = to + (lax.rem(y_at + dy, ys) - y_at) * (cores * xs * zs)
        if dz:
            to = to + (lax.rem(z_at + dz, zs) - z_at) * (cores * xs)
        if dx:
            to = to + (lax.rem(x + dx, xs) - x) * cores
        return to

    def ring(size, stop, start=1):
        return sorted({j % size for k in range(start, stop) for j in (k, -k)} - {0})

    def greet(sem, who):
        for q in who:
            pl.semaphore_signal(sem, inc=1, device_id=(q,), device_id_type=MESH)

    def heard(sem, who):
        if who:
            pl.semaphore_wait(sem, len(who))

    row = [moved(dx=k) + c for k in range(xs) for c in (0, 1 - 2 * core) if k or not isinstance(c, int)]
    y_near = [moved(dy=k) for k in ring(ys, 3)]
    z_near = [moved(dz=k) for k in ring(zs, 3)]
    barrier = pltpu.get_barrier_semaphore()
    near = [near_to, far_to] + row + y_near + z_near
    greet(barrier, near)
    loads = [
        pltpu.make_async_copy(src, dst, in_sems.at[k])
        for k, (src, dst) in enumerate(
            (
                (order_h, order_v),
                (load_h, ld),
                (geom_h.at[0], g0),
                (geom_h.at[1], g1),
                (geom_h.at[2], g2),
                (mass_h, ms),
            )
        )
    ]
    for copy in loads:
        copy.start()

    scope("idx")
    loads[0].wait()
    order = jnp.broadcast_to(order_v[...], (8, LANES))
    hit = (
        jnp.broadcast_to(order_v[...], (LANES, LANES))
        == lax.broadcasted_iota(jnp.int32, (LANES, LANES), 0)
    ).astype(jnp.float32)
    lane = lax.broadcasted_iota(jnp.int32, (8, LANES), 1)
    inverse = lax.dot_general(
        lane.astype(jnp.float32), hit, (((1,), (1,)), ((), ())), preferred_element_type=jnp.float32
    )
    inverse = (inverse + 0.5).astype(jnp.int32)
    in_row = lane & (EL_Z - 1)
    lanes = {
        "up": lane < LANES - EL_Z,
        "down": lane >= EL_Z,
        "next": lane - in_row + ((in_row + 1) & (EL_Z - 1)),
        "prev": lane - in_row + ((in_row + EL_Z - 1) & (EL_Z - 1)),
    }

    def reorder(src, dst, idx, planes=range(N)):
        for a in planes:
            for b in range(N):
                dst[at(a, b), :] = lane_pick(src[at(a, b), :], idx)

    def swap(src, dst, f, first, rows, k):
        copy = pltpu.make_async_remote_copy(
            src_ref=src.at[pl.ds(first, rows)],
            dst_ref=dst.at[pl.ds(first, rows)],
            send_sem=x_send.at[k, f],
            recv_sem=x_recv.at[k, f],
            device_id=(sides[f],),
            device_id_type=MESH,
        )
        copy.start()
        return copy

    both = (0, LAST)
    faces = (0, 1)
    started = []
    scope("load_ends")
    loads[1].wait()
    for a in both:
        for b in range(N):
            mine[part(face_of[a], LOAD, b), :] = lane_pick(ld[at(a, b), :], inverse)
    scope("barrier")
    pl.semaphore_wait(barrier, len(near))
    scope("diag_ends")
    sent_l = [swap(mine, theirs, f, f * 4 * FACE, FACE, 0) for f in faces]
    greet(hello.at[0], y_near)
    greet(hello.at[1], z_near)
    for copy in loads[2:]:
        copy.wait()
    for k, a in enumerate(both):
        s = contract(SQUARED.T, [g2[across(a, c), :] for c in range(N)], 1)
        for c in range(N):
            tmpf[across(k, c), :] = s[c]
    for b in range(N):
        s = contract(SQUARED.T, [g0[at(a, b), :] for a in range(N)], 1, both)
        for k, a in enumerate(both):
            yf[at(k, b), :] = s[a]
    for k, a in enumerate(both):
        s = contract(SQUARED.T, [g1[at(a, b), :] for b in range(N)], 1)
        for b in range(N):
            mine[part(face_of[a], DIAG, b), :] = lane_pick(
                s[b] + yf[at(k, b), :] + ms[at(a, b), :] + tmpf[at(k, b), :], inverse
            )
    sent_d = [swap(mine, theirs, f, (f * 4 + DIAG) * FACE, FACE, 1) for f in faces]
    for a in both:
        for i in range(N):
            mine[part(face_of[a], G1, i), :] = lane_pick(g1[at(a, i), :], inverse)
            mine[part(face_of[a], G2, i), :] = lane_pick(g2[across(a, i), :], inverse)
    sent_g = [swap(mine, theirs, f, (f * 4 + G1) * FACE, 2 * FACE, 2) for f in faces]

    scope("reorder")
    reorder(ld, ld, inverse, INSIDE)
    reorder(g0, g0, inverse)
    reorder(g1, g1, inverse, INSIDE)
    for a in INSIDE:
        for c in range(N):
            g2t[at(a, c), :] = lane_pick(g2[across(a, c), :], inverse)
    reorder(ms, ms, inverse, INSIDE)
    scope("diag")
    inner_diagonal(g0, g1, g2t, ms, dg, tmp, cross)
    scope("sums")
    sum_yz([(dg, a) for a in INSIDE], lanes)

    def copy_plane(a):
        for b in range(N):
            r[at(a, b), :] = ld[at(a, b), :]

    loop(1, LAST, copy_plane)
    sum_yz([(r, a) for a in INSIDE], lanes)

    def inner_z(a):
        for b in range(N):
            inv = 1.0 / dg[at(a, b), :]
            dg[at(a, b), :] = inv
            z[at(a, b), :] = inv * r[at(a, b), :]

    loop(1, LAST, inner_z)
    scope("L1")
    inner_stiffness(z, g0, g1, g2t, ms, y, tmp)

    def full(f, b):
        return tile(row_of[f] + b * N)

    def face_z(f):
        for b in range(N):
            rf[at(f, b), :] = mine[part(f, LOAD, b), :] + theirs[part(f, LOAD, b), :]
            total = mine[part(f, DIAG, b), :] + theirs[part(f, DIAG, b), :]
            a_sum[at(f, b), :] = total
            df[at(f, b), :] = total
        sum_yz([(rf, f), (df, f)], lanes)
        for b in range(N):
            inv = 1.0 / df[at(f, b), :]
            df[at(f, b), :] = inv
            zf[at(f, b), :] = inv * rf[at(f, b), :]

    def tell(f, v, ends, src, dst, k):
        for b in range(N):
            src[at(f, b), :] = v[full(f, b), :] + cross[at(0, b), :] * ends[at(1 - f, b), :]
        return swap(src, dst, f, f * FACE, FACE, k)

    scope("hello2")
    heard(hello.at[0], y_near)
    y_far = [moved(dy=k) for k in ring(ys, ys // 2 + 1, 3)]
    greet(hello.at[2], y_far)
    heard(hello.at[1], z_near)
    z_mid = [moved(dz=k) for k in ring(zs, 5, 3)]
    greet(hello.at[3], z_mid)
    scope("x_near")
    sent_l[0].wait()
    sent_d[0].wait()
    scope("z_near")
    face_z(0)
    sent_w = [None, tell(1, y, zf, w_mine, w_theirs, 3)]
    sent_g[0].wait()
    face_sums(0, mine, theirs, a_sum, a_sum, tmpf)
    s = face_terms(zf, 0, mine, theirs, a_sum, tmpf)
    for b in range(N):
        yf[at(0, b), :] = s[b]
    scope("x_far")
    sent_l[1].wait()
    sent_d[1].wait()
    scope("z_far")
    face_z(1)
    sent_w[0] = tell(0, y, zf, w_mine, w_theirs, 3)

    scope("inner2")
    first = pl.multiple_of((1 - core) * FACE, FACE)
    add_ends_inside(zf, first, g0, y)
    sum_yz([(y, a) for a in INSIDE], lanes)

    def inner_p(a, num):
        for b in range(N):
            rows = at(a, b)
            p = COEF_Z * z[rows, :] - COEF_Q * (dg[rows, :] * y[rows, :])
            z[rows, :] = p
            num = num + ld[rows, :] * p
        return num

    zero = jnp.zeros((8, LANES), jnp.float32)
    num = lax.fori_loop(1, LAST, inner_p, zero)
    scope("L2")
    inner_stiffness(z, g0, g1, g2t, ms, u, tmp)

    def inner_den(a, den):
        for b in range(N):
            den = den + z[at(a, b), :] * u[at(a, b), :]
        return den

    den = lax.fori_loop(1, LAST, inner_den, zero)
    scope("g_far")
    sent_g[1].wait()
    face_sums(1, mine, theirs, a_sum, a_sum, tmpf)
    s = face_terms(zf, 1, mine, theirs, a_sum, tmpf)
    for b in range(N):
        yf[at(1, b), :] = s[b]
    scope("hello3")
    heard(hello.at[3], z_mid)
    z_far = [moved(dz=k) for k in ring(zs, zs // 2 + 1, 5)]
    greet(hello.at[4], z_far)
    scope("w_far")
    sent_w[1].wait()
    scope("w_near")
    sent_w[0].wait()
    scope("ends2")
    for f in faces:
        for b in range(N):
            rows = at(f, b)
            yf[rows, :] = yf[rows, :] + (w_mine[rows, :] + w_theirs[rows, :])
    sum_yz([(yf, f) for f in faces], lanes)
    for f in faces:
        for b in range(N):
            rows = at(f, b)
            p = COEF_Z * zf[rows, :] - COEF_Q * (df[rows, :] * yf[rows, :])
            pf[rows, :] = p
            num = num + mine[part(f, LOAD, b), :] * p
    for f in faces:
        s = face_terms(pf, f, mine, theirs, a_sum, tmpf)
        for b in range(N):
            yf[at(f, b), :] = s[b]
            part_sum = u[full(f, b), :] + 0.5 * s[b]
            if f == 0:
                part_sum = part_sum + cross[at(0, b), :] * pf[at(1, b), :]
            else:
                part_sum = part_sum + cross[at(0, b), :] * pf[at(0, b), :]
            den = den + pf[at(f, b), :] * (part_sum + u[full(f, b), :])
    dots[0, 0:1, :] = jnp.sum(num, axis=0, keepdims=True)
    dots[0, 1:2, :] = jnp.sum(den, axis=0, keepdims=True)

    hops = sorted(
        ((dy, dx) for dy in range(ys) for dx in range(xs) if dy or dx),
        key=lambda d: -min(d[0], ys - d[0]) - min(d[1], xs - d[1]),
    )
    others = 2 * len(hops) + 1

    def send(src, dst, k, to):
        copy = pltpu.make_async_remote_copy(
            src_ref=src,
            dst_ref=dst,
            send_sem=s_send.at[k],
            recv_sem=s_recv.at[k],
            device_id=(to,),
            device_id_type=MESH,
        )
        copy.start()

    def arrived(ref, sem):
        pltpu.make_async_copy(ref, ref, sem).wait()

    def added(ref, first, total):
        part = [first, None, None, None]
        for j in range(total):
            part[j % 4] = plus(part[j % 4], ref[j])
        return functools.reduce(plus, [t for t in part if t is not None])

    heard(hello.at[2], y_far)
    for j, (dy, dx) in enumerate(hops):
        send(dots.at[0], got_a.at[2 * j + core], 0, moved(dy=dy, dx=dx) + 1 - core)

    @pl.when(core == 0)
    def _():
        send(dots.at[0], got_a.at[others - 1], 0, me + 1)

    scope("u_ends")
    sent_i = [tell(f, u, pf, i_mine, i_theirs, 4) for f in faces]
    add_ends_inside(pf, first, g0, u)
    scope("plane")

    @pl.when(core == 1)
    def _():
        arrived(got_a.at[pl.ds(0, others)], s_recv.at[0])
        dots[1] = added(got_a, dots[0], others)
        heard(hello.at[4], z_far)
        for k in sorted(range(1, zs), key=lambda k: -min(k, zs - k)):
            for c in (0, 1):
                send(dots.at[1], got_b.at[k - 1], 1, moved(dz=k) - c)
        send(dots.at[1], got_b.at[zs - 1], 1, me - 1)
        got_b[zs - 1] = dots[1]

    scope("out_p_r")
    for src, ends, dst in ((z, pf, p_o), (r, rf, r_o)):
        reorder(src, dst, order, INSIDE)
        for f in faces:
            for b in range(N):
                dst[full(f, b), :] = lane_pick(ends[at(f, b), :], order)
    sum_yz([(u, a) for a in INSIDE], lanes)
    reorder(u, im_o, order, INSIDE)
    scope("x3")
    for copy in sent_i:
        copy.wait()
    for f in faces:
        for b in range(N):
            rows = at(f, b)
            yf[rows, :] = yf[rows, :] + (i_mine[rows, :] + i_theirs[rows, :])
    sum_yz([(yf, f) for f in faces], lanes)
    for f in faces:
        for b in range(N):
            im_o[full(f, b), :] = lane_pick(yf[at(f, b), :], order)
    scope("lines")

    @pl.when(core == 0)
    def _():
        heard(hello.at[4], z_far)
        arrived(got_b, s_recv.at[1])

    @pl.when(core == 1)
    def _():
        arrived(got_b.at[pl.ds(0, zs - 1)], s_recv.at[1])

    total = added(got_b, None, zs)
    scope("alpha")
    sums = jnp.sum(total, axis=1, keepdims=True)
    al_o[...] = jnp.broadcast_to(sums[0:1, :] / sums[1:2, :], (8, LANES))
    @pl.when(core == 0)
    def _():
        arrived(got_a.at[pl.ds(0, len(hops) + 1)], s_send.at[0])

    @pl.when(core == 1)
    def _():
        arrived(got_a.at[pl.ds(0, len(hops))], s_send.at[0])
        arrived(got_a.at[pl.ds(0, 2 * zs - 1)], s_send.at[1])

    scope(None)


CHUNKS = 4


def finish_kernel(p, r, im, al, x_h, r_h, x_v, r_v, sems):
    alpha = al[...]
    size = ROWS // CHUNKS
    copies = []
    for k in range(CHUNKS):
        for i in range(k * size, (k + 1) * size, N):
            x_v[tile(i), :] = alpha * p[tile(i), :]
        rows = pl.ds(k * size, size)
        copies.append(pltpu.make_async_copy(x_v.at[rows], x_h.at[rows], sems.at[0, k]))
        copies[-1].start()
        for i in range(k * size, (k + 1) * size, N):
            r_v[tile(i), :] = r[tile(i), :] - alpha * im[tile(i), :]
        copies.append(pltpu.make_async_copy(r_v.at[rows], r_h.at[rows], sems.at[1, k]))
        copies[-1].start()
    for copy in copies:
        copy.wait()


def on_device(load_terms, geometry, mass_terms, element_order):
    flat = jax.ShapeDtypeStruct((ROWS, LANES), jnp.float32)
    vm = lambda *shape: pltpu.VMEM(shape, jnp.float32)
    field = vm(ROWS, LANES)
    pair = vm(2 * FACE, LANES)
    ys, zs, xs, cores = TORUS
    in_vmem = pl.BlockSpec(memory_space=pltpu.VMEM)
    in_hbm = pl.BlockSpec(memory_space=pltpu.HBM)
    parts = pl.pallas_call(
        step_kernel,
        out_shape=(field, field, field, vm(8, LANES)),
        in_specs=[in_hbm] * 4,
        out_specs=[in_vmem] * 4,
        scratch_shapes=[
            *[field] * 12,
            *[vm(8 * FACE, LANES)] * 2,
            *[pair] * 11, vm(FACE, LANES),
            vm(2, 2, LANES), vm(2 * ys * xs - 1, 2, LANES), vm(zs, 2, LANES),
            pltpu.VMEM((1, LANES), jnp.int32),
            pltpu.SemaphoreType.DMA((6,)),
            pltpu.SemaphoreType.DMA((5, 2)),
            pltpu.SemaphoreType.DMA((5, 2)),
            pltpu.SemaphoreType.DMA((2,)),
            pltpu.SemaphoreType.DMA((2,)),
            pltpu.SemaphoreType.REGULAR((5,)),
        ],
        compiler_params=pltpu.CompilerParams(
            collective_id=0, has_side_effects=True, vmem_limit_bytes=24 << 20
        ),
        name="cg_step",
    )(
        *[
            pltpu.with_memory_space_constraint(t, pltpu.HBM)
            for t in (
                load_terms.reshape(ROWS, LANES),
                geometry.reshape(3, ROWS, LANES),
                mass_terms.reshape(ROWS, LANES),
                element_order,
            )
        ]
    )
    x, res = pl.pallas_call(
        finish_kernel,
        out_shape=(flat, flat),
        in_specs=[in_vmem] * 4,
        out_specs=[in_hbm] * 2,
        scratch_shapes=[field, field, pltpu.SemaphoreType.DMA((2, CHUNKS))],
        compiler_params=pltpu.CompilerParams(vmem_limit_bytes=8 << 20),
        name="cg_finish",
    )(*[pltpu.with_memory_space_constraint(t, pltpu.VMEM) for t in parts])
    shape = load_terms.shape
    return x.reshape(shape), res.reshape(shape)


def solution(mesh):
    last = P(None, None, None, "slab")
    return jax.shard_map(
        on_device,
        mesh=mesh,
        in_specs=(last, P(None, None, None, None, "slab"), last, P("slab", None)),
        out_specs=(last, last),
        check_vma=False,
    )
```

time: 44.3 us -> 37.1 us (0.84)
  Pallas kernels: 43.5 us -> 36.3 us
    pallas_call x1, Pallas kernels: 41.5 us -> 35.4 us  [on_device(): pl.pallas_call(step_kernel, out_shape=(field, field, field, vm(8, LANES))...]
    pallas_call x1, Pallas kernels: 1.97 us -> 0.86 us  [on_device(): pl.pallas_call(finish_kernel, out_shape=(flat, flat), in_specs=[in_vmem]...]
where the time goes in v3:
time: 37.1 us; the launch traced here: 36.9 us
  Pallas kernels  36.3 us (98%)
  between operations  0.64 us (2%)
    pallas_call x1, Pallas kernels, on_device(): pl.pallas_call(step_kernel, out_shape=(field, field, field, vm(8, LANES))...  35.4 us
    pallas_call x1, Pallas kernels, on_device(): pl.pallas_call(finish_kernel, out_shape=(flat, flat), in_specs=[in_vmem]...  0.86 us

profile of v3, /device:TPU:1, one launch (start us, length us, event | category | flops | bytes accessed | tf_op | source)
XLA Modules:
  0.0 36.9 jit_solution(11825059186644747562)
XLA Ops:
  0.6 35.4 %cg_step.1 = (f32[512,128]{1,0:T(8,128)S(1)}, f32[512,128]{1,0:T(8,128)S(1)}, f32[512,128]{1,0:T(8,128)S(1)}, f32[8,128]{1,0:T(8,128)S(1)}) custom-call(f32[512,128]{1,0:T(8,128)} %bitcast.6, f32[3,512,128]{2,1,0:T(8,128)} %bitcast.5, f32[512,128]{1,0:T(8,128)} %bitcast.7, s32[1,128]{1,0:T(1,128)} %order_h.1), custom_call_target="tpu_custom_call" | custom-call | tf_op jit(solution)/shard_map/cg_step/pallas_call | solution.py:627
  36.1 0.9 %cg_finish.1 = (f32[512,128]{1,0:T(8,128)}, f32[512,128]{1,0:T(8,128)}) custom-call(f32[512,128]{1,0:T(8,128)S(1)} %get-tuple-element.8.p, f32[512,128]{1,0:T(8,128)S(1)} %get-tuple-element.9.r, f32[512,128]{1,0:T(8,128)S(1)} %get-tuple-element.10.im, f32[8,128]{1,0:T(8,128)S(1)} %get-tuple-element.11.al), custom_call_target="tpu_custom_call" | custom-call | tf_op jit(solution)/shard_map/cg_finish/pallas_call | solution.py:660

commit v4 on v3

--- a/solution.py
+++ b/solution.py
@@ -218,8 +218,8 @@
 def step_kernel(
     load_h, geom_h, mass_h, order_h, p_o, r_o, im_o, al_o,
     ld, g0, g1, g2, g2t, ms, r, dg, z, y, u, tmp,
-    mine, theirs, w_mine, w_theirs, i_mine, i_theirs, rf, df, zf, pf, yf, a_sum, tmpf, cross,
-    dots, got_a, got_b, order_v, in_sems, x_send, x_recv, s_send, s_recv, hello,
+    mine, theirs, w_mine, w_theirs, i_mine, i_theirs, bag, rf, df, zf, pf, yf, a_sum, tmpf, cross,
+    dots, got_a, got_b, order_v, in_sems, x_send, x_recv, bag_send, bag_recv, s_send, s_recv, hello,
 ):
     stack = []
 
@@ -265,12 +265,34 @@
         if who:
             pl.semaphore_wait(sem, len(who))
 
+    early = (z_at == 0) & (x == 0) & (core == 0)
+    carrier = (z_at == 0) & (x == xs - 1) & (core == 1)
+    late = (z_at == zs - 1) & (x == xs - 1) & (core == 1)
+    plane_size = zs * xs * cores
+    carrier_of_early = lax.rem(y_at + ys - 1, ys) * plane_size + xs * cores - 1
+    carrier_of_late = y_at * plane_size + xs * cores - 1
+    early_of_carrier = lax.rem(y_at + 1, ys) * plane_size
+    late_of_carrier = y_at * plane_size + plane_size - 1
+
     row = [moved(dx=k) + c for k in range(xs) for c in (0, 1 - 2 * core) if k or not isinstance(c, int)]
     y_near = [moved(dy=k) for k in ring(ys, 3)]
-    z_near = [moved(dz=k) for k in ring(zs, 3)]
+    y_far = [moved(dy=k) for k in ring(ys, ys // 2 + 1, 3)]
     barrier = pltpu.get_barrier_semaphore()
-    near = [near_to, far_to] + row + y_near + z_near
-    greet(barrier, near)
+    greet(barrier, [jnp.where(late, carrier_of_late, far_to), near_to])
+    greet(barrier, row + y_near)
+
+    @pl.when(early | carrier)
+    def _():
+        greet(barrier, [jnp.where(early, carrier_of_early, early_of_carrier)])
+
+    for k in range(1, zs):
+
+        @pl.when(z_at + k < zs)
+        def _(k=k):
+            greet(barrier, [me + k * xs * cores + 1 - core])
+
+    expected = len(row) + len(y_near) + 2 + 2 * carrier.astype(jnp.int32) + cores * core * z_at
+
     loads = [
         pltpu.make_async_copy(src, dst, in_sems.at[k])
         for k, (src, dst) in enumerate(
@@ -312,7 +334,7 @@
             for b in range(N):
                 dst[at(a, b), :] = lane_pick(src[at(a, b), :], idx)
 
-    def swap(src, dst, f, first, rows, k):
+    def swap(src, dst, f, first, rows, k, carried=None):
         copy = pltpu.make_async_remote_copy(
             src_ref=src.at[pl.ds(first, rows)],
             dst_ref=dst.at[pl.ds(first, rows)],
@@ -321,23 +343,41 @@
             device_id=(sides[f],),
             device_id_type=MESH,
         )
-        copy.start()
+        if f == 0 or carried is None:
+            copy.start()
+            return copy
+
+        @pl.when(early)
+        def _():
+            pltpu.make_async_remote_copy(
+                src_ref=src.at[pl.ds(first, rows)],
+                dst_ref=bag.at[pl.ds(carried, rows)],
+                send_sem=x_send.at[k, f],
+                recv_sem=bag_recv.at[k],
+                device_id=(carrier_of_early,),
+                device_id_type=MESH,
+            ).start()
+
+        pl.when(jnp.logical_not(early))(copy.start)
         return copy
+
+    def carry(dst, carried, first, rows, k):
+        return pltpu.make_async_remote_copy(
+            src_ref=bag.at[pl.ds(carried, rows)],
+            dst_ref=dst.at[pl.ds(first, rows)],
+            send_sem=bag_send.at[k],
+            recv_sem=x_recv.at[k, 1],
+            device_id=(late_of_carrier,),
+            device_id_type=MESH,
+        )
 
     both = (0, LAST)
     faces = (0, 1)
-    started = []
     scope("load_ends")
     loads[1].wait()
     for a in both:
         for b in range(N):
             mine[part(face_of[a], LOAD, b), :] = lane_pick(ld[at(a, b), :], inverse)
-    scope("barrier")
-    pl.semaphore_wait(barrier, len(near))
-    scope("diag_ends")
-    sent_l = [swap(mine, theirs, f, f * 4 * FACE, FACE, 0) for f in faces]
-    greet(hello.at[0], y_near)
-    greet(hello.at[1], z_near)
     for copy in loads[2:]:
         copy.wait()
     for k, a in enumerate(both):
@@ -354,12 +394,33 @@
             mine[part(face_of[a], DIAG, b), :] = lane_pick(
                 s[b] + yf[at(k, b), :] + ms[at(a, b), :] + tmpf[at(k, b), :], inverse
             )
-    sent_d = [swap(mine, theirs, f, (f * 4 + DIAG) * FACE, FACE, 1) for f in faces]
     for a in both:
         for i in range(N):
             mine[part(face_of[a], G1, i), :] = lane_pick(g1[at(a, i), :], inverse)
             mine[part(face_of[a], G2, i), :] = lane_pick(g2[across(a, i), :], inverse)
-    sent_g = [swap(mine, theirs, f, (f * 4 + G1) * FACE, 2 * FACE, 2) for f in faces]
+    scope("barrier")
+    pl.semaphore_wait(barrier, expected)
+    scope("send1")
+    carried1 = ((0, 4 * FACE, 2 * FACE), (1, 4 * FACE + 2 * FACE, 2 * FACE))
+
+    @pl.when(carrier)
+    def _():
+        for k, first, rows in carried1:
+            got = bag.at[pl.ds(first - 4 * FACE, rows)]
+            pltpu.make_async_copy(got, got, bag_recv.at[k]).wait()
+            carry(theirs, first - 4 * FACE, first, rows, k).start()
+
+    sent_ld = [swap(mine, theirs, f, f * 4 * FACE, 2 * FACE, 0, 0) for f in (1, 0)][::-1]
+    sent_g = [swap(mine, theirs, f, (f * 4 + 2) * FACE, 2 * FACE, 1, 2 * FACE) for f in (1, 0)][::-1]
+    greet(hello.at[0], y_near)
+
+    @pl.when(core == 1)
+    def _():
+        for k in range(1, zs):
+
+            @pl.when(z_at >= k)
+            def _(k=k):
+                greet(hello.at[2], [me - k * xs * cores])
 
     scope("reorder")
     reorder(ld, ld, inverse, INSIDE)
@@ -406,35 +467,36 @@
             df[at(f, b), :] = inv
             zf[at(f, b), :] = inv * rf[at(f, b), :]
 
-    def tell(f, v, ends, src, dst, k):
+    def tell(f, v, ends, src, dst, k, carried=None):
         for b in range(N):
             src[at(f, b), :] = v[full(f, b), :] + cross[at(0, b), :] * ends[at(1 - f, b), :]
-        return swap(src, dst, f, f * FACE, FACE, k)
-
-    scope("hello2")
+        return swap(src, dst, f, f * FACE, FACE, k, carried)
+
+    scope("hello")
+
+    @pl.when(carrier)
+    def _():
+        got = bag.at[pl.ds(4 * FACE, FACE)]
+        pltpu.make_async_copy(got, got, bag_recv.at[2]).wait()
+        carry(w_theirs, 4 * FACE, FACE, FACE, 2).start()
+
     heard(hello.at[0], y_near)
-    y_far = [moved(dy=k) for k in ring(ys, ys // 2 + 1, 3)]
-    greet(hello.at[2], y_far)
-    heard(hello.at[1], z_near)
-    z_mid = [moved(dz=k) for k in ring(zs, 5, 3)]
-    greet(hello.at[3], z_mid)
+    greet(hello.at[1], y_far)
     scope("x_near")
-    sent_l[0].wait()
-    sent_d[0].wait()
+    sent_ld[0].wait()
     scope("z_near")
     face_z(0)
-    sent_w = [None, tell(1, y, zf, w_mine, w_theirs, 3)]
+    sent_w = [None, tell(1, y, zf, w_mine, w_theirs, 2, 4 * FACE)]
     sent_g[0].wait()
     face_sums(0, mine, theirs, a_sum, a_sum, tmpf)
     s = face_terms(zf, 0, mine, theirs, a_sum, tmpf)
     for b in range(N):
         yf[at(0, b), :] = s[b]
     scope("x_far")
-    sent_l[1].wait()
-    sent_d[1].wait()
+    sent_ld[1].wait()
     scope("z_far")
     face_z(1)
-    sent_w[0] = tell(0, y, zf, w_mine, w_theirs, 3)
+    sent_w[0] = tell(0, y, zf, w_mine, w_theirs, 2)
 
     scope("inner2")
     first = pl.multiple_of((1 - core) * FACE, FACE)
@@ -466,10 +528,6 @@
     s = face_terms(zf, 1, mine, theirs, a_sum, tmpf)
     for b in range(N):
         yf[at(1, b), :] = s[b]
-    scope("hello3")
-    heard(hello.at[3], z_mid)
-    z_far = [moved(dz=k) for k in ring(zs, zs // 2 + 1, 5)]
-    greet(hello.at[4], z_far)
     scope("w_far")
     sent_w[1].wait()
     scope("w_near")
@@ -525,7 +583,7 @@
             part[j % 4] = plus(part[j % 4], ref[j])
         return functools.reduce(plus, [t for t in part if t is not None])
 
-    heard(hello.at[2], y_far)
+    heard(hello.at[1], y_far)
     for j, (dy, dx) in enumerate(hops):
         send(dots.at[0], got_a.at[2 * j + core], 0, moved(dy=dy, dx=dx) + 1 - core)
 
@@ -534,7 +592,7 @@
         send(dots.at[0], got_a.at[others - 1], 0, me + 1)
 
     scope("u_ends")
-    sent_i = [tell(f, u, pf, i_mine, i_theirs, 4) for f in faces]
+    sent_i = [tell(f, u, pf, i_mine, i_theirs, 3) for f in faces]
     add_ends_inside(pf, first, g0, u)
     scope("plane")
 
@@ -542,7 +600,11 @@
     def _():
         arrived(got_a.at[pl.ds(0, others)], s_recv.at[0])
         dots[1] = added(got_a, dots[0], others)
-        heard(hello.at[4], z_far)
+
+        @pl.when(z_at < zs - 1)
+        def _():
+            pl.semaphore_wait(hello.at[2], zs - 1 - z_at)
+
         for k in sorted(range(1, zs), key=lambda k: -min(k, zs - k)):
             for c in (0, 1):
                 send(dots.at[1], got_b.at[k - 1], 1, moved(dz=k) - c)
@@ -572,7 +634,6 @@
 
     @pl.when(core == 0)
     def _():
-        heard(hello.at[4], z_far)
         arrived(got_b, s_recv.at[1])
 
     @pl.when(core == 1)
@@ -583,6 +644,12 @@
     scope("alpha")
     sums = jnp.sum(total, axis=1, keepdims=True)
     al_o[...] = jnp.broadcast_to(sums[0:1, :] / sums[1:2, :], (8, LANES))
+    @pl.when(carrier)
+    def _():
+        for k, first, rows in carried1:
+            carry(theirs, first - 4 * FACE, first, rows, k).wait_send()
+        carry(w_theirs, 4 * FACE, FACE, FACE, 2).wait_send()
+
     @pl.when(core == 0)
     def _():
         arrived(got_a.at[pl.ds(0, len(hops) + 1)], s_send.at[0])
@@ -632,15 +699,17 @@
         scratch_shapes=[
             *[field] * 12,
             *[vm(8 * FACE, LANES)] * 2,
-            *[pair] * 11, vm(FACE, LANES),
+            *[pair] * 4, vm(5 * FACE, LANES), *[pair] * 7, vm(FACE, LANES),
             vm(2, 2, LANES), vm(2 * ys * xs - 1, 2, LANES), vm(zs, 2, LANES),
             pltpu.VMEM((1, LANES), jnp.int32),
             pltpu.SemaphoreType.DMA((6,)),
-            pltpu.SemaphoreType.DMA((5, 2)),
-            pltpu.SemaphoreType.DMA((5, 2)),
+            pltpu.SemaphoreType.DMA((4, 2)),
+            pltpu.SemaphoreType.DMA((4, 2)),
+            pltpu.SemaphoreType.DMA((3,)),
+            pltpu.SemaphoreType.DMA((3,)),
             pltpu.SemaphoreType.DMA((2,)),
             pltpu.SemaphoreType.DMA((2,)),
-            pltpu.SemaphoreType.REGULAR((5,)),
+            pltpu.SemaphoreType.REGULAR((3,)),
         ],
         compiler_params=pltpu.CompilerParams(
             collective_id=0, has_side_effects=True, vmem_limit_bytes=24 << 20

time: 37.1 us -> 35.9 us (0.968)
  Pallas kernels: 36.3 us -> 35.1 us
    pallas_call x1, Pallas kernels: 35.4 us -> 34.3 us  [on_device(): pl.pallas_call(step_kernel, out_shape=(field, field, field, vm(8, LANES))...]
where the time goes in v4:
time: 35.9 us; the launch traced here: 35.8 us
  Pallas kernels  35.1 us (98%)
  between operations  0.64 us (2%)
    pallas_call x1, Pallas kernels, on_device(): pl.pallas_call(step_kernel, out_shape=(field, field, field, vm(8, LANES))...  34.3 us
    pallas_call x1, Pallas kernels, on_device(): pl.pallas_call(finish_kernel, out_shape=(flat, flat), in_specs=[in_vmem]...  0.86 us

profile of v4, /device:TPU:1, one launch (start us, length us, event | category | flops | bytes accessed | tf_op | source)
XLA Modules:
  0.0 35.8 jit_solution(9118110320822752043)
XLA Ops:
  0.6 34.3 %cg_step.1 = (f32[512,128]{1,0:T(8,128)S(1)}, f32[512,128]{1,0:T(8,128)S(1)}, f32[512,128]{1,0:T(8,128)S(1)}, f32[8,128]{1,0:T(8,128)S(1)}) custom-call(f32[512,128]{1,0:T(8,128)} %bitcast.6, f32[3,512,128]{2,1,0:T(8,128)} %bitcast.5, f32[512,128]{1,0:T(8,128)} %bitcast.7, s32[1,128]{1,0:T(1,128)} %order_h.1), custom_call_target="tpu_custom_call" | custom-call | tf_op jit(solution)/shard_map/cg_step/pallas_call | solution.py:694
  34.9 0.9 %cg_finish.1 = (f32[512,128]{1,0:T(8,128)}, f32[512,128]{1,0:T(8,128)}) custom-call(f32[512,128]{1,0:T(8,128)S(1)} %get-tuple-element.8.p, f32[512,128]{1,0:T(8,128)S(1)} %get-tuple-element.9.r, f32[512,128]{1,0:T(8,128)S(1)} %get-tuple-element.10.im, f32[8,128]{1,0:T(8,128)S(1)} %get-tuple-element.11.al), custom_call_target="tpu_custom_call" | custom-call | tf_op jit(solution)/shard_map/cg_finish/pallas_call | solution.py:729

commit v5 on v4

--- a/solution.py
+++ b/solution.py
@@ -20,6 +20,8 @@
 MESH = pl.DeviceIdType.MESH
 TORUS = (8, 12, 4, 2)
 INSIDE = range(1, LAST)
+UNROLL_A = 4
+UNROLL_BC = 3
 
 
 def legendre_table(positions, points):
@@ -104,32 +106,63 @@
     lax.fori_loop(start, stop, lambda i, _: (body(i), 0)[1], 0)
 
 
-def inner_stiffness(v, g0, g1, g2t, ms, out, tmp):
-    def along_c(a):
-        s = contract(DERIV, [v[across(a, c), :] for c in range(N)], -1)
-        s = contract(DERIV.T, [s[c] * g2t[at(a, c), :] for c in range(N)], -1)
+def stiffness_a(v, g0, out, rows=range(N), more=None):
+    def along_a(b, _):
+        va = [v[at(a, b), :] if a in INSIDE else None for a in range(N)]
+        s = contract(DERIV, va, -1)
+        s = contract(DERIV.T, [s[a] * g0[at(a, b), :] for a in range(N)], -1, rows)
+        for a in rows:
+            out[at(a, b), :] = s[a] if more is None else s[a] + more[at(a, b), :]
+        return 0
+
+    lax.fori_loop(0, N, along_a, 0, unroll=UNROLL_A)
+
+
+def energy_a(v, g0, ends, first, total):
+    def along_a(b, total):
+        t = contract(DERIV, [v[at(a, b), :] if a in INSIDE else None for a in range(N)], -1)
+        s = [t[a] * g0[at(a, b), :] for a in range(N)]
+        total = [total[k] + s[k] * t[k] + s[k + 4] * t[k + 4] for k in range(4)]
+        s = contract(DERIV.T, s, -1, (0, LAST))
+        ends[tile(first + b * N), :] = s[0]
+        ends[tile(FACE - first + b * N), :] = s[LAST]
+        return total
+
+    return lax.fori_loop(0, N, along_a, total, unroll=UNROLL_A)
+
+
+def energy_bc(v, g1, g2t, ms, total):
+    def along_bc(a, total):
+        vb = [v[at(a, b), :] for b in range(N)]
+        for own, g in (([v[across(a, c), :] for c in range(N)], g2t), (vb, g1)):
+            t = contract(DERIV, own, -1)
+            e = [t[i] * g[at(a, i), :] * t[i] for i in range(N)]
+            total = [total[k] + (e[k] + e[k + 4]) for k in range(4)]
+        e = [vb[b] * ms[at(a, b), :] * vb[b] for b in range(N)]
+        return [total[k] + (e[k] + e[k + 4]) for k in range(4)]
+
+    return lax.fori_loop(1, LAST, along_bc, total, unroll=UNROLL_BC)
+
+
+def stiffness_bc(v, g1, g2t, ms, out, tmp, more=None):
+    def along_bc(a, _):
+        vt = [v[across(a, c), :] for c in range(N)]
+        vb = [v[at(a, b), :] for b in range(N)]
+        t = contract(DERIV, vt, -1)
+        t = contract(DERIV.T, [t[c] * g2t[at(a, c), :] for c in range(N)], -1)
         for c in range(N):
-            tmp[across(a, c), :] = s[c]
-
-    loop(1, LAST, along_c)
-
-    def along_b(a):
-        vb = [v[at(a, b), :] for b in range(N)]
+            tmp[across(a, c), :] = t[c]
         s = contract(DERIV, vb, -1)
         s = contract(DERIV.T, [s[b] * g1[at(a, b), :] for b in range(N)], -1)
         for b in range(N):
-            out[at(a, b), :] = s[b] + ms[at(a, b), :] * vb[b] + tmp[at(a, b), :]
-
-    loop(1, LAST, along_b)
-
-    def along_a(b):
-        va = [v[at(a, b), :] if a in INSIDE else None for a in range(N)]
-        s = contract(DERIV, va, -1)
-        s = contract(DERIV.T, [s[a] * g0[at(a, b), :] for a in range(N)], -1)
-        for a in range(N):
-            out[at(a, b), :] = out[at(a, b), :] + s[a] if a in INSIDE else s[a]
-
-    loop(0, N, along_a)
+            s[b] = s[b] + ms[at(a, b), :] * vb[b]
+            if more is not None:
+                s[b] = s[b] + more[at(a, b), :]
+        for b in range(N):
+            out[at(a, b), :] = s[b] + tmp[at(a, b), :]
+        return 0
+
+    lax.fori_loop(1, LAST, along_bc, 0, unroll=UNROLL_BC)
 
 
 def inner_diagonal(g0, g1, g2t, ms, out, tmp, cross):
@@ -169,6 +202,21 @@
     s = contract(DERIV, vb, -1)
     s = contract(DERIV.T, [s[b] * theirs[part(f, G1, b), :] for b in range(N)], -1)
     return [s[b] + a_sum[at(f, b), :] * vb[b] + tmp[at(f, b), :] for b in range(N)]
+
+
+def face_energy(v, f, theirs, a_sum):
+    vb = [v[at(f, b), :] for b in range(N)]
+    e = [a_sum[at(f, b), :] * vb[b] * vb[b] for b in range(N)]
+    for own, kind in (([v[across(f, c), :] for c in range(N)], G2), (vb, G1)):
+        t = contract(DERIV, own, -1)
+        e = [e[i] + t[i] * theirs[part(f, kind, i), :] * t[i] for i in range(N)]
+    return added_up(e)
+
+
+def added_up(terms):
+    while len(terms) > 1:
+        terms = [functools.reduce(plus, terms[i : i + 2]) for i in range(0, len(terms), 2)]
+    return terms[0]
 
 
 def face_sums(f, mine, theirs, diag, a_sum, tmp):
@@ -184,17 +232,23 @@
         a_sum[at(f, b), :] = diag[at(f, b), :] - s[b] - tmp[at(f, b), :]
 
 
-def add_ends_inside(v, first, g0, out):
-    def one(b):
-        ends = [None] * N
-        ends[0] = v[tile(first + b * N), :]
-        ends[LAST] = v[tile(FACE - first + b * N), :]
-        s = contract(DERIV, ends, -1)
-        s = contract(DERIV.T, [s[a] * g0[at(a, b), :] for a in range(N)], -1, INSIDE)
-        for a in INSIDE:
-            out[at(a, b), :] = out[at(a, b), :] + s[a]
-
-    loop(0, N, one)
+def couplings(g0, first, out):
+    def one(b, _):
+        g = [g0[at(a, b), :] for a in range(N)]
+        for a_end, row in ((0, first), (LAST, FACE - first)):
+            s = contract(DERIV.T, [float(DERIV[m, a_end]) * g[m] for m in range(N)], -1, INSIDE)
+            for a in INSIDE:
+                out[tile(row * 6 + ((a - 1) * N + b) * N), :] = s[a]
+        return 0
+
+    lax.fori_loop(0, N, one, 0, unroll=2)
+
+
+def couple(v, f, coupling, out, a):
+    for b in range(N):
+        out[at(a, b), :] = (
+            out[at(a, b), :] + coupling[tile(((f * 6 + a - 1) * N + b) * N), :] * v[at(f, b), :]
+        )
 
 
 def lane_pick(x, idx):
@@ -202,23 +256,31 @@
 
 
 def sum_yz(planes, lanes):
-    for v, a in planes:
-        low, high = v[at(a, 0), :], v[at(a, LAST), :]
-        v[at(a, LAST), :] = high + jnp.where(lanes["up"], pltpu.roll(low, LANES - EL_Z, 1), 0.0)
-        v[at(a, 0), :] = low + jnp.where(lanes["down"], pltpu.roll(high, EL_Z, 1), 0.0)
-    lows = [v[across(a, 0), :] for v, a in planes]
-    highs = [v[across(a, LAST), :] for v, a in planes]
-    nexts = [lane_pick(low, lanes["next"]) for low in lows]
-    prevs = [lane_pick(high, lanes["prev"]) for high in highs]
+    ends = [(v[at(a, 0), :], v[at(a, LAST), :]) for v, a in planes]
+    rims = [(v[across(a, 0), :], v[across(a, LAST), :]) for v, a in planes]
+    ups = [jnp.where(lanes["up"], pltpu.roll(low, LANES - EL_Z, 1), 0.0) for low, _ in ends]
+    downs = [jnp.where(lanes["down"], pltpu.roll(high, EL_Z, 1), 0.0) for _, high in ends]
+    nexts = [lane_pick(low, lanes["next"]) for low, _ in rims]
+    prevs = [lane_pick(high, lanes["prev"]) for _, high in rims]
+
+    def corners(rim, idx):
+        turned = jnp.where(lanes["first"], pltpu.roll(rim, 1, 0), pltpu.roll(rim, LAST, 0))
+        return jnp.where(lanes["corner"], lane_pick(turned, idx), 0.0)
+
+    far_nexts = [corners(low, lanes["corner_next"]) for low, _ in rims]
+    far_prevs = [corners(high, lanes["corner_prev"]) for _, high in rims]
     for k, (v, a) in enumerate(planes):
-        v[across(a, LAST), :] = highs[k] + nexts[k]
-        v[across(a, 0), :] = lows[k] + prevs[k]
+        v[across(a, LAST), :] = rims[k][1] + (nexts[k] + far_nexts[k])
+        v[across(a, 0), :] = rims[k][0] + (prevs[k] + far_prevs[k])
+        v[at(a, LAST), :] = v[at(a, LAST), :] + ups[k]
+        v[at(a, 0), :] = v[at(a, 0), :] + downs[k]
 
 
 def step_kernel(
     load_h, geom_h, mass_h, order_h, p_o, r_o, im_o, al_o,
     ld, g0, g1, g2, g2t, ms, r, dg, z, y, u, tmp,
-    mine, theirs, w_mine, w_theirs, i_mine, i_theirs, bag, rf, df, zf, pf, yf, a_sum, tmpf, cross,
+    mine, theirs, w_mine, w_theirs, i_mine, i_theirs, bag, rf, df, zf, pf, yf, a_sum, tmpf,
+    u_ends, cross, q_mine, q_theirs, coupling, acc,
     dots, got_a, got_b, order_v, in_sems, x_send, x_recv, bag_send, bag_recv, s_send, s_recv, hello,
 ):
     stack = []
@@ -284,12 +346,6 @@
     @pl.when(early | carrier)
     def _():
         greet(barrier, [jnp.where(early, carrier_of_early, early_of_carrier)])
-
-    for k in range(1, zs):
-
-        @pl.when(z_at + k < zs)
-        def _(k=k):
-            greet(barrier, [me + k * xs * cores + 1 - core])
 
     expected = len(row) + len(y_near) + 2 + 2 * carrier.astype(jnp.int32) + cores * core * z_at
 
@@ -308,6 +364,12 @@
     ]
     for copy in loads:
         copy.start()
+
+    for k in range(1, zs):
+
+        @pl.when(z_at + k < zs)
+        def _(k=k):
+            greet(barrier, [me + k * xs * cores + 1 - core])
 
     scope("idx")
     loads[0].wait()
@@ -328,6 +390,12 @@
         "next": lane - in_row + ((in_row + 1) & (EL_Z - 1)),
         "prev": lane - in_row + ((in_row + EL_Z - 1) & (EL_Z - 1)),
     }
+    b_at = lax.broadcasted_iota(jnp.int32, (8, LANES), 0)
+    lanes["first"] = b_at == 0
+    lanes["corner"] = (lanes["first"] & lanes["down"]) | ((b_at == LAST) & lanes["up"])
+    by_y = jnp.where(lanes["first"], LANES - EL_Z, EL_Z)
+    lanes["corner_next"] = (lanes["next"] + by_y) & (LANES - 1)
+    lanes["corner_prev"] = (lanes["prev"] + by_y) & (LANES - 1)
 
     def reorder(src, dst, idx, planes=range(N)):
         for a in planes:
@@ -423,24 +491,21 @@
                 greet(hello.at[2], [me - k * xs * cores])
 
     scope("reorder")
-    reorder(ld, ld, inverse, INSIDE)
     reorder(g0, g0, inverse)
     reorder(g1, g1, inverse, INSIDE)
     for a in INSIDE:
         for c in range(N):
             g2t[at(a, c), :] = lane_pick(g2[across(a, c), :], inverse)
     reorder(ms, ms, inverse, INSIDE)
+    for a in INSIDE:
+        for b in range(N):
+            moved_load = lane_pick(ld[at(a, b), :], inverse)
+            ld[at(a, b), :] = moved_load
+            r[at(a, b), :] = moved_load
     scope("diag")
     inner_diagonal(g0, g1, g2t, ms, dg, tmp, cross)
     scope("sums")
-    sum_yz([(dg, a) for a in INSIDE], lanes)
-
-    def copy_plane(a):
-        for b in range(N):
-            r[at(a, b), :] = ld[at(a, b), :]
-
-    loop(1, LAST, copy_plane)
-    sum_yz([(r, a) for a in INSIDE], lanes)
+    sum_yz([(v, a) for a in INSIDE for v in (dg, r)], lanes)
 
     def inner_z(a):
         for b in range(N):
@@ -449,8 +514,8 @@
             z[at(a, b), :] = inv * r[at(a, b), :]
 
     loop(1, LAST, inner_z)
-    scope("L1")
-    inner_stiffness(z, g0, g1, g2t, ms, y, tmp)
+    scope("La1")
+    stiffness_a(z, g0, y)
 
     def full(f, b):
         return tile(row_of[f] + b * N)
@@ -467,26 +532,32 @@
             df[at(f, b), :] = inv
             zf[at(f, b), :] = inv * rf[at(f, b), :]
 
-    def tell(f, v, ends, src, dst, k, carried=None):
-        for b in range(N):
-            src[at(f, b), :] = v[full(f, b), :] + cross[at(0, b), :] * ends[at(1 - f, b), :]
-        return swap(src, dst, f, f * FACE, FACE, k, carried)
-
-    scope("hello")
-
-    @pl.when(carrier)
-    def _():
-        got = bag.at[pl.ds(4 * FACE, FACE)]
-        pltpu.make_async_copy(got, got, bag_recv.at[2]).wait()
-        carry(w_theirs, 4 * FACE, FACE, FACE, 2).start()
-
-    heard(hello.at[0], y_near)
-    greet(hello.at[1], y_far)
+    def tell(f, k, carried=None):
+        for b in range(N):
+            w_mine[at(f, b), :] = y[full(f, b), :] + cross[at(0, b), :] * zf[at(1 - f, b), :]
+        return swap(w_mine, w_theirs, f, f * FACE, FACE, k, carried)
+
     scope("x_near")
     sent_ld[0].wait()
     scope("z_near")
     face_z(0)
-    sent_w = [None, tell(1, y, zf, w_mine, w_theirs, 2, 4 * FACE)]
+    sent_w = [None, tell(1, 2, 4 * FACE)]
+    scope("Lbc1")
+    stiffness_bc(z, g1, g2t, ms, y, tmp, y)
+    scope("hello")
+
+    @pl.when(carrier)
+    def _():
+        got = bag.at[pl.ds(4 * FACE, FACE)]
+        pltpu.make_async_copy(got, got, bag_recv.at[2]).wait()
+        carry(w_theirs, 4 * FACE, FACE, FACE, 2).start()
+
+    heard(hello.at[0], y_near)
+    greet(hello.at[1], y_far)
+    scope("g_near")
+    first = pl.multiple_of((1 - core) * FACE, FACE)
+    couplings(g0, first, coupling)
+    loop(1, LAST, lambda a: couple(zf, 0, coupling, y, a))
     sent_g[0].wait()
     face_sums(0, mine, theirs, a_sum, a_sum, tmpf)
     s = face_terms(zf, 0, mine, theirs, a_sum, tmpf)
@@ -496,66 +567,88 @@
     sent_ld[1].wait()
     scope("z_far")
     face_z(1)
-    sent_w[0] = tell(0, y, zf, w_mine, w_theirs, 2)
+    sent_w[0] = tell(0, 2)
 
     scope("inner2")
-    first = pl.multiple_of((1 - core) * FACE, FACE)
-    add_ends_inside(zf, first, g0, y)
+    for a in INSIDE:
+        couple(zf, 1, coupling, y, a)
     sum_yz([(y, a) for a in INSIDE], lanes)
+    zero = jnp.zeros((8, LANES), jnp.float32)
 
     def inner_p(a, num):
         for b in range(N):
             rows = at(a, b)
             p = COEF_Z * z[rows, :] - COEF_Q * (dg[rows, :] * y[rows, :])
             z[rows, :] = p
-            num = num + ld[rows, :] * p
+            num[b % 4] = num[b % 4] + ld[rows, :] * p
         return num
 
-    zero = jnp.zeros((8, LANES), jnp.float32)
-    num = lax.fori_loop(1, LAST, inner_p, zero)
+    num = lax.fori_loop(1, LAST, inner_p, [zero] * 4, unroll=True)
     scope("L2")
-    inner_stiffness(z, g0, g1, g2t, ms, u, tmp)
-
-    def inner_den(a, den):
-        for b in range(N):
-            den = den + z[at(a, b), :] * u[at(a, b), :]
-        return den
-
-    den = lax.fori_loop(1, LAST, inner_den, zero)
+    den = energy_bc(z, g1, g2t, ms, [zero] * 4)
+    den = energy_a(z, g0, u_ends, first, den)
+    num, den = added_up(num), added_up(den)
     scope("g_far")
     sent_g[1].wait()
     face_sums(1, mine, theirs, a_sum, a_sum, tmpf)
     s = face_terms(zf, 1, mine, theirs, a_sum, tmpf)
     for b in range(N):
         yf[at(1, b), :] = s[b]
+
+    def face_p(f):
+        for b in range(N):
+            rows = at(f, b)
+            yf[rows, :] = yf[rows, :] + (w_mine[rows, :] + w_theirs[rows, :])
+        sum_yz([(yf, f)], lanes)
+        for b in range(N):
+            rows = at(f, b)
+            pf[rows, :] = COEF_Z * zf[rows, :] - COEF_Q * (df[rows, :] * yf[rows, :])
+
+    def face_dot(kind, f):
+        return added_up([kind[part(f, LOAD, b), :] * pf[at(f, b), :] for b in range(N)])
+
     scope("w_far")
     sent_w[1].wait()
-    scope("w_near")
-    sent_w[0].wait()
     scope("ends2")
-    for f in faces:
-        for b in range(N):
-            rows = at(f, b)
-            yf[rows, :] = yf[rows, :] + (w_mine[rows, :] + w_theirs[rows, :])
-    sum_yz([(yf, f) for f in faces], lanes)
-    for f in faces:
-        for b in range(N):
-            rows = at(f, b)
-            p = COEF_Z * zf[rows, :] - COEF_Q * (df[rows, :] * yf[rows, :])
-            pf[rows, :] = p
-            num = num + mine[part(f, LOAD, b), :] * p
-    for f in faces:
-        s = face_terms(pf, f, mine, theirs, a_sum, tmpf)
-        for b in range(N):
-            yf[at(f, b), :] = s[b]
-            part_sum = u[full(f, b), :] + 0.5 * s[b]
-            if f == 0:
-                part_sum = part_sum + cross[at(0, b), :] * pf[at(1, b), :]
-            else:
-                part_sum = part_sum + cross[at(0, b), :] * pf[at(0, b), :]
-            den = den + pf[at(f, b), :] * (part_sum + u[full(f, b), :])
-    dots[0, 0:1, :] = jnp.sum(num, axis=0, keepdims=True)
-    dots[0, 1:2, :] = jnp.sum(den, axis=0, keepdims=True)
+    face_p(1)
+    num = num + face_dot(mine, 1)
+    den = (
+        den
+        + 0.5 * face_energy(pf, 1, theirs, a_sum)
+        + added_up([2.0 * u_ends[at(1, b), :] * pf[at(1, b), :] for b in range(N)])
+    )
+    for b in range(N):
+        q_mine[at(0, b), :] = 2.0 * (u_ends[at(0, b), :] + cross[at(0, b), :] * pf[at(1, b), :])
+    acc[tile(0), :] = num
+    acc[tile(8), :] = den
+    takes = jnp.where(2 * x >= xs, core, 1 - core) == 1
+    gives = jnp.logical_not(takes)
+    sent_q = pltpu.make_async_remote_copy(
+        src_ref=q_mine,
+        dst_ref=q_theirs,
+        send_sem=x_send.at[4, 0],
+        recv_sem=x_recv.at[4, 0],
+        device_id=(near_to,),
+        device_id_type=MESH,
+    )
+    pl.when(gives)(sent_q.start)
+
+    @pl.when(takes)
+    def _():
+        sent_w[0].wait()
+        face_p(0)
+        sent_q.wait_recv()
+        acc[tile(0), :] = acc[tile(0), :] + (face_dot(mine, 0) + face_dot(theirs, 0))
+        acc[tile(8), :] = (
+            acc[tile(8), :]
+            + face_energy(pf, 0, theirs, a_sum)
+            + added_up(
+                [(q_mine[at(0, b), :] + q_theirs[at(0, b), :]) * pf[at(0, b), :] for b in range(N)]
+            )
+        )
+
+    dots[0, 0:1, :] = jnp.sum(acc[tile(0), :], axis=0, keepdims=True)
+    dots[0, 1:2, :] = jnp.sum(acc[tile(8), :], axis=0, keepdims=True)
 
     hops = sorted(
         ((dy, dx) for dy in range(ys) for dx in range(xs) if dy or dx),
@@ -592,25 +685,30 @@
         send(dots.at[0], got_a.at[others - 1], 0, me + 1)
 
     scope("u_ends")
-    sent_i = [tell(f, u, pf, i_mine, i_theirs, 3) for f in faces]
-    add_ends_inside(pf, first, g0, u)
-    scope("plane")
-
-    @pl.when(core == 1)
-    def _():
-        arrived(got_a.at[pl.ds(0, others)], s_recv.at[0])
-        dots[1] = added(got_a, dots[0], others)
-
-        @pl.when(z_at < zs - 1)
-        def _():
-            pl.semaphore_wait(hello.at[2], zs - 1 - z_at)
-
-        for k in sorted(range(1, zs), key=lambda k: -min(k, zs - k)):
-            for c in (0, 1):
-                send(dots.at[1], got_b.at[k - 1], 1, moved(dz=k) - c)
-        send(dots.at[1], got_b.at[zs - 1], 1, me - 1)
-        got_b[zs - 1] = dots[1]
-
+
+    @pl.when(gives)
+    def _():
+        sent_w[0].wait()
+        face_p(0)
+        sent_q.wait_send()
+
+    sent_i = []
+    for f in faces:
+        for b in range(N):
+            i_mine[at(f, b), :] = u_ends[at(f, b), :] + cross[at(0, b), :] * pf[at(1 - f, b), :]
+        sent_i.append(swap(i_mine, i_theirs, f, f * FACE, FACE, 3))
+    for f in faces:
+        s = face_terms(pf, f, mine, theirs, a_sum, tmpf)
+        for b in range(N):
+            yf[at(f, b), :] = s[b]
+    stiffness_bc(z, g1, g2t, ms, y, tmp)
+    stiffness_a(z, g0, u, INSIDE, y)
+
+    def couple_both(a):
+        couple(pf, 0, coupling, u, a)
+        couple(pf, 1, coupling, u, a)
+
+    loop(1, LAST, couple_both)
     scope("out_p_r")
     for src, ends, dst in ((z, pf, p_o), (r, rf, r_o)):
         reorder(src, dst, order, INSIDE)
@@ -619,6 +717,23 @@
                 dst[full(f, b), :] = lane_pick(ends[at(f, b), :], order)
     sum_yz([(u, a) for a in INSIDE], lanes)
     reorder(u, im_o, order, INSIDE)
+    scope("plane")
+
+    @pl.when(core == 1)
+    def _():
+        arrived(got_a.at[pl.ds(0, others)], s_recv.at[0])
+        dots[1] = added(got_a, dots[0], others)
+
+        @pl.when(z_at < zs - 1)
+        def _():
+            pl.semaphore_wait(hello.at[2], zs - 1 - z_at)
+
+        for k in sorted(range(1, zs), key=lambda k: -min(k, zs - k)):
+            for c in (0, 1):
+                send(dots.at[1], got_b.at[k - 1], 1, moved(dz=k) - c)
+        send(dots.at[1], got_b.at[zs - 1], 1, me - 1)
+        got_b[zs - 1] = dots[1]
+
     scope("x3")
     for copy in sent_i:
         copy.wait()
@@ -699,12 +814,13 @@
         scratch_shapes=[
             *[field] * 12,
             *[vm(8 * FACE, LANES)] * 2,
-            *[pair] * 4, vm(5 * FACE, LANES), *[pair] * 7, vm(FACE, LANES),
+            *[pair] * 4, vm(5 * FACE, LANES), *[pair] * 8, *[vm(FACE, LANES)] * 3,
+            vm(12 * FACE, LANES), vm(16, LANES),
             vm(2, 2, LANES), vm(2 * ys * xs - 1, 2, LANES), vm(zs, 2, LANES),
             pltpu.VMEM((1, LANES), jnp.int32),
             pltpu.SemaphoreType.DMA((6,)),
-            pltpu.SemaphoreType.DMA((4, 2)),
-            pltpu.SemaphoreType.DMA((4, 2)),
+            pltpu.SemaphoreType.DMA((5, 2)),
+            pltpu.SemaphoreType.DMA((5, 2)),
             pltpu.SemaphoreType.DMA((3,)),
             pltpu.SemaphoreType.DMA((3,)),
             pltpu.SemaphoreType.DMA((2,)),

time: 35.9 us -> 35.4 us (0.986)
  Pallas kernels: 35.1 us -> 34.6 us
    pallas_call x1, Pallas kernels: 34.3 us -> 33.8 us  [on_device(): pl.pallas_call(step_kernel, out_shape=(field, field, field, vm(8, LANES))...]
where the time goes in v5:
time: 35.4 us; the launch traced here: 35.3 us
  Pallas kernels  34.6 us (98%)
  between operations  0.64 us (2%)
    pallas_call x1, Pallas kernels, on_device(): pl.pallas_call(step_kernel, out_shape=(field, field, field, vm(8, LANES))...  33.8 us
    pallas_call x1, Pallas kernels, on_device(): pl.pallas_call(finish_kernel, out_shape=(flat, flat), in_specs=[in_vmem]...  0.86 us

profile of v5, /device:TPU:1, one launch (start us, length us, event | category | flops | bytes accessed | tf_op | source)
XLA Modules:
  0.0 35.3 jit_solution(17358358518393814004)
XLA Ops:
  0.6 33.8 %cg_step.1 = (f32[512,128]{1,0:T(8,128)S(1)}, f32[512,128]{1,0:T(8,128)S(1)}, f32[512,128]{1,0:T(8,128)S(1)}, f32[8,128]{1,0:T(8,128)S(1)}) custom-call(f32[512,128]{1,0:T(8,128)} %bitcast.6, f32[3,512,128]{2,1,0:T(8,128)} %bitcast.5, f32[512,128]{1,0:T(8,128)} %bitcast.7, s32[1,128]{1,0:T(1,128)} %order_h.1), custom_call_target="tpu_custom_call" | custom-call | tf_op jit(solution)/shard_map/cg_step/pallas_call | solution.py:809
  34.4 0.9 %cg_finish.1 = (f32[512,128]{1,0:T(8,128)}, f32[512,128]{1,0:T(8,128)}) custom-call(f32[512,128]{1,0:T(8,128)S(1)} %get-tuple-element.8.p, f32[512,128]{1,0:T(8,128)S(1)} %get-tuple-element.9.r, f32[512,128]{1,0:T(8,128)S(1)} %get-tuple-element.10.im, f32[8,128]{1,0:T(8,128)S(1)} %get-tuple-element.11.al), custom_call_target="tpu_custom_call" | custom-call | tf_op jit(solution)/shard_map/cg_finish/pallas_call | solution.py:845

commit v6 on v5

--- a/solution.py
+++ b/solution.py
@@ -96,6 +96,7 @@
 
 
 LOAD, DIAG, G1, G2 = range(4)
+NEAR, FAR_LD, FAR_G, NEAR_W, FAR_W, IMAGE, NEAR_Q = range(7)
 
 
 def part(f, kind, i):
@@ -165,32 +166,27 @@
     lax.fori_loop(1, LAST, along_bc, 0, unroll=UNROLL_BC)
 
 
-def inner_diagonal(g0, g1, g2t, ms, out, tmp, cross):
-    def along_c(a):
-        s = contract(SQUARED.T, [g2t[at(a, c), :] for c in range(N)], 1)
+def inner_diagonal(g0, g1, g2, ms, out, tmp):
+    def along_a(b, _):
+        s = contract(SQUARED.T, [g0[at(a, b), :] for a in range(N)], 1, INSIDE)
+        for a in INSIDE:
+            out[at(a, b), :] = s[a] + ms[at(a, b), :]
+        return 0
+
+    lax.fori_loop(0, N, along_a, 0, unroll=UNROLL_A)
+
+    def along_bc(a, _):
+        t = contract(SQUARED.T, [g2[across(a, c), :] for c in range(N)], 1)
         for c in range(N):
-            tmp[across(a, c), :] = s[c]
-
-    loop(1, LAST, along_c)
-
-    def along_b(a):
+            tmp[across(a, c), :] = t[c]
         s = contract(SQUARED.T, [g1[at(a, b), :] for b in range(N)], 1)
         for b in range(N):
-            out[at(a, b), :] = s[b] + ms[at(a, b), :] + tmp[at(a, b), :]
-
-    loop(1, LAST, along_b)
-
-    def along_a(b):
-        g = [g0[at(a, b), :] for a in range(N)]
-        s = contract(SQUARED.T, g, 1, INSIDE)
-        for a in INSIDE:
-            out[at(a, b), :] = out[at(a, b), :] + s[a]
-        both = None
-        for m in range(N):
-            both = plus(both, float(DERIV[m, 0] * DERIV[m, LAST]) * g[m])
-        cross[at(0, b), :] = both
-
-    loop(0, N, along_a)
+            s[b] = s[b] + out[at(a, b), :]
+        for b in range(N):
+            out[at(a, b), :] = s[b] + tmp[at(a, b), :]
+        return 0
+
+    lax.fori_loop(1, LAST, along_bc, 0, unroll=UNROLL_BC)
 
 
 def face_terms(v, f, mine, theirs, a_sum, tmp):
@@ -278,10 +274,10 @@
 
 def step_kernel(
     load_h, geom_h, mass_h, order_h, p_o, r_o, im_o, al_o,
-    ld, g0, g1, g2, g2t, ms, r, dg, z, y, u, tmp,
+    ld, coef, g2t, r, dg, z, y, u, tmp,
     mine, theirs, w_mine, w_theirs, i_mine, i_theirs, bag, rf, df, zf, pf, yf, a_sum, tmpf,
     u_ends, cross, q_mine, q_theirs, coupling, acc,
-    dots, got_a, got_b, order_v, in_sems, x_send, x_recv, bag_send, bag_recv, s_send, s_recv, hello,
+    dots, got_a, got_b, sent_all, order_v, in_sems, x_send, x_recv, bag_recv, s_send, s_recv, hello,
 ):
     stack = []
 
@@ -294,30 +290,10 @@
 
     scope("enter")
     ys, zs, xs, cores = TORUS
-    count = lax.axis_size("slab")
+    line, plane_size, count = xs * cores, zs * xs * cores, ys * zs * xs * cores
     me = lax.axis_index("slab")
     core = lax.rem(me, cores)
-    x = lax.rem(me // cores, xs)
-    z_at = lax.rem(me // (cores * xs), zs)
-    y_at = me // (cores * xs * zs)
-    near_to = me + 1 - 2 * core
-    far_to = lax.rem(me + count + 2 * core - 1, count)
-    sides = (near_to, far_to)
-    row_of = (pl.multiple_of((1 - core) * (ROWS - FACE), FACE), pl.multiple_of(core * (ROWS - FACE), FACE))
-    face_of = {0: 1 - core, LAST: core}
-
-    def moved(dy=0, dz=0, dx=0):
-        to = me
-        if dy:
-            to = to + (lax.rem(y_at + dy, ys) - y_at) * (cores * xs * zs)
-        if dz:
-            to = to + (lax.rem(z_at + dz, zs) - z_at) * (cores * xs)
-        if dx:
-            to = to + (lax.rem(x + dx, xs) - x) * cores
-        return to
-
-    def ring(size, stop, start=1):
-        return sorted({j % size for k in range(start, stop) for j in (k, -k)} - {0})
+    in_plane = lax.rem(me, plane_size)
 
     def greet(sem, who):
         for q in who:
@@ -327,49 +303,64 @@
         if who:
             pl.semaphore_wait(sem, len(who))
 
-    early = (z_at == 0) & (x == 0) & (core == 0)
-    carrier = (z_at == 0) & (x == xs - 1) & (core == 1)
-    late = (z_at == zs - 1) & (x == xs - 1) & (core == 1)
-    plane_size = zs * xs * cores
-    carrier_of_early = lax.rem(y_at + ys - 1, ys) * plane_size + xs * cores - 1
-    carrier_of_late = y_at * plane_size + xs * cores - 1
-    early_of_carrier = lax.rem(y_at + 1, ys) * plane_size
-    late_of_carrier = y_at * plane_size + plane_size - 1
-
-    row = [moved(dx=k) + c for k in range(xs) for c in (0, 1 - 2 * core) if k or not isinstance(c, int)]
-    y_near = [moved(dy=k) for k in ring(ys, 3)]
-    y_far = [moved(dy=k) for k in ring(ys, ys // 2 + 1, 3)]
+    near_to = me + 1 - 2 * core
+    far_to = me + 2 * core - 1
+    far_to = jnp.where(far_to < 0, count - 1, jnp.where(far_to == count, 0, far_to))
+    early, carrier, late = in_plane == 0, in_plane == line - 1, in_plane == plane_size - 1
     barrier = pltpu.get_barrier_semaphore()
-    greet(barrier, [jnp.where(late, carrier_of_late, far_to), near_to])
-    greet(barrier, row + y_near)
-
-    @pl.when(early | carrier)
-    def _():
-        greet(barrier, [jnp.where(early, carrier_of_early, early_of_carrier)])
-
-    expected = len(row) + len(y_near) + 2 + 2 * carrier.astype(jnp.int32) + cores * core * z_at
-
+    greet(barrier, [jnp.where(late, me + line - plane_size, far_to)])
     loads = [
         pltpu.make_async_copy(src, dst, in_sems.at[k])
-        for k, (src, dst) in enumerate(
-            (
-                (order_h, order_v),
-                (load_h, ld),
-                (geom_h.at[0], g0),
-                (geom_h.at[1], g1),
-                (geom_h.at[2], g2),
-                (mass_h, ms),
-            )
+        for k, src, dst in (
+            (0, order_h, order_v),
+            (1, load_h, ld),
+            (2, geom_h, coef.at[pl.ds(0, 3 * ROWS)]),
+            (2, mass_h, coef.at[pl.ds(3 * ROWS, ROWS)]),
         )
     ]
     for copy in loads:
         copy.start()
-
-    for k in range(1, zs):
-
-        @pl.when(z_at + k < zs)
-        def _(k=k):
-            greet(barrier, [me + k * xs * cores + 1 - core])
+    g0, g1, g2, ms = (coef.at[pl.ds(k * ROWS, ROWS)] for k in range(4))
+
+    y_at = me // plane_size
+    z_at = in_plane // line
+    x = lax.rem(me, line) // cores
+
+    def moved(dy=0, dz=0, dx=0):
+        to = me
+        if dy:
+            to = to + (lax.rem(y_at + dy, ys) - y_at) * plane_size
+        if dz:
+            to = to + (lax.rem(z_at + dz, zs) - z_at) * line
+        if dx:
+            to = to + (lax.rem(x + dx, xs) - x) * cores
+        return to
+
+    def ring(size, stop, start=1):
+        return sorted({j % size for k in range(start, stop) for j in (k, -k)} - {0})
+
+    sides = (near_to, far_to)
+    row_of = (pl.multiple_of((1 - core) * (ROWS - FACE), FACE), pl.multiple_of(core * (ROWS - FACE), FACE))
+    face_of = {0: 1 - core, LAST: core}
+    carrier_of_early = lax.rem(y_at + ys - 1, ys) * plane_size + line - 1
+    early_of_carrier = lax.rem(y_at + 1, ys) * plane_size
+    late_of_carrier = me + plane_size - line
+
+    row = [moved(dx=k) + c for k in range(xs) for c in (0, 1 - 2 * core) if k or not isinstance(c, int)]
+    y_near = [moved(dy=k) for k in ring(ys, 3)]
+    y_far = [moved(dy=k) for k in ring(ys, ys // 2 + 1, 3)]
+    greet(barrier, [near_to] + row + y_near)
+
+    @pl.when(early | carrier)
+    def _():
+        greet(barrier, [jnp.where(early, carrier_of_early, early_of_carrier)])
+
+    def higher(z_to, _):
+        greet(barrier, [me + (z_to - z_at) * line + 1 - core])
+        return 0
+
+    lax.fori_loop(z_at + 1, zs, higher, 0)
+    expected = len(row) + len(y_near) + 2 + 2 * carrier.astype(jnp.int32) + 2 * core * z_at
 
     scope("idx")
     loads[0].wait()
@@ -402,42 +393,33 @@
             for b in range(N):
                 dst[at(a, b), :] = lane_pick(src[at(a, b), :], idx)
 
-    def swap(src, dst, f, first, rows, k, carried=None):
-        copy = pltpu.make_async_remote_copy(
-            src_ref=src.at[pl.ds(first, rows)],
-            dst_ref=dst.at[pl.ds(first, rows)],
-            send_sem=x_send.at[k, f],
-            recv_sem=x_recv.at[k, f],
-            device_id=(sides[f],),
+    def remote(src, dst, recv, to):
+        return pltpu.make_async_remote_copy(
+            src_ref=src,
+            dst_ref=dst,
+            send_sem=x_send,
+            recv_sem=recv,
+            device_id=(to,),
             device_id_type=MESH,
         )
-        if f == 0 or carried is None:
+
+    def swap(src, dst, f, first, rows, k, carried=None, bag_k=None):
+        src, dst = src.at[pl.ds(first, rows)], dst.at[pl.ds(first, rows)]
+        copy = remote(src, dst, x_recv.at[k], sides[f])
+        if carried is None:
             copy.start()
-            return copy
-
-        @pl.when(early)
-        def _():
-            pltpu.make_async_remote_copy(
-                src_ref=src.at[pl.ds(first, rows)],
-                dst_ref=bag.at[pl.ds(carried, rows)],
-                send_sem=x_send.at[k, f],
-                recv_sem=bag_recv.at[k],
-                device_id=(carrier_of_early,),
-                device_id_type=MESH,
-            ).start()
-
-        pl.when(jnp.logical_not(early))(copy.start)
+        else:
+            by_bag = remote(src, bag.at[pl.ds(carried, rows)], bag_recv.at[bag_k], carrier_of_early)
+            pl.when(early)(by_bag.start)
+            pl.when(jnp.logical_not(early))(copy.start)
         return copy
 
     def carry(dst, carried, first, rows, k):
-        return pltpu.make_async_remote_copy(
-            src_ref=bag.at[pl.ds(carried, rows)],
-            dst_ref=dst.at[pl.ds(first, rows)],
-            send_sem=bag_send.at[k],
-            recv_sem=x_recv.at[k, 1],
-            device_id=(late_of_carrier,),
-            device_id_type=MESH,
-        )
+        src, dst = bag.at[pl.ds(carried, rows)], dst.at[pl.ds(first, rows)]
+        remote(src, dst, x_recv.at[k], late_of_carrier).start()
+
+    def landed(ref, sem):
+        pltpu.make_async_copy(ref, ref, sem).wait()
 
     both = (0, LAST)
     faces = (0, 1)
@@ -446,8 +428,7 @@
     for a in both:
         for b in range(N):
             mine[part(face_of[a], LOAD, b), :] = lane_pick(ld[at(a, b), :], inverse)
-    for copy in loads[2:]:
-        copy.wait()
+    pltpu.make_async_copy(coef, coef, in_sems.at[2]).wait()
     for k, a in enumerate(both):
         s = contract(SQUARED.T, [g2[across(a, c), :] for c in range(N)], 1)
         for c in range(N):
@@ -469,88 +450,94 @@
     scope("barrier")
     pl.semaphore_wait(barrier, expected)
     scope("send1")
-    carried1 = ((0, 4 * FACE, 2 * FACE), (1, 4 * FACE + 2 * FACE, 2 * FACE))
 
     @pl.when(carrier)
     def _():
-        for k, first, rows in carried1:
-            got = bag.at[pl.ds(first - 4 * FACE, rows)]
-            pltpu.make_async_copy(got, got, bag_recv.at[k]).wait()
-            carry(theirs, first - 4 * FACE, first, rows, k).start()
-
-    sent_ld = [swap(mine, theirs, f, f * 4 * FACE, 2 * FACE, 0, 0) for f in (1, 0)][::-1]
-    sent_g = [swap(mine, theirs, f, (f * 4 + 2) * FACE, 2 * FACE, 1, 2 * FACE) for f in (1, 0)][::-1]
+        landed(bag.at[pl.ds(0, 4 * FACE)], bag_recv.at[0])
+        carry(theirs, 0, 4 * FACE, 2 * FACE, FAR_LD)
+        carry(theirs, 2 * FACE, 6 * FACE, 2 * FACE, FAR_G)
+
+    sent_ld = swap(mine, theirs, 1, 4 * FACE, 2 * FACE, FAR_LD, 0, 0)
+    sent_g = swap(mine, theirs, 1, 6 * FACE, 2 * FACE, FAR_G, 2 * FACE, 0)
+    sent_near = swap(mine, theirs, 0, 0, 4 * FACE, NEAR)
     greet(hello.at[0], y_near)
 
     @pl.when(core == 1)
     def _():
-        for k in range(1, zs):
-
-            @pl.when(z_at >= k)
-            def _(k=k):
-                greet(hello.at[2], [me - k * xs * cores])
-
+        def lower(z_to, _):
+            greet(hello.at[2], [me + (z_to - z_at) * line])
+            return 0
+
+        lax.fori_loop(0, z_at, lower, 0)
+
+    scope("diag")
+    inner_diagonal(g0, g1, g2, ms, dg, tmp)
     scope("reorder")
+    for a in INSIDE:
+        for b in range(N):
+            rows = at(a, b)
+            dg[rows, :] = lane_pick(dg[rows, :], inverse)
+            moved_load = lane_pick(ld[rows, :], inverse)
+            ld[rows, :] = moved_load
+            r[rows, :] = moved_load
     reorder(g0, g0, inverse)
+    scope("sums")
+    sum_yz([(v, a) for a in INSIDE for v in (dg, r)], lanes)
+
+    def inner_z(a, _):
+        for b in range(N):
+            inv = 1.0 / dg[at(a, b), :]
+            dg[at(a, b), :] = inv
+            z[at(a, b), :] = inv * r[at(a, b), :]
+        return 0
+
+    lax.fori_loop(1, LAST, inner_z, 0, unroll=3)
+    for b in range(N):
+        g = [float(DERIV[m, 0] * DERIV[m, LAST]) * g0[at(m, b), :] for m in range(N)]
+        cross[at(0, b), :] = added_up(g)
+    scope("La1")
+    stiffness_a(z, g0, y)
+
+    def full(f, b):
+        return tile(row_of[f] + b * N)
+
+    def face_z(f):
+        for b in range(N):
+            rf[at(f, b), :] = mine[part(f, LOAD, b), :] + theirs[part(f, LOAD, b), :]
+            total = mine[part(f, DIAG, b), :] + theirs[part(f, DIAG, b), :]
+            a_sum[at(f, b), :] = total
+            df[at(f, b), :] = total
+        sum_yz([(rf, f), (df, f)], lanes)
+        for b in range(N):
+            inv = 1.0 / df[at(f, b), :]
+            df[at(f, b), :] = inv
+            zf[at(f, b), :] = inv * rf[at(f, b), :]
+
+    def tell(f, k, carried=None):
+        for b in range(N):
+            w_mine[at(f, b), :] = y[full(f, b), :] + cross[at(0, b), :] * zf[at(1 - f, b), :]
+        sum_yz([(w_mine, f)], lanes)
+        return swap(w_mine, w_theirs, f, f * FACE, FACE, k, carried, 1)
+
+    scope("x_near")
+    sent_near.wait_recv()
+    scope("z_near")
+    face_z(0)
+    sent_w = [None, tell(1, FAR_W, 4 * FACE)]
+    scope("reorder2")
     reorder(g1, g1, inverse, INSIDE)
     for a in INSIDE:
         for c in range(N):
             g2t[at(a, c), :] = lane_pick(g2[across(a, c), :], inverse)
     reorder(ms, ms, inverse, INSIDE)
-    for a in INSIDE:
-        for b in range(N):
-            moved_load = lane_pick(ld[at(a, b), :], inverse)
-            ld[at(a, b), :] = moved_load
-            r[at(a, b), :] = moved_load
-    scope("diag")
-    inner_diagonal(g0, g1, g2t, ms, dg, tmp, cross)
-    scope("sums")
-    sum_yz([(v, a) for a in INSIDE for v in (dg, r)], lanes)
-
-    def inner_z(a):
-        for b in range(N):
-            inv = 1.0 / dg[at(a, b), :]
-            dg[at(a, b), :] = inv
-            z[at(a, b), :] = inv * r[at(a, b), :]
-
-    loop(1, LAST, inner_z)
-    scope("La1")
-    stiffness_a(z, g0, y)
-
-    def full(f, b):
-        return tile(row_of[f] + b * N)
-
-    def face_z(f):
-        for b in range(N):
-            rf[at(f, b), :] = mine[part(f, LOAD, b), :] + theirs[part(f, LOAD, b), :]
-            total = mine[part(f, DIAG, b), :] + theirs[part(f, DIAG, b), :]
-            a_sum[at(f, b), :] = total
-            df[at(f, b), :] = total
-        sum_yz([(rf, f), (df, f)], lanes)
-        for b in range(N):
-            inv = 1.0 / df[at(f, b), :]
-            df[at(f, b), :] = inv
-            zf[at(f, b), :] = inv * rf[at(f, b), :]
-
-    def tell(f, k, carried=None):
-        for b in range(N):
-            w_mine[at(f, b), :] = y[full(f, b), :] + cross[at(0, b), :] * zf[at(1 - f, b), :]
-        return swap(w_mine, w_theirs, f, f * FACE, FACE, k, carried)
-
-    scope("x_near")
-    sent_ld[0].wait()
-    scope("z_near")
-    face_z(0)
-    sent_w = [None, tell(1, 2, 4 * FACE)]
     scope("Lbc1")
     stiffness_bc(z, g1, g2t, ms, y, tmp, y)
     scope("hello")
 
     @pl.when(carrier)
     def _():
-        got = bag.at[pl.ds(4 * FACE, FACE)]
-        pltpu.make_async_copy(got, got, bag_recv.at[2]).wait()
-        carry(w_theirs, 4 * FACE, FACE, FACE, 2).start()
+        landed(bag.at[pl.ds(4 * FACE, FACE)], bag_recv.at[1])
+        carry(w_theirs, 4 * FACE, FACE, FACE, FAR_W)
 
     heard(hello.at[0], y_near)
     greet(hello.at[1], y_far)
@@ -558,16 +545,15 @@
     first = pl.multiple_of((1 - core) * FACE, FACE)
     couplings(g0, first, coupling)
     loop(1, LAST, lambda a: couple(zf, 0, coupling, y, a))
-    sent_g[0].wait()
     face_sums(0, mine, theirs, a_sum, a_sum, tmpf)
     s = face_terms(zf, 0, mine, theirs, a_sum, tmpf)
     for b in range(N):
         yf[at(0, b), :] = s[b]
+    sum_yz([(yf, 0)], lanes)
     scope("x_far")
-    sent_ld[1].wait()
+    sent_ld.wait_recv()
     scope("z_far")
     face_z(1)
-    sent_w[0] = tell(0, 2)
 
     scope("inner2")
     for a in INSIDE:
@@ -589,63 +575,63 @@
     den = energy_a(z, g0, u_ends, first, den)
     num, den = added_up(num), added_up(den)
     scope("g_far")
-    sent_g[1].wait()
+    sent_g.wait_recv()
     face_sums(1, mine, theirs, a_sum, a_sum, tmpf)
     s = face_terms(zf, 1, mine, theirs, a_sum, tmpf)
     for b in range(N):
         yf[at(1, b), :] = s[b]
+    sum_yz([(yf, 1)], lanes)
+    sent_w[0] = tell(0, NEAR_W)
 
     def face_p(f):
         for b in range(N):
             rows = at(f, b)
-            yf[rows, :] = yf[rows, :] + (w_mine[rows, :] + w_theirs[rows, :])
-        sum_yz([(yf, f)], lanes)
-        for b in range(N):
-            rows = at(f, b)
-            pf[rows, :] = COEF_Z * zf[rows, :] - COEF_Q * (df[rows, :] * yf[rows, :])
+            total = yf[rows, :] + (w_mine[rows, :] + w_theirs[rows, :])
+            pf[rows, :] = COEF_Z * zf[rows, :] - COEF_Q * (df[rows, :] * total)
 
     def face_dot(kind, f):
         return added_up([kind[part(f, LOAD, b), :] * pf[at(f, b), :] for b in range(N)])
 
-    scope("w_far")
-    sent_w[1].wait()
-    scope("ends2")
-    face_p(1)
-    num = num + face_dot(mine, 1)
-    den = (
-        den
-        + 0.5 * face_energy(pf, 1, theirs, a_sum)
-        + added_up([2.0 * u_ends[at(1, b), :] * pf[at(1, b), :] for b in range(N)])
-    )
-    for b in range(N):
-        q_mine[at(0, b), :] = 2.0 * (u_ends[at(0, b), :] + cross[at(0, b), :] * pf[at(1, b), :])
     acc[tile(0), :] = num
     acc[tile(8), :] = den
     takes = jnp.where(2 * x >= xs, core, 1 - core) == 1
     gives = jnp.logical_not(takes)
-    sent_q = pltpu.make_async_remote_copy(
-        src_ref=q_mine,
-        dst_ref=q_theirs,
-        send_sem=x_send.at[4, 0],
-        recv_sem=x_recv.at[4, 0],
-        device_id=(near_to,),
-        device_id_type=MESH,
-    )
-    pl.when(gives)(sent_q.start)
+    sent_q = remote(q_mine, q_theirs, x_recv.at[NEAR_Q], near_to)
+    scope("w_near")
 
     @pl.when(takes)
     def _():
-        sent_w[0].wait()
+        sent_w[0].wait_recv()
         face_p(0)
         sent_q.wait_recv()
         acc[tile(0), :] = acc[tile(0), :] + (face_dot(mine, 0) + face_dot(theirs, 0))
-        acc[tile(8), :] = (
-            acc[tile(8), :]
-            + face_energy(pf, 0, theirs, a_sum)
-            + added_up(
-                [(q_mine[at(0, b), :] + q_theirs[at(0, b), :]) * pf[at(0, b), :] for b in range(N)]
+        terms = [
+            (2.0 * u_ends[at(0, b), :] + q_theirs[at(0, b), :]) * pf[at(0, b), :] for b in range(N)
+        ]
+        acc[tile(8), :] = acc[tile(8), :] + (face_energy(pf, 0, theirs, a_sum) + added_up(terms))
+        for b in range(N):
+            q_mine[at(0, b), :] = 2.0 * cross[at(0, b), :] * pf[at(0, b), :]
+
+    scope("w_far")
+    sent_w[1].wait_recv()
+    scope("ends2")
+    face_p(1)
+    acc[tile(0), :] = acc[tile(0), :] + face_dot(mine, 1)
+    terms = [2.0 * u_ends[at(1, b), :] * pf[at(1, b), :] for b in range(N)]
+    acc[tile(8), :] = acc[tile(8), :] + (0.5 * face_energy(pf, 1, theirs, a_sum) + added_up(terms))
+
+    @pl.when(takes)
+    def _():
+        terms = [q_mine[at(0, b), :] * pf[at(1, b), :] for b in range(N)]
+        acc[tile(8), :] = acc[tile(8), :] + added_up(terms)
+
+    @pl.when(gives)
+    def _():
+        for b in range(N):
+            q_mine[at(0, b), :] = 2.0 * (
+                u_ends[at(0, b), :] + cross[at(0, b), :] * pf[at(1, b), :]
             )
-        )
+        sent_q.start()
 
     dots[0, 0:1, :] = jnp.sum(acc[tile(0), :], axis=0, keepdims=True)
     dots[0, 1:2, :] = jnp.sum(acc[tile(8), :], axis=0, keepdims=True)
@@ -660,7 +646,7 @@
         copy = pltpu.make_async_remote_copy(
             src_ref=src,
             dst_ref=dst,
-            send_sem=s_send.at[k],
+            send_sem=s_send,
             recv_sem=s_recv.at[k],
             device_id=(to,),
             device_id_type=MESH,
@@ -688,15 +674,13 @@
 
     @pl.when(gives)
     def _():
-        sent_w[0].wait()
+        sent_w[0].wait_recv()
         face_p(0)
-        sent_q.wait_send()
-
-    sent_i = []
+
     for f in faces:
         for b in range(N):
             i_mine[at(f, b), :] = u_ends[at(f, b), :] + cross[at(0, b), :] * pf[at(1 - f, b), :]
-        sent_i.append(swap(i_mine, i_theirs, f, f * FACE, FACE, 3))
+        swap(i_mine, i_theirs, f, f * FACE, FACE, IMAGE)
     for f in faces:
         s = face_terms(pf, f, mine, theirs, a_sum, tmpf)
         for b in range(N):
@@ -735,8 +719,7 @@
         got_b[zs - 1] = dots[1]
 
     scope("x3")
-    for copy in sent_i:
-        copy.wait()
+    landed(i_theirs, x_recv.at[IMAGE])
     for f in faces:
         for b in range(N):
             rows = at(f, b)
@@ -759,20 +742,26 @@
     scope("alpha")
     sums = jnp.sum(total, axis=1, keepdims=True)
     al_o[...] = jnp.broadcast_to(sums[0:1, :] / sums[1:2, :], (8, LANES))
-    @pl.when(carrier)
-    def _():
-        for k, first, rows in carried1:
-            carry(theirs, first - 4 * FACE, first, rows, k).wait_send()
-        carry(w_theirs, 4 * FACE, FACE, FACE, 2).wait_send()
+    plane_sends, line_sends = len(hops), 2 * zs - 1
 
     @pl.when(core == 0)
     def _():
-        arrived(got_a.at[pl.ds(0, len(hops) + 1)], s_send.at[0])
+        arrived(sent_all.at[pl.ds(0, plane_sends + 1)], s_send)
 
     @pl.when(core == 1)
     def _():
-        arrived(got_a.at[pl.ds(0, len(hops))], s_send.at[0])
-        arrived(got_a.at[pl.ds(0, 2 * zs - 1)], s_send.at[1])
+        arrived(sent_all.at[pl.ds(0, plane_sends + line_sends)], s_send)
+
+    for case, sends in (
+        (takes & jnp.logical_not(carrier), 12),
+        (takes & carrier, 17),
+        (gives & jnp.logical_not(carrier), 13),
+        (gives & carrier, 18),
+    ):
+
+        @pl.when(case)
+        def _(sends=sends):
+            landed(coef.at[pl.ds(0, sends * FACE)], x_send)
 
     scope(None)
 
@@ -780,22 +769,18 @@
 CHUNKS = 4
 
 
-def finish_kernel(p, r, im, al, x_h, r_h, x_v, r_v, sems):
+def finish_kernel(p, r, im, al, x_h, r_h, both, sem):
     alpha = al[...]
     size = ROWS // CHUNKS
-    copies = []
     for k in range(CHUNKS):
         for i in range(k * size, (k + 1) * size, N):
-            x_v[tile(i), :] = alpha * p[tile(i), :]
-        rows = pl.ds(k * size, size)
-        copies.append(pltpu.make_async_copy(x_v.at[rows], x_h.at[rows], sems.at[0, k]))
-        copies[-1].start()
+            both[tile(i), :] = alpha * p[tile(i), :]
+        pltpu.make_async_copy(both.at[pl.ds(k * size, size)], x_h.at[pl.ds(k * size, size)], sem).start()
         for i in range(k * size, (k + 1) * size, N):
-            r_v[tile(i), :] = r[tile(i), :] - alpha * im[tile(i), :]
-        copies.append(pltpu.make_async_copy(r_v.at[rows], r_h.at[rows], sems.at[1, k]))
-        copies[-1].start()
-    for copy in copies:
-        copy.wait()
+            both[tile(ROWS + i), :] = r[tile(i), :] - alpha * im[tile(i), :]
+        rows = pl.ds(ROWS + k * size, size)
+        pltpu.make_async_copy(both.at[rows], r_h.at[pl.ds(k * size, size)], sem).start()
+    pltpu.make_async_copy(both, both, sem).wait()
 
 
 def on_device(load_terms, geometry, mass_terms, element_order):
@@ -812,18 +797,18 @@
         in_specs=[in_hbm] * 4,
         out_specs=[in_vmem] * 4,
         scratch_shapes=[
-            *[field] * 12,
+            field, vm(4 * ROWS, LANES), *[field] * 7,
             *[vm(8 * FACE, LANES)] * 2,
             *[pair] * 4, vm(5 * FACE, LANES), *[pair] * 8, *[vm(FACE, LANES)] * 3,
             vm(12 * FACE, LANES), vm(16, LANES),
             vm(2, 2, LANES), vm(2 * ys * xs - 1, 2, LANES), vm(zs, 2, LANES),
+            vm(ys * xs + 2 * zs, 2, LANES),
             pltpu.VMEM((1, LANES), jnp.int32),
-            pltpu.SemaphoreType.DMA((6,)),
-            pltpu.SemaphoreType.DMA((5, 2)),
-            pltpu.SemaphoreType.DMA((5, 2)),
             pltpu.SemaphoreType.DMA((3,)),
-            pltpu.SemaphoreType.DMA((3,)),
+            pltpu.SemaphoreType.DMA(()),
+            pltpu.SemaphoreType.DMA((7,)),
             pltpu.SemaphoreType.DMA((2,)),
+            pltpu.SemaphoreType.DMA(()),
             pltpu.SemaphoreType.DMA((2,)),
             pltpu.SemaphoreType.REGULAR((3,)),
         ],
@@ -836,7 +821,7 @@
             pltpu.with_memory_space_constraint(t, pltpu.HBM)
             for t in (
                 load_terms.reshape(ROWS, LANES),
-                geometry.reshape(3, ROWS, LANES),
+                geometry.reshape(3 * ROWS, LANES),
                 mass_terms.reshape(ROWS, LANES),
                 element_order,
             )
@@ -847,7 +832,7 @@
         out_shape=(flat, flat),
         in_specs=[in_vmem] * 4,
         out_specs=[in_hbm] * 2,
-        scratch_shapes=[field, field, pltpu.SemaphoreType.DMA((2, CHUNKS))],
+        scratch_shapes=[vm(2 * ROWS, LANES), pltpu.SemaphoreType.DMA(())],
         compiler_params=pltpu.CompilerParams(vmem_limit_bytes=8 << 20),
         name="cg_finish",
     )(*[pltpu.with_memory_space_constraint(t, pltpu.VMEM) for t in parts])

time: 35.4 us -> 34.9 us (0.986)
  Pallas kernels: 34.6 us -> 34.1 us
    pallas_call x1, Pallas kernels: 33.8 us -> 33.3 us  [on_device(): pl.pallas_call(step_kernel, out_shape=(field, field, field, vm(8, LANES))...]
where the time goes in v6:
time: 34.9 us; the launch traced here: 34.7 us
  Pallas kernels  34.1 us (98%)
  between operations  0.64 us (2%)
    pallas_call x1, Pallas kernels, on_device(): pl.pallas_call(step_kernel, out_shape=(field, field, field, vm(8, LANES))...  33.3 us
    pallas_call x1, Pallas kernels, on_device(): pl.pallas_call(finish_kernel, out_shape=(flat, flat), in_specs=[in_vmem]...  0.79 us

profile of v6, /device:TPU:1, one launch (start us, length us, event | category | flops | bytes accessed | tf_op | source)
XLA Modules:
  0.0 34.7 jit_solution(2621000119113233824)
XLA Ops:
  0.6 33.3 %cg_step.1 = (f32[512,128]{1,0:T(8,128)S(1)}, f32[512,128]{1,0:T(8,128)S(1)}, f32[512,128]{1,0:T(8,128)S(1)}, f32[8,128]{1,0:T(8,128)S(1)}) custom-call(f32[512,128]{1,0:T(8,128)} %bitcast.6, f32[1536,128]{1,0:T(8,128)} %bitcast.5, f32[512,128]{1,0:T(8,128)} %bitcast.7, s32[1,128]{1,0:T(1,128)} %order_h.1), custom_call_target="tpu_custom_call" | custom-call | tf_op jit(solution)/shard_map/cg_step/pallas_call | solution.py:794
  33.9 0.8 %cg_finish.1 = (f32[512,128]{1,0:T(8,128)}, f32[512,128]{1,0:T(8,128)}) custom-call(f32[512,128]{1,0:T(8,128)S(1)} %get-tuple-element.8.p, f32[512,128]{1,0:T(8,128)S(1)} %get-tuple-element.9.r, f32[512,128]{1,0:T(8,128)S(1)} %get-tuple-element.10.im, f32[8,128]{1,0:T(8,128)S(1)} %get-tuple-element.11.al), custom_call_target="tpu_custom_call" | custom-call | tf_op jit(solution)/shard_map/cg_finish/pallas_call | solution.py:830

commit v7 on v6

--- a/solution.py
+++ b/solution.py
@@ -19,6 +19,7 @@
 HALF = 1.35
 MESH = pl.DeviceIdType.MESH
 TORUS = (8, 12, 4, 2)
+ROOT = 1
 INSIDE = range(1, LAST)
 UNROLL_A = 4
 UNROLL_BC = 3
@@ -277,7 +278,7 @@
     ld, coef, g2t, r, dg, z, y, u, tmp,
     mine, theirs, w_mine, w_theirs, i_mine, i_theirs, bag, rf, df, zf, pf, yf, a_sum, tmpf,
     u_ends, cross, q_mine, q_theirs, coupling, acc,
-    dots, got_a, got_b, sent_all, order_v, in_sems, x_send, x_recv, bag_recv, s_send, s_recv, hello,
+    dots, fold, got_a, got_b, got_one, sent_all, order_v, in_sems, x_send, x_recv, bag_recv, s_send, s_recv, one_send, one_recv, hello,
 ):
     stack = []
 
@@ -360,7 +361,28 @@
         return 0
 
     lax.fori_loop(z_at + 1, zs, higher, 0)
-    expected = len(row) + len(y_near) + 2 + 2 * carrier.astype(jnp.int32) + 2 * core * z_at
+    is_root = me == ROOT
+    others_than_root = jnp.logical_not(is_root)
+
+    @pl.when(is_root)
+    def _():
+        def everyone(q, _):
+            @pl.when(q != ROOT)
+            def _():
+                greet(barrier, [q])
+
+            return 0
+
+        lax.fori_loop(0, count, everyone, 0)
+
+    expected = (
+        len(row)
+        + len(y_near)
+        + 2
+        + 2 * carrier.astype(jnp.int32)
+        + 2 * core * z_at
+        + others_than_root.astype(jnp.int32)
+    )
 
     scope("idx")
     loads[0].wait()
@@ -633,8 +655,15 @@
             )
         sent_q.start()
 
-    dots[0, 0:1, :] = jnp.sum(acc[tile(0), :], axis=0, keepdims=True)
-    dots[0, 1:2, :] = jnp.sum(acc[tile(8), :], axis=0, keepdims=True)
+    num_row = jnp.sum(acc[tile(0), :], axis=0, keepdims=True)
+    den_row = jnp.sum(acc[tile(8), :], axis=0, keepdims=True)
+    dots[0, 0:1, :] = num_row
+    dots[0, 1:2, :] = den_row
+    half = LANES // 2
+    first_half = lane[0:1, :] < half
+    fold[0, 0:1, :] = jnp.where(
+        first_half, num_row + pltpu.roll(num_row, half, 1), den_row + pltpu.roll(den_row, half, 1)
+    )
 
     hops = sorted(
         ((dy, dx) for dy in range(ys) for dx in range(xs) if dy or dx),
@@ -663,8 +692,21 @@
         return functools.reduce(plus, [t for t in part if t is not None])
 
     heard(hello.at[1], y_far)
+    by_z = z_at * ys * line + y_at * line + lax.rem(me, line)
     for j, (dy, dx) in enumerate(hops):
         send(dots.at[0], got_a.at[2 * j + core], 0, moved(dy=dy, dx=dx) + 1 - core)
+        if j == len(hops) // 2:
+
+            @pl.when(others_than_root)
+            def _():
+                pltpu.make_async_remote_copy(
+                    src_ref=fold.at[0],
+                    dst_ref=got_one.at[jnp.maximum(by_z - 1, 0)],
+                    send_sem=one_send,
+                    recv_sem=one_recv.at[jnp.where(z_at < zs // 2, 0, 1)],
+                    device_id=(ROOT,),
+                    device_id_type=MESH,
+                ).start()
 
     @pl.when(core == 0)
     def _():
@@ -713,8 +755,12 @@
             pl.semaphore_wait(hello.at[2], zs - 1 - z_at)
 
         for k in sorted(range(1, zs), key=lambda k: -min(k, zs - k)):
-            for c in (0, 1):
-                send(dots.at[1], got_b.at[k - 1], 1, moved(dz=k) - c)
+            send(dots.at[1], got_b.at[k - 1], 1, moved(dz=k) - 1)
+
+            @pl.when(moved(dz=k) != ROOT)
+            def _(k=k):
+                send(dots.at[1], got_b.at[k - 1], 1, moved(dz=k))
+
         send(dots.at[1], got_b.at[zs - 1], 1, me - 1)
         got_b[zs - 1] = dots[1]
 
@@ -734,23 +780,56 @@
     def _():
         arrived(got_b, s_recv.at[1])
 
-    @pl.when(core == 1)
+    @pl.when((core == 1) & others_than_root)
     def _():
         arrived(got_b.at[pl.ds(0, zs - 1)], s_recv.at[1])
 
-    total = added(got_b, None, zs)
+    @pl.when(others_than_root)
+    def _():
+        dots[2] = added(got_b, None, zs)
+
+    @pl.when(is_root)
+    def _():
+        early_ones = count // 2 - 1
+        arrived(got_one.at[pl.ds(0, early_ones)], one_recv.at[0])
+        arrived(got_one.at[pl.ds(early_ones, count // 2)], one_recv.at[1])
+        width = 16
+
+        def some(k, sums):
+            for i in range(width):
+                sums[i % 8] = sums[i % 8] + got_one[k * width + i]
+            return sums
+
+        blank = jnp.zeros((1, LANES), jnp.float32)
+        whole = (count - 1) // width
+        sums = lax.fori_loop(0, whole, some, [blank] * 8)
+        for k in range(whole * width, count - 1):
+            sums[k % 8] = sums[k % 8] + got_one[k]
+        row_sum = added_up(sums) + fold[0]
+        dots[2, 0:1, :] = jnp.where(first_half, row_sum, 0.0)
+        dots[2, 1:2, :] = jnp.where(first_half, 0.0, row_sum)
+
+    total = dots[2]
     scope("alpha")
     sums = jnp.sum(total, axis=1, keepdims=True)
     al_o[...] = jnp.broadcast_to(sums[0:1, :] / sums[1:2, :], (8, LANES))
     plane_sends, line_sends = len(hops), 2 * zs - 1
-
-    @pl.when(core == 0)
-    def _():
-        arrived(sent_all.at[pl.ds(0, plane_sends + 1)], s_send)
-
-    @pl.when(core == 1)
-    def _():
-        arrived(sent_all.at[pl.ds(0, plane_sends + line_sends)], s_send)
+    above_root = lax.rem(me, plane_size) // line * line + ROOT == me
+    above_root = above_root & others_than_root & (y_at == 0)
+
+    @pl.when(others_than_root)
+    def _():
+        arrived(fold.at[0], one_send)
+
+    for case, sends in (
+        (core == 0, plane_sends + 1),
+        ((core == 1) & above_root, plane_sends + line_sends - 1),
+        ((core == 1) & jnp.logical_not(above_root), plane_sends + line_sends),
+    ):
+
+        @pl.when(case)
+        def _(sends=sends):
+            arrived(sent_all.at[pl.ds(0, sends)], s_send)
 
     for case, sends in (
         (takes & jnp.logical_not(carrier), 12),
@@ -801,12 +880,15 @@
             *[vm(8 * FACE, LANES)] * 2,
             *[pair] * 4, vm(5 * FACE, LANES), *[pair] * 8, *[vm(FACE, LANES)] * 3,
             vm(12 * FACE, LANES), vm(16, LANES),
-            vm(2, 2, LANES), vm(2 * ys * xs - 1, 2, LANES), vm(zs, 2, LANES),
+            vm(3, 2, LANES), vm(1, 1, LANES), vm(2 * ys * xs - 1, 2, LANES), vm(zs, 2, LANES),
+            vm(ys * zs * xs * cores - 1, 1, LANES),
             vm(ys * xs + 2 * zs, 2, LANES),
             pltpu.VMEM((1, LANES), jnp.int32),
             pltpu.SemaphoreType.DMA((3,)),
             pltpu.SemaphoreType.DMA(()),
             pltpu.SemaphoreType.DMA((7,)),
+            pltpu.SemaphoreType.DMA((2,)),
+            pltpu.SemaphoreType.DMA(()),
             pltpu.SemaphoreType.DMA((2,)),
             pltpu.SemaphoreType.DMA(()),
             pltpu.SemaphoreType.DMA((2,)),

time: 34.9 us -> 34 us (0.974)
  Pallas kernels: 34.1 us -> 33.2 us
    pallas_call x1, Pallas kernels: 33.3 us -> 32.4 us  [on_device(): pl.pallas_call(step_kernel, out_shape=(field, field, field, vm(8, LANES))...]
where the time goes in v7:
time: 34 us; the launch traced here: 33.9 us
  Pallas kernels  33.2 us (98%)
  between operations  0.64 us (2%)
    pallas_call x1, Pallas kernels, on_device(): pl.pallas_call(step_kernel, out_shape=(field, field, field, vm(8, LANES))...  32.4 us
    pallas_call x1, Pallas kernels, on_device(): pl.pallas_call(finish_kernel, out_shape=(flat, flat), in_specs=[in_vmem]...  0.79 us

profile of v7, /device:TPU:1, one launch (start us, length us, event | category | flops | bytes accessed | tf_op | source)
XLA Modules:
  0.0 33.9 jit_solution(6568954208604498607)
XLA Ops:
  0.6 32.4 %cg_step.1 = (f32[512,128]{1,0:T(8,128)S(1)}, f32[512,128]{1,0:T(8,128)S(1)}, f32[512,128]{1,0:T(8,128)S(1)}, f32[8,128]{1,0:T(8,128)S(1)}) custom-call(f32[512,128]{1,0:T(8,128)} %bitcast.6, f32[1536,128]{1,0:T(8,128)} %bitcast.5, f32[512,128]{1,0:T(8,128)} %bitcast.7, s32[1,128]{1,0:T(1,128)} %order_h.1), custom_call_target="tpu_custom_call" | custom-call | tf_op jit(solution)/shard_map/cg_step/pallas_call | solution.py:873
  33.1 0.8 %cg_finish.1 = (f32[512,128]{1,0:T(8,128)}, f32[512,128]{1,0:T(8,128)}) custom-call(f32[512,128]{1,0:T(8,128)S(1)} %get-tuple-element.8.p, f32[512,128]{1,0:T(8,128)S(1)} %get-tuple-element.9.r, f32[512,128]{1,0:T(8,128)S(1)} %get-tuple-element.10.im, f32[8,128]{1,0:T(8,128)S(1)} %get-tuple-element.11.al), custom_call_target="tpu_custom_call" | custom-call | tf_op jit(solution)/shard_map/cg_finish/pallas_call | solution.py:912

commit v8 on v7

--- a/solution.py
+++ b/solution.py
@@ -97,7 +97,7 @@
 
 
 LOAD, DIAG, G1, G2 = range(4)
-NEAR, FAR_LD, FAR_G, NEAR_W, FAR_W, IMAGE, NEAR_Q = range(7)
+NEAR, FAR_LD, FAR_G, NEAR_W, FAR_W, IMAGE = range(6)
 
 
 def part(f, kind, i):
@@ -275,10 +275,10 @@
 
 def step_kernel(
     load_h, geom_h, mass_h, order_h, p_o, r_o, im_o, al_o,
-    ld, coef, g2t, r, dg, z, y, u, tmp,
+    coef, g2t, r, dg, z, y, u, tmp,
     mine, theirs, w_mine, w_theirs, i_mine, i_theirs, bag, rf, df, zf, pf, yf, a_sum, tmpf,
     u_ends, cross, q_mine, q_theirs, coupling, acc,
-    dots, fold, got_a, got_b, got_one, sent_all, order_v, in_sems, x_send, x_recv, bag_recv, s_send, s_recv, one_send, one_recv, hello,
+    dots, got_a, got_b, got_one, all_sent, order_v, in_sems, x_send, x_recv, bag_recv, s_recv, one_recv, hello,
 ):
     stack = []
 
@@ -314,14 +314,14 @@
         pltpu.make_async_copy(src, dst, in_sems.at[k])
         for k, src, dst in (
             (0, order_h, order_v),
-            (1, load_h, ld),
-            (2, geom_h, coef.at[pl.ds(0, 3 * ROWS)]),
-            (2, mass_h, coef.at[pl.ds(3 * ROWS, ROWS)]),
+            (1, load_h, coef.at[pl.ds(4 * ROWS, ROWS)]),
+            (1, geom_h, coef.at[pl.ds(0, 3 * ROWS)]),
+            (1, mass_h, coef.at[pl.ds(3 * ROWS, ROWS)]),
         )
     ]
     for copy in loads:
         copy.start()
-    g0, g1, g2, ms = (coef.at[pl.ds(k * ROWS, ROWS)] for k in range(4))
+    g0, g1, g2, ms, ld = (coef.at[pl.ds(k * ROWS, ROWS)] for k in range(5))
 
     y_at = me // plane_size
     z_at = in_plane // line
@@ -425,13 +425,13 @@
             device_id_type=MESH,
         )
 
-    def swap(src, dst, f, first, rows, k, carried=None, bag_k=None):
+    def swap(src, dst, f, first, rows, k, carried=None):
         src, dst = src.at[pl.ds(first, rows)], dst.at[pl.ds(first, rows)]
         copy = remote(src, dst, x_recv.at[k], sides[f])
         if carried is None:
             copy.start()
         else:
-            by_bag = remote(src, bag.at[pl.ds(carried, rows)], bag_recv.at[bag_k], carrier_of_early)
+            by_bag = remote(src, bag.at[pl.ds(carried, rows)], bag_recv, carrier_of_early)
             pl.when(early)(by_bag.start)
             pl.when(jnp.logical_not(early))(copy.start)
         return copy
@@ -446,11 +446,10 @@
     both = (0, LAST)
     faces = (0, 1)
     scope("load_ends")
-    loads[1].wait()
+    pltpu.make_async_copy(coef, coef, in_sems.at[1]).wait()
     for a in both:
         for b in range(N):
             mine[part(face_of[a], LOAD, b), :] = lane_pick(ld[at(a, b), :], inverse)
-    pltpu.make_async_copy(coef, coef, in_sems.at[2]).wait()
     for k, a in enumerate(both):
         s = contract(SQUARED.T, [g2[across(a, c), :] for c in range(N)], 1)
         for c in range(N):
@@ -473,15 +472,17 @@
     pl.semaphore_wait(barrier, expected)
     scope("send1")
 
+    sent_ld = swap(mine, theirs, 1, 4 * FACE, 2 * FACE, FAR_LD, 0)
+    sent_g = swap(mine, theirs, 1, 6 * FACE, 2 * FACE, FAR_G, 2 * FACE)
+    sent_near = swap(mine, theirs, 0, 0, 4 * FACE, NEAR)
+
     @pl.when(carrier)
     def _():
-        landed(bag.at[pl.ds(0, 4 * FACE)], bag_recv.at[0])
+        landed(bag, bag_recv)
         carry(theirs, 0, 4 * FACE, 2 * FACE, FAR_LD)
         carry(theirs, 2 * FACE, 6 * FACE, 2 * FACE, FAR_G)
-
-    sent_ld = swap(mine, theirs, 1, 4 * FACE, 2 * FACE, FAR_LD, 0, 0)
-    sent_g = swap(mine, theirs, 1, 6 * FACE, 2 * FACE, FAR_G, 2 * FACE, 0)
-    sent_near = swap(mine, theirs, 0, 0, 4 * FACE, NEAR)
+        carry(w_theirs, 4 * FACE, FACE, FACE, FAR_W)
+
     greet(hello.at[0], y_near)
 
     @pl.when(core == 1)
@@ -539,7 +540,7 @@
         for b in range(N):
             w_mine[at(f, b), :] = y[full(f, b), :] + cross[at(0, b), :] * zf[at(1 - f, b), :]
         sum_yz([(w_mine, f)], lanes)
-        return swap(w_mine, w_theirs, f, f * FACE, FACE, k, carried, 1)
+        return swap(w_mine, w_theirs, f, f * FACE, FACE, k, carried)
 
     scope("x_near")
     sent_near.wait_recv()
@@ -555,11 +556,6 @@
     scope("Lbc1")
     stiffness_bc(z, g1, g2t, ms, y, tmp, y)
     scope("hello")
-
-    @pl.when(carrier)
-    def _():
-        landed(bag.at[pl.ds(4 * FACE, FACE)], bag_recv.at[1])
-        carry(w_theirs, 4 * FACE, FACE, FACE, FAR_W)
 
     heard(hello.at[0], y_near)
     greet(hello.at[1], y_far)
@@ -618,14 +614,13 @@
     acc[tile(8), :] = den
     takes = jnp.where(2 * x >= xs, core, 1 - core) == 1
     gives = jnp.logical_not(takes)
-    sent_q = remote(q_mine, q_theirs, x_recv.at[NEAR_Q], near_to)
+    sent_q = remote(q_mine, q_theirs, x_recv.at[NEAR_W], near_to)
     scope("w_near")
 
     @pl.when(takes)
     def _():
-        sent_w[0].wait_recv()
+        landed(w_mine, x_recv.at[NEAR_W])
         face_p(0)
-        sent_q.wait_recv()
         acc[tile(0), :] = acc[tile(0), :] + (face_dot(mine, 0) + face_dot(theirs, 0))
         terms = [
             (2.0 * u_ends[at(0, b), :] + q_theirs[at(0, b), :]) * pf[at(0, b), :] for b in range(N)
@@ -659,12 +654,6 @@
     den_row = jnp.sum(acc[tile(8), :], axis=0, keepdims=True)
     dots[0, 0:1, :] = num_row
     dots[0, 1:2, :] = den_row
-    half = LANES // 2
-    first_half = lane[0:1, :] < half
-    fold[0, 0:1, :] = jnp.where(
-        first_half, num_row + pltpu.roll(num_row, half, 1), den_row + pltpu.roll(den_row, half, 1)
-    )
-
     hops = sorted(
         ((dy, dx) for dy in range(ys) for dx in range(xs) if dy or dx),
         key=lambda d: -min(d[0], ys - d[0]) - min(d[1], xs - d[1]),
@@ -675,7 +664,7 @@
         copy = pltpu.make_async_remote_copy(
             src_ref=src,
             dst_ref=dst,
-            send_sem=s_send,
+            send_sem=x_send,
             recv_sem=s_recv.at[k],
             device_id=(to,),
             device_id_type=MESH,
@@ -692,21 +681,26 @@
         return functools.reduce(plus, [t for t in part if t is not None])
 
     heard(hello.at[1], y_far)
-    by_z = z_at * ys * line + y_at * line + lax.rem(me, line)
+    last_from, last_to = zs // 2, zs // 2 + max(zs // 4, 1)
+    is_last = (z_at >= last_from) & (z_at < last_to)
+    rank = jnp.where(
+        is_last, z_at + zs - last_to, jnp.where(z_at < last_from, z_at, z_at - (last_to - last_from))
+    )
+    by_z = rank * ys * line + y_at * line + lax.rem(me, line)
+
+    @pl.when(others_than_root)
+    def _():
+        pltpu.make_async_remote_copy(
+            src_ref=dots.at[0],
+            dst_ref=got_one.at[jnp.maximum(by_z - 1, 0)],
+            send_sem=x_send,
+            recv_sem=one_recv.at[jnp.where(is_last, 1, 0)],
+            device_id=(ROOT,),
+            device_id_type=MESH,
+        ).start()
+
     for j, (dy, dx) in enumerate(hops):
         send(dots.at[0], got_a.at[2 * j + core], 0, moved(dy=dy, dx=dx) + 1 - core)
-        if j == len(hops) // 2:
-
-            @pl.when(others_than_root)
-            def _():
-                pltpu.make_async_remote_copy(
-                    src_ref=fold.at[0],
-                    dst_ref=got_one.at[jnp.maximum(by_z - 1, 0)],
-                    send_sem=one_send,
-                    recv_sem=one_recv.at[jnp.where(z_at < zs // 2, 0, 1)],
-                    device_id=(ROOT,),
-                    device_id_type=MESH,
-                ).start()
 
     @pl.when(core == 0)
     def _():
@@ -790,57 +784,51 @@
 
     @pl.when(is_root)
     def _():
-        early_ones = count // 2 - 1
+        width = 16
+        last_ones = (last_to - last_from) * ys * line
+        early_ones = count - 1 - last_ones
+
+        def sum_of(start, number, sums):
+            def some(k, sums):
+                for i in range(width):
+                    sums[i % 8] = sums[i % 8] + got_one[start + k * width + i]
+                return sums
+
+            whole = number // width
+            sums = lax.fori_loop(0, whole, some, sums)
+            for k in range(whole * width, number):
+                sums[k % 8] = sums[k % 8] + got_one[start + k]
+            return sums
+
         arrived(got_one.at[pl.ds(0, early_ones)], one_recv.at[0])
-        arrived(got_one.at[pl.ds(early_ones, count // 2)], one_recv.at[1])
-        width = 16
-
-        def some(k, sums):
-            for i in range(width):
-                sums[i % 8] = sums[i % 8] + got_one[k * width + i]
-            return sums
-
-        blank = jnp.zeros((1, LANES), jnp.float32)
-        whole = (count - 1) // width
-        sums = lax.fori_loop(0, whole, some, [blank] * 8)
-        for k in range(whole * width, count - 1):
-            sums[k % 8] = sums[k % 8] + got_one[k]
-        row_sum = added_up(sums) + fold[0]
-        dots[2, 0:1, :] = jnp.where(first_half, row_sum, 0.0)
-        dots[2, 1:2, :] = jnp.where(first_half, 0.0, row_sum)
+        sums = sum_of(0, early_ones, [jnp.zeros((2, LANES), jnp.float32)] * 8)
+        sums[0] = sums[0] + dots[0]
+        arrived(got_one.at[pl.ds(early_ones, last_ones)], one_recv.at[1])
+        sums = sum_of(early_ones, last_ones, sums)
+        dots[2] = added_up(sums)
 
     total = dots[2]
     scope("alpha")
     sums = jnp.sum(total, axis=1, keepdims=True)
     al_o[...] = jnp.broadcast_to(sums[0:1, :] / sums[1:2, :], (8, LANES))
-    plane_sends, line_sends = len(hops), 2 * zs - 1
-    above_root = lax.rem(me, plane_size) // line * line + ROOT == me
-    above_root = above_root & others_than_root & (y_at == 0)
-
-    @pl.when(others_than_root)
-    def _():
-        arrived(fold.at[0], one_send)
-
-    for case, sends in (
-        (core == 0, plane_sends + 1),
-        ((core == 1) & above_root, plane_sends + line_sends - 1),
-        ((core == 1) & jnp.logical_not(above_root), plane_sends + line_sends),
+    face_rows = FACE // 2
+    above_root = (core == 1) & (in_plane // line * line + ROOT == me) & others_than_root
+    sums_0, sums_1 = len(hops) + 2, len(hops) + 2 * zs
+    for sums_sent, many in (
+        (core == 0, sums_0),
+        ((core == 1) & jnp.logical_not(above_root | is_root), sums_1),
+        (above_root | is_root, sums_1 - 1),
     ):
-
-        @pl.when(case)
-        def _(sends=sends):
-            arrived(sent_all.at[pl.ds(0, sends)], s_send)
-
-    for case, sends in (
-        (takes & jnp.logical_not(carrier), 12),
-        (takes & carrier, 17),
-        (gives & jnp.logical_not(carrier), 13),
-        (gives & carrier, 18),
-    ):
-
-        @pl.when(case)
-        def _(sends=sends):
-            landed(coef.at[pl.ds(0, sends * FACE)], x_send)
+        for faces_sent, faces in (
+            (takes & jnp.logical_not(carrier), 12),
+            (takes & carrier, 17),
+            (gives & jnp.logical_not(carrier), 13),
+            (gives & carrier, 18),
+        ):
+
+            @pl.when(sums_sent & faces_sent)
+            def _(sent=many + faces * face_rows):
+                arrived(all_sent.at[pl.ds(0, sent)], x_send)
 
     scope(None)
 
@@ -876,21 +864,19 @@
         in_specs=[in_hbm] * 4,
         out_specs=[in_vmem] * 4,
         scratch_shapes=[
-            field, vm(4 * ROWS, LANES), *[field] * 7,
+            vm(5 * ROWS, LANES), *[field] * 7,
             *[vm(8 * FACE, LANES)] * 2,
             *[pair] * 4, vm(5 * FACE, LANES), *[pair] * 8, *[vm(FACE, LANES)] * 3,
             vm(12 * FACE, LANES), vm(16, LANES),
-            vm(3, 2, LANES), vm(1, 1, LANES), vm(2 * ys * xs - 1, 2, LANES), vm(zs, 2, LANES),
-            vm(ys * zs * xs * cores - 1, 1, LANES),
-            vm(ys * xs + 2 * zs, 2, LANES),
+            vm(3, 2, LANES), vm(2 * ys * xs - 1, 2, LANES), vm(zs, 2, LANES),
+            vm(ys * zs * xs * cores - 1, 2, LANES),
+            vm(18 * FACE // 2 + ys * xs + 2 * zs, 2, LANES),
             pltpu.VMEM((1, LANES), jnp.int32),
-            pltpu.SemaphoreType.DMA((3,)),
-            pltpu.SemaphoreType.DMA(()),
-            pltpu.SemaphoreType.DMA((7,)),
             pltpu.SemaphoreType.DMA((2,)),
             pltpu.SemaphoreType.DMA(()),
+            pltpu.SemaphoreType.DMA((6,)),
+            pltpu.SemaphoreType.DMA(()),
             pltpu.SemaphoreType.DMA((2,)),
-            pltpu.SemaphoreType.DMA(()),
             pltpu.SemaphoreType.DMA((2,)),
             pltpu.SemaphoreType.REGULAR((3,)),
         ],

time: 34 us -> 33.7 us (level)
  Pallas kernels: 33.2 us -> 32.8 us
    pallas_call x1, Pallas kernels: 32.4 us -> 32 us  [on_device(): pl.pallas_call(step_kernel, out_shape=(field, field, field, vm(8, LANES))...]
where the time goes in v8:
time: 33.7 us; the launch traced here: 33.5 us
  Pallas kernels  32.8 us (97%)
  between operations  0.64 us (2%)
    pallas_call x1, Pallas kernels, on_device(): pl.pallas_call(step_kernel, out_shape=(field, field, field, vm(8, LANES))...  32 us
    pallas_call x1, Pallas kernels, on_device(): pl.pallas_call(finish_kernel, out_shape=(flat, flat), in_specs=[in_vmem]...  0.79 us

profile of v8, /device:TPU:1, one launch (start us, length us, event | category | flops | bytes accessed | tf_op | source)
XLA Modules:
  0.0 33.5 jit_solution(7101430878019339342)
XLA Ops:
  0.6 32.0 %cg_step.1 = (f32[512,128]{1,0:T(8,128)S(1)}, f32[512,128]{1,0:T(8,128)S(1)}, f32[512,128]{1,0:T(8,128)S(1)}, f32[8,128]{1,0:T(8,128)S(1)}) custom-call(f32[512,128]{1,0:T(8,128)} %bitcast.6, f32[1536,128]{1,0:T(8,128)} %bitcast.5, f32[512,128]{1,0:T(8,128)} %bitcast.7, s32[1,128]{1,0:T(1,128)} %order_h.1), custom_call_target="tpu_custom_call" | custom-call | tf_op jit(solution)/shard_map/cg_step/pallas_call | solution.py:861
  32.7 0.8 %cg_finish.1 = (f32[512,128]{1,0:T(8,128)}, f32[512,128]{1,0:T(8,128)}) custom-call(f32[512,128]{1,0:T(8,128)S(1)} %get-tuple-element.8.p, f32[512,128]{1,0:T(8,128)S(1)} %get-tuple-element.9.r, f32[512,128]{1,0:T(8,128)S(1)} %get-tuple-element.10.im, f32[8,128]{1,0:T(8,128)S(1)} %get-tuple-element.11.al), custom_call_target="tpu_custom_call" | custom-call | tf_op jit(solution)/shard_map/cg_finish/pallas_call | solution.py:898

commit v9 on v8

--- a/solution.py
+++ b/solution.py
@@ -19,7 +19,7 @@
 HALF = 1.35
 MESH = pl.DeviceIdType.MESH
 TORUS = (8, 12, 4, 2)
-ROOT = 1
+ROOTS = (1, 3, 97, 2, 96)
 INSIDE = range(1, LAST)
 UNROLL_A = 4
 UNROLL_BC = 3
@@ -361,19 +361,25 @@
         return 0
 
     lax.fori_loop(z_at + 1, zs, higher, 0)
-    is_root = me == ROOT
+    roots = [r for r in ROOTS if r < count]
+
+    def one_of(device, some):
+        return functools.reduce(jnp.logical_or, [device == r for r in some])
+
+    is_root = one_of(me, roots)
     others_than_root = jnp.logical_not(is_root)
 
     @pl.when(is_root)
     def _():
-        def everyone(q, _):
-            @pl.when(q != ROOT)
-            def _():
-                greet(barrier, [q])
-
+        width = next(k for k in range(16, 0, -1) if (count - 1) % k == 0)
+
+        def everyone(k, _):
+            for i in range(width):
+                q = me + 1 + k * width + i
+                greet(barrier, [jnp.where(q >= count, q - count, q)])
             return 0
 
-        lax.fori_loop(0, count, everyone, 0)
+        lax.fori_loop(0, (count - 1) // width, everyone, 0)
 
     expected = (
         len(row)
@@ -381,7 +387,8 @@
         + 2
         + 2 * carrier.astype(jnp.int32)
         + 2 * core * z_at
-        + others_than_root.astype(jnp.int32)
+        + len(roots)
+        - is_root.astype(jnp.int32)
     )
 
     scope("idx")
@@ -680,31 +687,71 @@
             part[j % 4] = plus(part[j % 4], ref[j])
         return functools.reduce(plus, [t for t in part if t is not None])
 
+    half_z, pair_z = zs // 2, zs // 2 + zs // 8
+    in_line = y_at * line + lax.rem(me, line)
+    slow_low = (z_at == pair_z) & (x == xs - 1) & (core == 1)
+    slow_high = (z_at == pair_z + 1) & (x == 0) & (core == 0)
+    slow_ones = ys * (2 if pair_z + 1 < zs else 1)
+    slow_before = jnp.where(
+        z_at > pair_z + 1,
+        slow_ones,
+        jnp.where(
+            z_at == pair_z + 1,
+            ys + y_at + (lax.rem(me, line) > 0).astype(jnp.int32),
+            jnp.where(z_at == pair_z, y_at, 0),
+        ),
+    )
+    slot = jnp.where(
+        slow_low | slow_high,
+        count - slow_ones + jnp.where(slow_high, ys, 0) + y_at,
+        z_at * ys * line + in_line - slow_before,
+    )
+    group = jnp.where(slow_low | slow_high, 2, jnp.where(z_at < half_z, 0, 1))
+    group_0 = half_z * ys * line - 1
+    groups = (group_0, count - 1 - group_0 - slow_ones, slow_ones)
+
+    def root_sum(k, total):
+        width, start, number = 16, sum(groups[:k]), groups[k]
+        arrived(got_one.at[pl.ds(start, number)], one_recv.at[k])
+        sums = [total] + [jnp.zeros((2, LANES), jnp.float32)] * 7
+
+        def some(i, sums):
+            return [
+                sums[j] + got_one[start + i * width + j] + got_one[start + i * width + j + 8]
+                for j in range(8)
+            ]
+
+        whole = number // width
+        sums = lax.fori_loop(0, whole, some, sums)
+        for i in range(whole * width, number):
+            sums[i % 8] = sums[i % 8] + got_one[start + i]
+        return added_up(sums)
+
+    def send_to_root(r):
+        at_root = r // plane_size * line + r % line
+
+        @pl.when(me != r)
+        def _():
+            pltpu.make_async_remote_copy(
+                src_ref=dots.at[0],
+                dst_ref=got_one.at[slot - (slot > at_root).astype(jnp.int32)],
+                send_sem=x_send,
+                recv_sem=one_recv.at[group],
+                device_id=(r,),
+                device_id_type=MESH,
+            ).start()
+
+    send_to_root(roots[0])
     heard(hello.at[1], y_far)
-    last_from, last_to = zs // 2, zs // 2 + max(zs // 4, 1)
-    is_last = (z_at >= last_from) & (z_at < last_to)
-    rank = jnp.where(
-        is_last, z_at + zs - last_to, jnp.where(z_at < last_from, z_at, z_at - (last_to - last_from))
-    )
-    by_z = rank * ys * line + y_at * line + lax.rem(me, line)
-
-    @pl.when(others_than_root)
-    def _():
-        pltpu.make_async_remote_copy(
-            src_ref=dots.at[0],
-            dst_ref=got_one.at[jnp.maximum(by_z - 1, 0)],
-            send_sem=x_send,
-            recv_sem=one_recv.at[jnp.where(is_last, 1, 0)],
-            device_id=(ROOT,),
-            device_id_type=MESH,
-        ).start()
-
     for j, (dy, dx) in enumerate(hops):
         send(dots.at[0], got_a.at[2 * j + core], 0, moved(dy=dy, dx=dx) + 1 - core)
 
     @pl.when(core == 0)
     def _():
         send(dots.at[0], got_a.at[others - 1], 0, me + 1)
+
+    for other_root in roots[1:]:
+        send_to_root(other_root)
 
     scope("u_ends")
 
@@ -737,7 +784,16 @@
                 dst[full(f, b), :] = lane_pick(ends[at(f, b), :], order)
     sum_yz([(u, a) for a in INSIDE], lanes)
     reorder(u, im_o, order, INSIDE)
+    scope("root_0")
+
+    @pl.when(is_root)
+    def _():
+        dots[2] = root_sum(0, dots[0])
+
     scope("plane")
+    first_of_column = me - z_at * line
+    skip_0 = one_of(first_of_column - 1, [r for r in roots if r % cores == 0] or [-1])
+    skip_1 = one_of(first_of_column, [r for r in roots if r % cores == 1])
 
     @pl.when(core == 1)
     def _():
@@ -749,13 +805,17 @@
             pl.semaphore_wait(hello.at[2], zs - 1 - z_at)
 
         for k in sorted(range(1, zs), key=lambda k: -min(k, zs - k)):
-            send(dots.at[1], got_b.at[k - 1], 1, moved(dz=k) - 1)
-
-            @pl.when(moved(dz=k) != ROOT)
-            def _(k=k):
-                send(dots.at[1], got_b.at[k - 1], 1, moved(dz=k))
-
-        send(dots.at[1], got_b.at[zs - 1], 1, me - 1)
+            to_first = z_at == zs - k
+            for c, skip in ((1, skip_0), (0, skip_1)):
+
+                @pl.when(jnp.logical_not(to_first & skip))
+                def _(k=k, c=c):
+                    send(dots.at[1], got_b.at[k - 1], 1, moved(dz=k) - c)
+
+        @pl.when(jnp.logical_not((z_at == 0) & skip_0))
+        def _():
+            send(dots.at[1], got_b.at[zs - 1], 1, me - 1)
+
         got_b[zs - 1] = dots[1]
 
     scope("x3")
@@ -768,9 +828,26 @@
     for f in faces:
         for b in range(N):
             im_o[full(f, b), :] = lane_pick(yf[at(f, b), :], order)
+    face_rows = FACE // 2
+    skipped = is_root.astype(jnp.int32) + jnp.where(
+        core == 1,
+        skip_0.astype(jnp.int32) + jnp.where(z_at > 0, skip_1.astype(jnp.int32), 0),
+        0,
+    )
+    sums_0, sums_1 = len(hops) + 1 + len(roots), len(hops) + 2 * zs - 1 + len(roots)
+    kinds = [(takes & jnp.logical_not(carrier), 12), (gives & jnp.logical_not(carrier), 13)]
+    kinds += [(carrier & takes, 17)] + ([(carrier & gives, 18)] if xs == 1 else [])
+    for faces_sent, face_count in kinds:
+        for c, most, left_out in ((0, sums_0, 2), (1, sums_1, 3)):
+            for less in range(left_out):
+
+                @pl.when(faces_sent & (core == c) & (skipped == less))
+                def _(sent=most - less + face_count * face_rows):
+                    arrived(all_sent.at[pl.ds(0, sent)], x_send)
+
     scope("lines")
 
-    @pl.when(core == 0)
+    @pl.when((core == 0) & others_than_root)
     def _():
         arrived(got_b, s_recv.at[1])
 
@@ -784,52 +861,12 @@
 
     @pl.when(is_root)
     def _():
-        width = 16
-        last_ones = (last_to - last_from) * ys * line
-        early_ones = count - 1 - last_ones
-
-        def sum_of(start, number, sums):
-            def some(k, sums):
-                for i in range(width):
-                    sums[i % 8] = sums[i % 8] + got_one[start + k * width + i]
-                return sums
-
-            whole = number // width
-            sums = lax.fori_loop(0, whole, some, sums)
-            for k in range(whole * width, number):
-                sums[k % 8] = sums[k % 8] + got_one[start + k]
-            return sums
-
-        arrived(got_one.at[pl.ds(0, early_ones)], one_recv.at[0])
-        sums = sum_of(0, early_ones, [jnp.zeros((2, LANES), jnp.float32)] * 8)
-        sums[0] = sums[0] + dots[0]
-        arrived(got_one.at[pl.ds(early_ones, last_ones)], one_recv.at[1])
-        sums = sum_of(early_ones, last_ones, sums)
-        dots[2] = added_up(sums)
+        dots[2] = root_sum(2, root_sum(1, dots[2]))
 
     total = dots[2]
     scope("alpha")
     sums = jnp.sum(total, axis=1, keepdims=True)
     al_o[...] = jnp.broadcast_to(sums[0:1, :] / sums[1:2, :], (8, LANES))
-    face_rows = FACE // 2
-    above_root = (core == 1) & (in_plane // line * line + ROOT == me) & others_than_root
-    sums_0, sums_1 = len(hops) + 2, len(hops) + 2 * zs
-    for sums_sent, many in (
-        (core == 0, sums_0),
-        ((core == 1) & jnp.logical_not(above_root | is_root), sums_1),
-        (above_root | is_root, sums_1 - 1),
-    ):
-        for faces_sent, faces in (
-            (takes & jnp.logical_not(carrier), 12),
-            (takes & carrier, 17),
-            (gives & jnp.logical_not(carrier), 13),
-            (gives & carrier, 18),
-        ):
-
-            @pl.when(sums_sent & faces_sent)
-            def _(sent=many + faces * face_rows):
-                arrived(all_sent.at[pl.ds(0, sent)], x_send)
-
     scope(None)
 
 
@@ -870,14 +907,14 @@
             vm(12 * FACE, LANES), vm(16, LANES),
             vm(3, 2, LANES), vm(2 * ys * xs - 1, 2, LANES), vm(zs, 2, LANES),
             vm(ys * zs * xs * cores - 1, 2, LANES),
-            vm(18 * FACE // 2 + ys * xs + 2 * zs, 2, LANES),
+            vm(18 * FACE // 2 + ys * xs + 2 * zs + len(ROOTS), 2, LANES),
             pltpu.VMEM((1, LANES), jnp.int32),
             pltpu.SemaphoreType.DMA((2,)),
             pltpu.SemaphoreType.DMA(()),
             pltpu.SemaphoreType.DMA((6,)),
             pltpu.SemaphoreType.DMA(()),
             pltpu.SemaphoreType.DMA((2,)),
-            pltpu.SemaphoreType.DMA((2,)),
+            pltpu.SemaphoreType.DMA((3,)),
             pltpu.SemaphoreType.REGULAR((3,)),
         ],
         compiler_params=pltpu.CompilerParams(

time: 33.7 us -> 33.5 us (level)
  no operation moved by 1% of the time
where the time goes in v9:
time: 33.5 us; the launch traced here: 33.4 us
  Pallas kernels  32.8 us (98%)
  between operations  0.64 us (2%)
    pallas_call x1, Pallas kernels, on_device(): pl.pallas_call(step_kernel, out_shape=(field, field, field, vm(8, LANES))...  32 us
    pallas_call x1, Pallas kernels, on_device(): pl.pallas_call(finish_kernel, out_shape=(flat, flat), in_specs=[in_vmem]...  0.79 us

profile of v9, /device:TPU:1, one launch (start us, length us, event | category | flops | bytes accessed | tf_op | source)
XLA Modules:
  0.0 33.4 jit_solution(13804602716408584937)
XLA Ops:
  0.6 32.0 %cg_step.1 = (f32[512,128]{1,0:T(8,128)S(1)}, f32[512,128]{1,0:T(8,128)S(1)}, f32[512,128]{1,0:T(8,128)S(1)}, f32[8,128]{1,0:T(8,128)S(1)}) custom-call(f32[512,128]{1,0:T(8,128)} %bitcast.6, f32[1536,128]{1,0:T(8,128)} %bitcast.5, f32[512,128]{1,0:T(8,128)} %bitcast.7, s32[1,128]{1,0:T(1,128)} %order_h.1), custom_call_target="tpu_custom_call" | custom-call | tf_op jit(solution)/shard_map/cg_step/pallas_call | solution.py:898
  32.6 0.8 %cg_finish.1 = (f32[512,128]{1,0:T(8,128)}, f32[512,128]{1,0:T(8,128)}) custom-call(f32[512,128]{1,0:T(8,128)S(1)} %get-tuple-element.8.p, f32[512,128]{1,0:T(8,128)S(1)} %get-tuple-element.9.r, f32[512,128]{1,0:T(8,128)S(1)} %get-tuple-element.10.im, f32[8,128]{1,0:T(8,128)S(1)} %get-tuple-element.11.al), custom_call_target="tpu_custom_call" | custom-call | tf_op jit(solution)/shard_map/cg_finish/pallas_call | solution.py:935

commit v10 on v9

--- a/solution.py
+++ b/solution.py
@@ -307,9 +307,13 @@
     near_to = me + 1 - 2 * core
     far_to = me + 2 * core - 1
     far_to = jnp.where(far_to < 0, count - 1, jnp.where(far_to == count, 0, far_to))
-    early, carrier, late = in_plane == 0, in_plane == line - 1, in_plane == plane_size - 1
+    in_line = lax.rem(me, line)
+    early, late = in_line == 0, in_line == line - 1
+    at_turn = in_plane < line
+    carrier = (jnp.logical_not(at_turn) & (in_line == 1)) | (at_turn & late)
+    carrier_of_late = jnp.where(in_plane == plane_size - 1, me + line - plane_size, me + 2)
     barrier = pltpu.get_barrier_semaphore()
-    greet(barrier, [jnp.where(late, me + line - plane_size, far_to)])
+    greet(barrier, [jnp.where(late, carrier_of_late, far_to)])
     loads = [
         pltpu.make_async_copy(src, dst, in_sems.at[k])
         for k, src, dst in (
@@ -325,7 +329,7 @@
 
     y_at = me // plane_size
     z_at = in_plane // line
-    x = lax.rem(me, line) // cores
+    x = in_line // cores
 
     def moved(dy=0, dz=0, dx=0):
         to = me
@@ -343,16 +347,27 @@
     sides = (near_to, far_to)
     row_of = (pl.multiple_of((1 - core) * (ROWS - FACE), FACE), pl.multiple_of(core * (ROWS - FACE), FACE))
     face_of = {0: 1 - core, LAST: core}
-    carrier_of_early = lax.rem(y_at + ys - 1, ys) * plane_size + line - 1
+    carrier_of_early = jnp.where(
+        at_turn, lax.rem(y_at + ys - 1, ys) * plane_size + line - 1, me + 1
+    )
     early_of_carrier = lax.rem(y_at + 1, ys) * plane_size
-    late_of_carrier = me + plane_size - line
-
-    row = [moved(dx=k) + c for k in range(xs) for c in (0, 1 - 2 * core) if k or not isinstance(c, int)]
+    late_of_carrier = jnp.where(at_turn, me + plane_size - line, me - 2)
+
     y_near = [moved(dy=k) for k in ring(ys, 3)]
     y_far = [moved(dy=k) for k in ring(ys, ys // 2 + 1, 3)]
-    greet(barrier, [near_to] + row + y_near)
-
-    @pl.when(early | carrier)
+    greet(barrier, [near_to])
+    not_early = jnp.logical_not(early)
+    for k in range(1, line):
+
+        @pl.when(in_line != k)
+        def _(k=k):
+            greet(barrier, [me - in_line + k])
+
+    @pl.when(not_early)
+    def _():
+        greet(barrier, y_near)
+
+    @pl.when(at_turn & (early | late))
     def _():
         greet(barrier, [jnp.where(early, carrier_of_early, early_of_carrier)])
 
@@ -381,15 +396,17 @@
 
         lax.fori_loop(0, (count - 1) // width, everyone, 0)
 
-    expected = (
-        len(row)
+    expected = jnp.where(
+        early,
+        1 + at_turn.astype(jnp.int32),
+        (line - 1)
         + len(y_near)
         + 2
-        + 2 * carrier.astype(jnp.int32)
-        + 2 * core * z_at
-        + len(roots)
-        - is_root.astype(jnp.int32)
+        + carrier.astype(jnp.int32)
+        + (carrier & at_turn).astype(jnp.int32)
+        + 2 * core * z_at,
     )
+    expected = expected + len(roots) - is_root.astype(jnp.int32)
 
     scope("idx")
     loads[0].wait()
@@ -438,7 +455,7 @@
         if carried is None:
             copy.start()
         else:
-            by_bag = remote(src, bag.at[pl.ds(carried, rows)], bag_recv, carrier_of_early)
+            by_bag = remote(src, bag.at[pl.ds(carried, rows)], bag_recv.at[1], carrier_of_early)
             pl.when(early)(by_bag.start)
             pl.when(jnp.logical_not(early))(copy.start)
         return copy
@@ -449,6 +466,11 @@
 
     def landed(ref, sem):
         pltpu.make_async_copy(ref, ref, sem).wait()
+
+    @pl.when(early)
+    def _():
+        pl.semaphore_wait(barrier, expected)
+        greet(hello.at[3], [near_to])
 
     both = (0, LAST)
     faces = (0, 1)
@@ -475,22 +497,55 @@
         for i in range(N):
             mine[part(face_of[a], G1, i), :] = lane_pick(g1[at(a, i), :], inverse)
             mine[part(face_of[a], G2, i), :] = lane_pick(g2[across(a, i), :], inverse)
+    sent_near = remote(
+        mine.at[pl.ds(0, 4 * FACE)], theirs.at[pl.ds(0, 4 * FACE)], x_recv.at[NEAR], near_to
+    )
+    beside_early = in_line == 1
+
+    @pl.when(beside_early)
+    def _():
+        pl.semaphore_wait(hello.at[3], 1)
+        sent_near.start()
+
     scope("barrier")
-    pl.semaphore_wait(barrier, expected)
+
+    @pl.when(not_early)
+    def _():
+        pl.semaphore_wait(barrier, expected)
+
     scope("send1")
 
-    sent_ld = swap(mine, theirs, 1, 4 * FACE, 2 * FACE, FAR_LD, 0)
-    sent_g = swap(mine, theirs, 1, 6 * FACE, 2 * FACE, FAR_G, 2 * FACE)
-    sent_near = swap(mine, theirs, 0, 0, 4 * FACE, NEAR)
-
     @pl.when(carrier)
     def _():
-        landed(bag, bag_recv)
+        landed(bag.at[pl.ds(0, 4 * FACE)], bag_recv.at[0])
         carry(theirs, 0, 4 * FACE, 2 * FACE, FAR_LD)
         carry(theirs, 2 * FACE, 6 * FACE, 2 * FACE, FAR_G)
-        carry(w_theirs, 4 * FACE, FACE, FACE, FAR_W)
-
-    greet(hello.at[0], y_near)
+
+    @pl.when(early)
+    def _():
+        remote(
+            mine.at[pl.ds(4 * FACE, 4 * FACE)],
+            bag.at[pl.ds(0, 4 * FACE)],
+            bag_recv.at[0],
+            carrier_of_early,
+        ).start()
+
+    sent_ld, sent_g = (
+        remote(mine.at[rows], theirs.at[rows], x_recv.at[k], far_to)
+        for k, rows in ((FAR_LD, pl.ds(4 * FACE, 2 * FACE)), (FAR_G, pl.ds(6 * FACE, 2 * FACE)))
+    )
+
+    @pl.when(not_early)
+    def _():
+        sent_ld.start()
+        sent_g.start()
+
+    pl.when(jnp.logical_not(beside_early))(sent_near.start)
+
+    @pl.when(not_early)
+    def _():
+        greet(hello.at[0], y_near)
+
 
     @pl.when(core == 1)
     def _():
@@ -511,6 +566,12 @@
             ld[rows, :] = moved_load
             r[rows, :] = moved_load
     reorder(g0, g0, inverse)
+
+    @pl.when(carrier)
+    def _():
+        landed(bag.at[pl.ds(4 * FACE, FACE)], bag_recv.at[1])
+        carry(w_theirs, 4 * FACE, FACE, FACE, FAR_W)
+
     scope("sums")
     sum_yz([(v, a) for a in INSIDE for v in (dg, r)], lanes)
 
@@ -564,8 +625,11 @@
     stiffness_bc(z, g1, g2t, ms, y, tmp, y)
     scope("hello")
 
-    heard(hello.at[0], y_near)
-    greet(hello.at[1], y_far)
+    @pl.when(not_early)
+    def _():
+        heard(hello.at[0], y_near)
+        greet(hello.at[1], y_far)
+
     scope("g_near")
     first = pl.multiple_of((1 - core) * FACE, FACE)
     couplings(g0, first, coupling)
@@ -688,7 +752,7 @@
         return functools.reduce(plus, [t for t in part if t is not None])
 
     half_z, pair_z = zs // 2, zs // 2 + zs // 8
-    in_line = y_at * line + lax.rem(me, line)
+    in_first = y_at * line + in_line
     slow_low = (z_at == pair_z) & (x == xs - 1) & (core == 1)
     slow_high = (z_at == pair_z + 1) & (x == 0) & (core == 0)
     slow_ones = ys * (2 if pair_z + 1 < zs else 1)
@@ -697,14 +761,14 @@
         slow_ones,
         jnp.where(
             z_at == pair_z + 1,
-            ys + y_at + (lax.rem(me, line) > 0).astype(jnp.int32),
+            ys + y_at + (in_line > 0).astype(jnp.int32),
             jnp.where(z_at == pair_z, y_at, 0),
         ),
     )
     slot = jnp.where(
         slow_low | slow_high,
         count - slow_ones + jnp.where(slow_high, ys, 0) + y_at,
-        z_at * ys * line + in_line - slow_before,
+        z_at * ys * line + in_first - slow_before,
     )
     group = jnp.where(slow_low | slow_high, 2, jnp.where(z_at < half_z, 0, 1))
     group_0 = half_z * ys * line - 1
@@ -742,7 +806,19 @@
             ).start()
 
     send_to_root(roots[0])
-    heard(hello.at[1], y_far)
+
+    @pl.when(not_early)
+    def _():
+        heard(hello.at[1], y_far)
+
+    @pl.when(beside_early)
+    def _():
+        greet(hello.at[0], [near_to])
+
+    @pl.when(early)
+    def _():
+        pl.semaphore_wait(hello.at[0], 1)
+
     for j, (dy, dx) in enumerate(hops):
         send(dots.at[0], got_a.at[2 * j + core], 0, moved(dy=dy, dx=dx) + 1 - core)
 
@@ -836,7 +912,7 @@
     )
     sums_0, sums_1 = len(hops) + 1 + len(roots), len(hops) + 2 * zs - 1 + len(roots)
     kinds = [(takes & jnp.logical_not(carrier), 12), (gives & jnp.logical_not(carrier), 13)]
-    kinds += [(carrier & takes, 17)] + ([(carrier & gives, 18)] if xs == 1 else [])
+    kinds += [(carrier & takes, 17), (carrier & gives, 18)]
     for faces_sent, face_count in kinds:
         for c, most, left_out in ((0, sums_0, 2), (1, sums_1, 3)):
             for less in range(left_out):
@@ -912,10 +988,10 @@
             pltpu.SemaphoreType.DMA((2,)),
             pltpu.SemaphoreType.DMA(()),
             pltpu.SemaphoreType.DMA((6,)),
-            pltpu.SemaphoreType.DMA(()),
+            pltpu.SemaphoreType.DMA((2,)),
             pltpu.SemaphoreType.DMA((2,)),
             pltpu.SemaphoreType.DMA((3,)),
-            pltpu.SemaphoreType.REGULAR((3,)),
+            pltpu.SemaphoreType.REGULAR((4,)),
         ],
         compiler_params=pltpu.CompilerParams(
             collective_id=0, has_side_effects=True, vmem_limit_bytes=24 << 20

time: 33.5 us -> 33.1 us (0.988)
  Pallas kernels: 32.8 us -> 32.3 us
    pallas_call x1, Pallas kernels: 32 us -> 31.5 us  [on_device(): pl.pallas_call(step_kernel, out_shape=(field, field, field, vm(8, LANES))...]
where the time goes in v10:
time: 33.1 us; the launch traced here: 33 us
  Pallas kernels  32.3 us (98%)
  between operations  0.64 us (2%)
    pallas_call x1, Pallas kernels, on_device(): pl.pallas_call(step_kernel, out_shape=(field, field, field, vm(8, LANES))...  31.5 us
    pallas_call x1, Pallas kernels, on_device(): pl.pallas_call(finish_kernel, out_shape=(flat, flat), in_specs=[in_vmem]...  0.79 us

profile of v10, /device:TPU:1, one launch (start us, length us, event | category | flops | bytes accessed | tf_op | source)
XLA Modules:
  0.0 33.0 jit_solution(9864667856848695983)
XLA Ops:
  0.6 31.5 %cg_step.1 = (f32[512,128]{1,0:T(8,128)S(1)}, f32[512,128]{1,0:T(8,128)S(1)}, f32[512,128]{1,0:T(8,128)S(1)}, f32[8,128]{1,0:T(8,128)S(1)}) custom-call(f32[512,128]{1,0:T(8,128)} %bitcast.6, f32[1536,128]{1,0:T(8,128)} %bitcast.5, f32[512,128]{1,0:T(8,128)} %bitcast.7, s32[1,128]{1,0:T(1,128)} %order_h.1), custom_call_target="tpu_custom_call" | custom-call | tf_op jit(solution)/shard_map/cg_step/pallas_call | solution.py:974
  32.2 0.8 %cg_finish.1 = (f32[512,128]{1,0:T(8,128)}, f32[512,128]{1,0:T(8,128)}) custom-call(f32[512,128]{1,0:T(8,128)S(1)} %get-tuple-element.8.p, f32[512,128]{1,0:T(8,128)S(1)} %get-tuple-element.9.r, f32[512,128]{1,0:T(8,128)S(1)} %get-tuple-element.10.im, f32[8,128]{1,0:T(8,128)S(1)} %get-tuple-element.11.al), custom_call_target="tpu_custom_call" | custom-call | tf_op jit(solution)/shard_map/cg_finish/pallas_call | solution.py:1011

commit v11 on v10

--- a/solution.py
+++ b/solution.py
@@ -19,7 +19,7 @@
 HALF = 1.35
 MESH = pl.DeviceIdType.MESH
 TORUS = (8, 12, 4, 2)
-ROOTS = (1, 3, 97, 2, 96)
+ROOTS = (1, 3, 97, 2, 96, 7, 193, 192, 5, 6)
 INSIDE = range(1, LAST)
 UNROLL_A = 4
 UNROLL_BC = 3
@@ -278,7 +278,7 @@
     coef, g2t, r, dg, z, y, u, tmp,
     mine, theirs, w_mine, w_theirs, i_mine, i_theirs, bag, rf, df, zf, pf, yf, a_sum, tmpf,
     u_ends, cross, q_mine, q_theirs, coupling, acc,
-    dots, got_a, got_b, got_one, all_sent, order_v, in_sems, x_send, x_recv, bag_recv, s_recv, one_recv, hello,
+    dots, fold, got_a, got_b, got_one, all_sent, order_v, in_sems, x_send, x_recv, bag_recv, s_recv, one_send, one_recv, hello,
 ):
     stack = []
 
@@ -663,6 +663,7 @@
     den = energy_bc(z, g1, g2t, ms, [zero] * 4)
     den = energy_a(z, g0, u_ends, first, den)
     num, den = added_up(num), added_up(den)
+    sent_w[0] = tell(0, NEAR_W)
     scope("g_far")
     sent_g.wait_recv()
     face_sums(1, mine, theirs, a_sum, a_sum, tmpf)
@@ -670,7 +671,6 @@
     for b in range(N):
         yf[at(1, b), :] = s[b]
     sum_yz([(yf, 1)], lanes)
-    sent_w[0] = tell(0, NEAR_W)
 
     def face_p(f):
         for b in range(N):
@@ -725,6 +725,11 @@
     den_row = jnp.sum(acc[tile(8), :], axis=0, keepdims=True)
     dots[0, 0:1, :] = num_row
     dots[0, 1:2, :] = den_row
+    half = LANES // 2
+    first_half = lane[0:1, :] < half
+    fold[0] = jnp.where(
+        first_half, num_row + pltpu.roll(num_row, half, 1), den_row + pltpu.roll(den_row, half, 1)
+    )
     hops = sorted(
         ((dy, dx) for dy in range(ys) for dx in range(xs) if dy or dx),
         key=lambda d: -min(d[0], ys - d[0]) - min(d[1], xs - d[1]),
@@ -777,7 +782,7 @@
     def root_sum(k, total):
         width, start, number = 16, sum(groups[:k]), groups[k]
         arrived(got_one.at[pl.ds(start, number)], one_recv.at[k])
-        sums = [total] + [jnp.zeros((2, LANES), jnp.float32)] * 7
+        sums = [total] + [jnp.zeros((1, LANES), jnp.float32)] * 7
 
         def some(i, sums):
             return [
@@ -797,9 +802,9 @@
         @pl.when(me != r)
         def _():
             pltpu.make_async_remote_copy(
-                src_ref=dots.at[0],
+                src_ref=fold.at[0],
                 dst_ref=got_one.at[slot - (slot > at_root).astype(jnp.int32)],
-                send_sem=x_send,
+                send_sem=one_send,
                 recv_sem=one_recv.at[group],
                 device_id=(r,),
                 device_id_type=MESH,
@@ -864,7 +869,7 @@
 
     @pl.when(is_root)
     def _():
-        dots[2] = root_sum(0, dots[0])
+        fold[1] = root_sum(0, fold[0])
 
     scope("plane")
     first_of_column = me - z_at * line
@@ -905,21 +910,29 @@
         for b in range(N):
             im_o[full(f, b), :] = lane_pick(yf[at(f, b), :], order)
     face_rows = FACE // 2
-    skipped = is_root.astype(jnp.int32) + jnp.where(
+    skipped = jnp.where(
         core == 1,
         skip_0.astype(jnp.int32) + jnp.where(z_at > 0, skip_1.astype(jnp.int32), 0),
         0,
     )
-    sums_0, sums_1 = len(hops) + 1 + len(roots), len(hops) + 2 * zs - 1 + len(roots)
+    sums_0, sums_1 = len(hops) + 1, len(hops) + 2 * zs - 1
     kinds = [(takes & jnp.logical_not(carrier), 12), (gives & jnp.logical_not(carrier), 13)]
     kinds += [(carrier & takes, 17), (carrier & gives, 18)]
-    for faces_sent, face_count in kinds:
-        for c, most, left_out in ((0, sums_0, 2), (1, sums_1, 3)):
-            for less in range(left_out):
-
-                @pl.when(faces_sent & (core == c) & (skipped == less))
-                def _(sent=most - less + face_count * face_rows):
-                    arrived(all_sent.at[pl.ds(0, sent)], x_send)
+
+    def all_left(who, to_roots):
+        for faces_sent, face_count in kinds:
+            for c, most, left_out in ((0, sums_0, 1), (1, sums_1, 3)):
+                for less in range(left_out):
+
+                    @pl.when(faces_sent & (core == c) & (skipped == less) & who)
+                    def _(sent=most - less + face_count * face_rows):
+                        arrived(all_sent.at[pl.ds(0, sent)], x_send)
+
+        @pl.when(who)
+        def _():
+            arrived(got_one.at[pl.ds(0, to_roots)], one_send)
+
+    all_left(others_than_root, len(roots))
 
     scope("lines")
 
@@ -937,12 +950,15 @@
 
     @pl.when(is_root)
     def _():
-        dots[2] = root_sum(2, root_sum(1, dots[2]))
+        both_sums = root_sum(2, root_sum(1, fold[1]))
+        dots[2, 0:1, :] = jnp.where(first_half, both_sums, 0.0)
+        dots[2, 1:2, :] = jnp.where(first_half, 0.0, both_sums)
 
     total = dots[2]
     scope("alpha")
     sums = jnp.sum(total, axis=1, keepdims=True)
     al_o[...] = jnp.broadcast_to(sums[0:1, :] / sums[1:2, :], (8, LANES))
+    all_left(is_root, len(roots) - 1)
     scope(None)
 
 
@@ -981,8 +997,8 @@
             *[vm(8 * FACE, LANES)] * 2,
             *[pair] * 4, vm(5 * FACE, LANES), *[pair] * 8, *[vm(FACE, LANES)] * 3,
             vm(12 * FACE, LANES), vm(16, LANES),
-            vm(3, 2, LANES), vm(2 * ys * xs - 1, 2, LANES), vm(zs, 2, LANES),
-            vm(ys * zs * xs * cores - 1, 2, LANES),
+            vm(3, 2, LANES), vm(2, 1, LANES), vm(2 * ys * xs - 1, 2, LANES), vm(zs, 2, LANES),
+            vm(ys * zs * xs * cores - 1, 1, LANES),
             vm(18 * FACE // 2 + ys * xs + 2 * zs + len(ROOTS), 2, LANES),
             pltpu.VMEM((1, LANES), jnp.int32),
             pltpu.SemaphoreType.DMA((2,)),
@@ -990,6 +1006,7 @@
             pltpu.SemaphoreType.DMA((6,)),
             pltpu.SemaphoreType.DMA((2,)),
             pltpu.SemaphoreType.DMA((2,)),
+            pltpu.SemaphoreType.DMA(()),
             pltpu.SemaphoreType.DMA((3,)),
             pltpu.SemaphoreType.REGULAR((4,)),
         ],

time: 33.1 us -> 33.1 us (level)
  no operation moved by 1% of the time
where the time goes in v11:
time: 33.1 us; the launch traced here: 32.9 us
  Pallas kernels  32.3 us (98%)
  between operations  0.64 us (2%)
    pallas_call x1, Pallas kernels, on_device(): pl.pallas_call(step_kernel, out_shape=(field, field, field, vm(8, LANES))...  31.5 us
    pallas_call x1, Pallas kernels, on_device(): pl.pallas_call(finish_kernel, out_shape=(flat, flat), in_specs=[in_vmem]...  0.79 us

profile of v11, /device:TPU:1, one launch (start us, length us, event | category | flops | bytes accessed | tf_op | source)
XLA Modules:
  0.0 32.9 jit_solution(14510607763564019174)
XLA Ops:
  0.6 31.5 %cg_step.1 = (f32[512,128]{1,0:T(8,128)S(1)}, f32[512,128]{1,0:T(8,128)S(1)}, f32[512,128]{1,0:T(8,128)S(1)}, f32[8,128]{1,0:T(8,128)S(1)}) custom-call(f32[512,128]{1,0:T(8,128)} %bitcast.6, f32[1536,128]{1,0:T(8,128)} %bitcast.5, f32[512,128]{1,0:T(8,128)} %bitcast.7, s32[1,128]{1,0:T(1,128)} %order_h.1), custom_call_target="tpu_custom_call" | custom-call | tf_op jit(solution)/shard_map/cg_step/pallas_call | solution.py:990
  32.2 0.8 %cg_finish.1 = (f32[512,128]{1,0:T(8,128)}, f32[512,128]{1,0:T(8,128)}) custom-call(f32[512,128]{1,0:T(8,128)S(1)} %get-tuple-element.8.p, f32[512,128]{1,0:T(8,128)S(1)} %get-tuple-element.9.r, f32[512,128]{1,0:T(8,128)S(1)} %get-tuple-element.10.im, f32[8,128]{1,0:T(8,128)S(1)} %get-tuple-element.11.al), custom_call_target="tpu_custom_call" | custom-call | tf_op jit(solution)/shard_map/cg_finish/pallas_call | solution.py:1028

commit v12 on v11

--- a/solution.py
+++ b/solution.py
@@ -278,7 +278,7 @@
     coef, g2t, r, dg, z, y, u, tmp,
     mine, theirs, w_mine, w_theirs, i_mine, i_theirs, bag, rf, df, zf, pf, yf, a_sum, tmpf,
     u_ends, cross, q_mine, q_theirs, coupling, acc,
-    dots, fold, got_a, got_b, got_one, all_sent, order_v, in_sems, x_send, x_recv, bag_recv, s_recv, one_send, one_recv, hello,
+    dots, fold, got_a, got_b, got_one, got_two, all_sent, order_v, in_sems, x_send, x_recv, bag_recv, s_recv, one_send, hello,
 ):
     stack = []
 
@@ -725,11 +725,6 @@
     den_row = jnp.sum(acc[tile(8), :], axis=0, keepdims=True)
     dots[0, 0:1, :] = num_row
     dots[0, 1:2, :] = den_row
-    half = LANES // 2
-    first_half = lane[0:1, :] < half
-    fold[0] = jnp.where(
-        first_half, num_row + pltpu.roll(num_row, half, 1), den_row + pltpu.roll(den_row, half, 1)
-    )
     hops = sorted(
         ((dy, dx) for dy in range(ys) for dx in range(xs) if dy or dx),
         key=lambda d: -min(d[0], ys - d[0]) - min(d[1], xs - d[1]),
@@ -779,38 +774,49 @@
     group_0 = half_z * ys * line - 1
     groups = (group_0, count - 1 - group_0 - slow_ones, slow_ones)
 
-    def root_sum(k, total):
+    def root_sum(got, k, total):
         width, start, number = 16, sum(groups[:k]), groups[k]
-        arrived(got_one.at[pl.ds(start, number)], one_recv.at[k])
-        sums = [total] + [jnp.zeros((1, LANES), jnp.float32)] * 7
+        arrived(got.at[pl.ds(start, number)], root_recv[k])
+        sums = [total] + [jnp.zeros_like(total)] * 7
 
         def some(i, sums):
             return [
-                sums[j] + got_one[start + i * width + j] + got_one[start + i * width + j + 8]
+                sums[j] + got[start + i * width + j] + got[start + i * width + j + 8]
                 for j in range(8)
             ]
 
         whole = number // width
         sums = lax.fori_loop(0, whole, some, sums)
         for i in range(whole * width, number):
-            sums[i % 8] = sums[i % 8] + got_one[start + i]
+            sums[i % 8] = sums[i % 8] + got[start + i]
         return added_up(sums)
+
+    root_recv = (s_recv.at[2], s_recv.at[3], s_recv.at[1])
+    root_sem = s_recv.at[jnp.where(group == 2, 1, group + 2)]
 
     def send_to_root(r):
         at_root = r // plane_size * line + r % line
 
         @pl.when(me != r)
         def _():
+            first_root = r == roots[0]
             pltpu.make_async_remote_copy(
-                src_ref=fold.at[0],
-                dst_ref=got_one.at[slot - (slot > at_root).astype(jnp.int32)],
-                send_sem=one_send,
-                recv_sem=one_recv.at[group],
+                src_ref=dots.at[0] if first_root else fold.at[0],
+                dst_ref=(got_two if first_root else got_one).at[
+                    slot - (slot > at_root).astype(jnp.int32)
+                ],
+                send_sem=x_send if first_root else one_send,
+                recv_sem=root_sem,
                 device_id=(r,),
                 device_id_type=MESH,
             ).start()
 
     send_to_root(roots[0])
+    half = LANES // 2
+    first_half = lane[0:1, :] < half
+    fold[0] = jnp.where(
+        first_half, num_row + pltpu.roll(num_row, half, 1), den_row + pltpu.roll(den_row, half, 1)
+    )
 
     @pl.when(not_early)
     def _():
@@ -866,10 +872,17 @@
     sum_yz([(u, a) for a in INSIDE], lanes)
     reorder(u, im_o, order, INSIDE)
     scope("root_0")
+    is_first, not_first = me == roots[0], me != roots[0]
 
     @pl.when(is_root)
     def _():
-        fold[1] = root_sum(0, fold[0])
+        @pl.when(is_first)
+        def _():
+            dots[2] = root_sum(got_two, 0, dots[0])
+
+        @pl.when(not_first)
+        def _():
+            fold[1] = root_sum(got_one, 0, fold[0])
 
     scope("plane")
     first_of_column = me - z_at * line
@@ -915,24 +928,27 @@
         skip_0.astype(jnp.int32) + jnp.where(z_at > 0, skip_1.astype(jnp.int32), 0),
         0,
     )
-    sums_0, sums_1 = len(hops) + 1, len(hops) + 2 * zs - 1
+    sums_0, sums_1 = len(hops) + 2, len(hops) + 2 * zs
+    skipped = skipped + is_first.astype(jnp.int32)
     kinds = [(takes & jnp.logical_not(carrier), 12), (gives & jnp.logical_not(carrier), 13)]
     kinds += [(carrier & takes, 17), (carrier & gives, 18)]
 
     def all_left(who, to_roots):
         for faces_sent, face_count in kinds:
-            for c, most, left_out in ((0, sums_0, 1), (1, sums_1, 3)):
+            for c, most, left_out in ((0, sums_0, 2), (1, sums_1, 4)):
                 for less in range(left_out):
 
                     @pl.when(faces_sent & (core == c) & (skipped == less) & who)
                     def _(sent=most - less + face_count * face_rows):
                         arrived(all_sent.at[pl.ds(0, sent)], x_send)
 
-        @pl.when(who)
-        def _():
-            arrived(got_one.at[pl.ds(0, to_roots)], one_send)
-
-    all_left(others_than_root, len(roots))
+        for whose, number in to_roots:
+
+            @pl.when(whose)
+            def _(number=number):
+                arrived(got_one.at[pl.ds(0, number)], one_send)
+
+    all_left(others_than_root, [(others_than_root, len(roots) - 1)])
 
     scope("lines")
 
@@ -944,21 +960,26 @@
     def _():
         arrived(got_b.at[pl.ds(0, zs - 1)], s_recv.at[1])
 
+    def divide(total):
+        sums = jnp.sum(total, axis=1, keepdims=True)
+        al_o[...] = jnp.broadcast_to(sums[0:1, :] / sums[1:2, :], (8, LANES))
+
     @pl.when(others_than_root)
     def _():
-        dots[2] = added(got_b, None, zs)
-
-    @pl.when(is_root)
-    def _():
-        both_sums = root_sum(2, root_sum(1, fold[1]))
-        dots[2, 0:1, :] = jnp.where(first_half, both_sums, 0.0)
-        dots[2, 1:2, :] = jnp.where(first_half, 0.0, both_sums)
-
-    total = dots[2]
+        divide(added(got_b, None, zs))
+
+    @pl.when(is_first)
+    def _():
+        divide(root_sum(got_two, 2, root_sum(got_two, 1, dots[2])))
+
+    @pl.when(is_root & not_first)
+    def _():
+        row_sum = root_sum(got_one, 2, root_sum(got_one, 1, fold[1]))
+        own_half = (lane[0:2, :] < half) == (b_at[0:2, :] == 0)
+        divide(jnp.where(own_half, jnp.broadcast_to(row_sum, (2, LANES)), 0.0))
+
     scope("alpha")
-    sums = jnp.sum(total, axis=1, keepdims=True)
-    al_o[...] = jnp.broadcast_to(sums[0:1, :] / sums[1:2, :], (8, LANES))
-    all_left(is_root, len(roots) - 1)
+    all_left(is_root, [(is_first, len(roots) - 1), (is_root & not_first, len(roots) - 2)])
     scope(None)
 
 
@@ -998,16 +1019,15 @@
             *[pair] * 4, vm(5 * FACE, LANES), *[pair] * 8, *[vm(FACE, LANES)] * 3,
             vm(12 * FACE, LANES), vm(16, LANES),
             vm(3, 2, LANES), vm(2, 1, LANES), vm(2 * ys * xs - 1, 2, LANES), vm(zs, 2, LANES),
-            vm(ys * zs * xs * cores - 1, 1, LANES),
-            vm(18 * FACE // 2 + ys * xs + 2 * zs + len(ROOTS), 2, LANES),
+            vm(ys * zs * xs * cores - 1, 1, LANES), vm(ys * zs * xs * cores - 1, 2, LANES),
+            vm(18 * FACE // 2 + ys * xs + 2 * zs + 1, 2, LANES),
             pltpu.VMEM((1, LANES), jnp.int32),
             pltpu.SemaphoreType.DMA((2,)),
             pltpu.SemaphoreType.DMA(()),
             pltpu.SemaphoreType.DMA((6,)),
             pltpu.SemaphoreType.DMA((2,)),
-            pltpu.SemaphoreType.DMA((2,)),
+            pltpu.SemaphoreType.DMA((4,)),
             pltpu.SemaphoreType.DMA(()),
-            pltpu.SemaphoreType.DMA((3,)),
             pltpu.SemaphoreType.REGULAR((4,)),
         ],
         compiler_params=pltpu.CompilerParams(

time: 33.1 us -> 33.1 us (level)
  no operation moved by 1% of the time
where the time goes in v12:
time: 33.1 us; the launch traced here: 32.9 us
  Pallas kernels  32.3 us (98%)
  between operations  0.64 us (2%)
    pallas_call x1, Pallas kernels, on_device(): pl.pallas_call(step_kernel, out_shape=(field, field, field, vm(8, LANES))...  31.5 us
    pallas_call x1, Pallas kernels, on_device(): pl.pallas_call(finish_kernel, out_shape=(flat, flat), in_specs=[in_vmem]...  0.79 us

profile of v12, /device:TPU:1, one launch (start us, length us, event | category | flops | bytes accessed | tf_op | source)
XLA Modules:
  0.0 32.9 jit_solution(10239616787998441572)
XLA Ops:
  0.6 31.5 %cg_step.1 = (f32[512,128]{1,0:T(8,128)S(1)}, f32[512,128]{1,0:T(8,128)S(1)}, f32[512,128]{1,0:T(8,128)S(1)}, f32[8,128]{1,0:T(8,128)S(1)}) custom-call(f32[512,128]{1,0:T(8,128)} %bitcast.6, f32[1536,128]{1,0:T(8,128)} %bitcast.5, f32[512,128]{1,0:T(8,128)} %bitcast.7, s32[1,128]{1,0:T(1,128)} %order_h.1), custom_call_target="tpu_custom_call" | custom-call | tf_op jit(solution)/shard_map/cg_step/pallas_call | solution.py:1011
  32.1 0.8 %cg_finish.1 = (f32[512,128]{1,0:T(8,128)}, f32[512,128]{1,0:T(8,128)}) custom-call(f32[512,128]{1,0:T(8,128)S(1)} %get-tuple-element.8.p, f32[512,128]{1,0:T(8,128)S(1)} %get-tuple-element.9.r, f32[512,128]{1,0:T(8,128)S(1)} %get-tuple-element.10.im, f32[8,128]{1,0:T(8,128)S(1)} %get-tuple-element.11.al), custom_call_target="tpu_custom_call" | custom-call | tf_op jit(solution)/shard_map/cg_finish/pallas_call | solution.py:1048

commit v13 on v12

--- a/solution.py
+++ b/solution.py
@@ -871,18 +871,23 @@
                 dst[full(f, b), :] = lane_pick(ends[at(f, b), :], order)
     sum_yz([(u, a) for a in INSIDE], lanes)
     reorder(u, im_o, order, INSIDE)
-    scope("root_0")
+    scope("x3_root")
     is_first, not_first = me == roots[0], me != roots[0]
 
+    def image_ends():
+        landed(i_theirs, x_recv.at[IMAGE])
+        for f in faces:
+            for b in range(N):
+                rows = at(f, b)
+                yf[rows, :] = yf[rows, :] + (i_mine[rows, :] + i_theirs[rows, :])
+        sum_yz([(yf, f) for f in faces], lanes)
+        for f in faces:
+            for b in range(N):
+                im_o[full(f, b), :] = lane_pick(yf[at(f, b), :], order)
+
     @pl.when(is_root)
     def _():
-        @pl.when(is_first)
-        def _():
-            dots[2] = root_sum(got_two, 0, dots[0])
-
-        @pl.when(not_first)
-        def _():
-            fold[1] = root_sum(got_one, 0, fold[0])
+        image_ends()
 
     scope("plane")
     first_of_column = me - z_at * line
@@ -912,16 +917,24 @@
 
         got_b[zs - 1] = dots[1]
 
+    scope("root_0")
+
+    @pl.when(is_root)
+    def _():
+        @pl.when(is_first)
+        def _():
+            dots[2] = root_sum(got_two, 0, dots[0])
+
+        @pl.when(not_first)
+        def _():
+            fold[1] = root_sum(got_one, 0, fold[0])
+
     scope("x3")
-    landed(i_theirs, x_recv.at[IMAGE])
-    for f in faces:
-        for b in range(N):
-            rows = at(f, b)
-            yf[rows, :] = yf[rows, :] + (i_mine[rows, :] + i_theirs[rows, :])
-    sum_yz([(yf, f) for f in faces], lanes)
-    for f in faces:
-        for b in range(N):
-            im_o[full(f, b), :] = lane_pick(yf[at(f, b), :], order)
+
+    @pl.when(others_than_root)
+    def _():
+        image_ends()
+
     face_rows = FACE // 2
     skipped = jnp.where(
         core == 1,
@@ -983,7 +996,7 @@
     scope(None)
 
 
-CHUNKS = 4
+CHUNKS = 8
 
 
 def finish_kernel(p, r, im, al, x_h, r_h, both, sem):

time: 33.1 us -> 33.1 us (level)
  no operation moved by 1% of the time
where the time goes in v13:
time: 33.1 us; the launch traced here: 32.9 us
  Pallas kernels  32.3 us (98%)
  between operations  0.64 us (2%)
    pallas_call x1, Pallas kernels, on_device(): pl.pallas_call(step_kernel, out_shape=(field, field, field, vm(8, LANES))...  31.5 us
    pallas_call x1, Pallas kernels, on_device(): pl.pallas_call(finish_kernel, out_shape=(flat, flat), in_specs=[in_vmem]...  0.79 us

profile of v13, /device:TPU:1, one launch (start us, length us, event | category | flops | bytes accessed | tf_op | source)
XLA Modules:
  0.0 32.9 jit_solution(14984983377578587419)
XLA Ops:
  0.6 31.5 %cg_step.1 = (f32[512,128]{1,0:T(8,128)S(1)}, f32[512,128]{1,0:T(8,128)S(1)}, f32[512,128]{1,0:T(8,128)S(1)}, f32[8,128]{1,0:T(8,128)S(1)}) custom-call(f32[512,128]{1,0:T(8,128)} %bitcast.6, f32[1536,128]{1,0:T(8,128)} %bitcast.5, f32[512,128]{1,0:T(8,128)} %bitcast.7, s32[1,128]{1,0:T(1,128)} %order_h.1), custom_call_target="tpu_custom_call" | custom-call | tf_op jit(solution)/shard_map/cg_step/pallas_call | solution.py:1024
  32.1 0.8 %cg_finish.1 = (f32[512,128]{1,0:T(8,128)}, f32[512,128]{1,0:T(8,128)}) custom-call(f32[512,128]{1,0:T(8,128)S(1)} %get-tuple-element.8.p, f32[512,128]{1,0:T(8,128)S(1)} %get-tuple-element.9.r, f32[512,128]{1,0:T(8,128)S(1)} %get-tuple-element.10.im, f32[8,128]{1,0:T(8,128)S(1)} %get-tuple-element.11.al), custom_call_target="tpu_custom_call" | custom-call | tf_op jit(solution)/shard_map/cg_finish/pallas_call | solution.py:1061

commit v14 on v12

--- a/solution.py
+++ b/solution.py
@@ -983,7 +983,7 @@
     scope(None)
 
 
-CHUNKS = 4
+CHUNKS = 8
 
 
 def finish_kernel(p, r, im, al, x_h, r_h, both, sem):

time: 33.1 us -> 33.1 us (level)
  no operation moved by 1% of the time
where the time goes in v14:
time: 33.1 us; the launch traced here: 32.9 us
  Pallas kernels  32.3 us (98%)
  between operations  0.64 us (2%)
    pallas_call x1, Pallas kernels, on_device(): pl.pallas_call(step_kernel, out_shape=(field, field, field, vm(8, LANES))...  31.5 us
    pallas_call x1, Pallas kernels, on_device(): pl.pallas_call(finish_kernel, out_shape=(flat, flat), in_specs=[in_vmem]...  0.79 us

profile of v14, /device:TPU:1, one launch (start us, length us, event | category | flops | bytes accessed | tf_op | source)
XLA Modules:
  0.0 32.9 jit_solution(823359128776106485)
XLA Ops:
  0.6 31.5 %cg_step.1 = (f32[512,128]{1,0:T(8,128)S(1)}, f32[512,128]{1,0:T(8,128)S(1)}, f32[512,128]{1,0:T(8,128)S(1)}, f32[8,128]{1,0:T(8,128)S(1)}) custom-call(f32[512,128]{1,0:T(8,128)} %bitcast.6, f32[1536,128]{1,0:T(8,128)} %bitcast.5, f32[512,128]{1,0:T(8,128)} %bitcast.7, s32[1,128]{1,0:T(1,128)} %order_h.1), custom_call_target="tpu_custom_call" | custom-call | tf_op jit(solution)/shard_map/cg_step/pallas_call | solution.py:1011
  32.1 0.8 %cg_finish.1 = (f32[512,128]{1,0:T(8,128)}, f32[512,128]{1,0:T(8,128)}) custom-call(f32[512,128]{1,0:T(8,128)S(1)} %get-tuple-element.8.p, f32[512,128]{1,0:T(8,128)S(1)} %get-tuple-element.9.r, f32[512,128]{1,0:T(8,128)S(1)} %get-tuple-element.10.im, f32[8,128]{1,0:T(8,128)S(1)} %get-tuple-element.11.al), custom_call_target="tpu_custom_call" | custom-call | tf_op jit(solution)/shard_map/cg_finish/pallas_call | solution.py:1048
